TPU v7x, 32 devices: a 4x4x1 block of a 4x4x8 slice. The times are simulated.
32 devices in a mesh: data: 1 (over z), model: 32 (over y, x, core).
Axes of the slice: x: 4, y: 4, z: 1, core: 2. Of those that a mesh axis runs over, the one named last changes fastest.
The devices are a block of a 4x4x8 slice.
Arguments:
- x_in: bfloat16 [32, 256, 2048], P('data')
- seg_ids: int32 [32, 256], P('data')
- ln_gain: bfloat16 [2048], replicated
- w_qkv: bfloat16 [2048, 32, 3, 64], P(None, 'model')
- w_out: bfloat16 [32, 64, 2048], P('model')
- w_up: bfloat16 [2048, 8192], P(None, 'model')
- w_down: bfloat16 [8192, 2048], P('model')
- dy_in: bfloat16 [32, 256, 2048], P('data')
Outputs:
- output 1: bfloat16 [32, 256, 2048], P('data')
- output 2: bfloat16 [32, 256, 2048], P('data')
- output 3: bfloat16 [2048], P('data')
- output 4: bfloat16 [2048, 32, 3, 64], P('data', 'model')
- output 5: bfloat16 [32, 64, 2048], P(('data', 'model'))
- output 6: bfloat16 [2048, 8192], P('data', 'model')
- output 7: bfloat16 [8192, 2048], P(('data', 'model'))
All inputs are finite; a program needn't handle non-finite values.
Results may differ from a plain program's by a relative error of at most 0.0183751.
Values are sent between devices in bfloat16 or wider.
A program may use at most 768 MiB of HBM per device.

v0:
```python
import jax
import jax.numpy as jnp
from jax import lax
from jax.sharding import PartitionSpec as P

LN_EPS = 1e-5


def layer_norm_fwd(x_f32, ln_gain):
    mean_val = jnp.mean(x_f32, axis=-1, keepdims=True)
    centered = x_f32 - mean_val
    inv_std = lax.rsqrt(jnp.mean(centered * centered, axis=-1, keepdims=True) + LN_EPS)
    normed_f32 = centered * inv_std
    normed = (normed_f32 * ln_gain.astype(jnp.float32)).astype(jnp.bfloat16)
    return normed, normed_f32, inv_std


def layer_norm_bwd(d_normed, normed_f32, inv_std, ln_gain):
    grad_f32 = d_normed.astype(jnp.float32)
    d_gain = jnp.sum(grad_f32 * normed_f32, axis=(0, 1))
    d_hat = grad_f32 * ln_gain.astype(jnp.float32)
    d_x = inv_std * (d_hat - jnp.mean(d_hat, axis=-1, keepdims=True) - normed_f32 * jnp.mean(d_hat * normed_f32, axis=-1, keepdims=True))
    return d_x, d_gain


def gelu_round(up_proj):
    return jax.nn.gelu(up_proj.astype(jnp.float32), approximate=False).astype(jnp.bfloat16)


def attention_allowed(seg_ids):
    positions = jnp.arange(seg_ids.shape[1])
    causal = positions[None, :] <= positions[:, None]
    same_doc = seg_ids[:, :, None] == seg_ids[:, None, :]
    return (causal[None] & same_doc)[:, None]


def attention_fwd(qkv_proj, allowed):
    score_scale = qkv_proj.shape[-1] ** -0.5
    scores = jnp.einsum('bqnd,bknd->bnqk', qkv_proj[:, :, :, 0], qkv_proj[:, :, :, 1], preferred_element_type=jnp.float32) * score_scale
    attn_probs = jax.nn.softmax(jnp.where(allowed, scores, -1e30), axis=-1)
    probs_bf16 = attn_probs.astype(jnp.bfloat16)
    attn_out = jnp.einsum('bnqk,bknd->bqnd', probs_bf16, qkv_proj[:, :, :, 2], preferred_element_type=jnp.float32).astype(jnp.bfloat16)
    return attn_out, attn_probs, probs_bf16


def attention_bwd(d_attn, qkv_proj, attn_probs, probs_bf16):
    score_scale = qkv_proj.shape[-1] ** -0.5
    query = qkv_proj[:, :, :, 0]
    keys = qkv_proj[:, :, :, 1]
    values = qkv_proj[:, :, :, 2]
    d_probs = jnp.einsum('bqnd,bknd->bnqk', d_attn, values, preferred_element_type=jnp.float32)
    d_scores = (attn_probs * (d_probs - jnp.sum(d_probs * attn_probs, axis=-1, keepdims=True)) * score_scale).astype(jnp.bfloat16)
    d_query = jnp.einsum('bnqk,bknd->bqnd', d_scores, keys, preferred_element_type=jnp.float32).astype(jnp.bfloat16)
    d_keys = jnp.einsum('bnqk,bqnd->bknd', d_scores, query, preferred_element_type=jnp.float32).astype(jnp.bfloat16)
    d_values = jnp.einsum('bnqk,bqnd->bknd', probs_bf16, d_attn, preferred_element_type=jnp.float32).astype(jnp.bfloat16)
    return jnp.stack([d_query, d_keys, d_values], axis=3)


def solution(mesh):
    def body(x_in, seg_ids, ln_gain, w_qkv, w_out, w_up, w_down, dy_in):
        x_f32 = x_in.astype(jnp.float32)
        normed, normed_f32, inv_std = layer_norm_fwd(x_f32, ln_gain)
        qkv_proj = jnp.einsum('bsh,hnjd->bsnjd', normed, w_qkv, preferred_element_type=jnp.float32).astype(jnp.bfloat16)
        attn_out, attn_probs, probs_bf16 = attention_fwd(qkv_proj, attention_allowed(seg_ids))
        up_proj = jnp.einsum('bsh,hf->bsf', normed, w_up, preferred_element_type=jnp.float32).astype(jnp.bfloat16)
        hidden_act, gelu_vjp = jax.vjp(gelu_round, up_proj)
        share = jnp.einsum('bqnd,ndh->bqh', attn_out, w_out, preferred_element_type=jnp.float32) + jnp.einsum('bsf,fh->bsh', hidden_act, w_down, preferred_element_type=jnp.float32)
        mixed = lax.psum(share.astype(jnp.bfloat16), 'model')
        y_out = (x_f32 + mixed.astype(jnp.float32)).astype(jnp.bfloat16)
        d_wout = jnp.einsum('bsnd,bsh->ndh', attn_out, dy_in, preferred_element_type=jnp.float32).astype(jnp.bfloat16)
        d_wdown = jnp.einsum('bsf,bsh->fh', hidden_act, dy_in, preferred_element_type=jnp.float32).astype(jnp.bfloat16)
        d_attn = jnp.einsum('bsh,ndh->bsnd', dy_in, w_out, preferred_element_type=jnp.float32).astype(jnp.bfloat16)
        d_hidden = jnp.einsum('bsh,fh->bsf', dy_in, w_down, preferred_element_type=jnp.float32).astype(jnp.bfloat16)
        (d_up,) = gelu_vjp(d_hidden)
        d_qkv = attention_bwd(d_attn, qkv_proj, attn_probs, probs_bf16)
        d_wqkv = jnp.einsum('bsh,bsnjd->hnjd', normed, d_qkv, preferred_element_type=jnp.float32).astype(jnp.bfloat16)
        d_wup = jnp.einsum('bsh,bsf->hf', normed, d_up, preferred_element_type=jnp.float32).astype(jnp.bfloat16)
        d_share = jnp.einsum('bsnjd,hnjd->bsh', d_qkv, w_qkv, preferred_element_type=jnp.float32) + jnp.einsum('bsf,hf->bsh', d_up, w_up, preferred_element_type=jnp.float32)
        d_normed = lax.psum(d_share.astype(jnp.bfloat16), 'model')
        d_x, d_gain = layer_norm_bwd(d_normed, normed_f32, inv_std, ln_gain)
        dx_out = (dy_in.astype(jnp.float32) + d_x).astype(jnp.bfloat16)
        return y_out, dx_out, d_gain.astype(jnp.bfloat16), d_wqkv, d_wout, d_wup, d_wdown

    in_specs = (P('data'), P('data'), P(), P(None, 'model'), P('model'), P(None, 'model'), P('model'), P('data'))
    out_specs = (P('data'), P('data'), P('data'), P('data', 'model'), P(('data', 'model')), P('data', 'model'), P(('data', 'model')))
    return jax.shard_map(body, mesh=mesh, in_specs=in_specs, out_specs=out_specs, check_vma=False)
```

profile of v0, /device:TPU:97, one launch (start us, length us, event | category | flops | bytes accessed | tf_op | source)
XLA Modules:
  0.0 848.0 jit_solution(1793730479236186933)
XLA Ops:
  7.2 0.0 copy-start
  7.2 0.1 all-reduce.3.cloned.1.call-start
  7.3 0.8 convert_element_type.125
  8.1 11.2 %convert_reduce_fusion = f32[32,256]{1,0:T(8,128)S(1)} fusion(bf16[32,256,2048]{2,1,0:T(8,128)(2,1)} %param.8), kind=kLoop, calls=%fused_computation.4 | loop fusion | flops 33546240 | bytes 33587200 | tf_op jit(solution)/shard_map/reduce_sum | solution.py:10
  19.3 0.0 copy-start.12
  19.3 0.0 copy-start.10
  19.3 12.9 %fusion.14 = f32[32,256]{1,0:T(8,128)S(1)} fusion(bf16[32,256,2048]{2,1,0:T(8,128)(2,1)} %param.8, f32[32,256]{1,0:T(8,128)S(1)} %broadcast_multiply_fusion.2), kind=kLoop, calls=%fused_computation.19 | loop fusion | flops 67100672 | bytes 33619968 | tf_op jit(solution)/shard_map/reduce_sum | solution.py:12
  32.3 0.0 copy-done.10
  32.3 0.0 copy-start.14
  32.3 17.2 %convert_bitcast_fusion = bf16[32,256,1,3,64]{1,4,3,0,2:T(8,128)(2,1)S(1)} fusion(bf16[2048,1,3,64]{0,3,2,1:T(8,128)(2,1)S(1)} %copy-done.10, bf16[32,256,2048]{2,1,0:T(8,128)(2,1)} %param.8, f32[2048]{0:T(1024)S(1)} %convert_element_type.125, f32[32,256]{1,0:T(8,128)S(1)} %add_rsqrt_fusion, f32[32,256]{1,0:T(8,128)S(1)} %broadcast_multiply_fusion.2), kind=kOutput, calls=%fused_computation.90 | convolution fusion | flops 6527909888 | bytes 37560320 | tf_op jit(solution)/shard_map/bsh,hnjd->bsnjd/dot_general | solution.py:63
  49.5 0.0 copy-start.3
  49.5 1.6 copy-done.3
  51.2 1.3 fusion.125
  52.5 0.0 copy-done.8
  52.5 16.7 %convolution_convert_fusion.1 = bf16[32,256,64]{1,2,0:T(8,128)(2,1)S(1)} fusion(bf16[32,256,2048]{2,1,0:T(8,128)(2,1)} %param.15, bf16[1,64,2048]{2,1,0:T(8,128)(2,1)S(1)} %copy-done.8), kind=kOutput, calls=%fused_computation.108 | convolution fusion | flops 2148007936 | bytes 34865152 | tf_op jit(solution)/shard_map/bsh,ndh->bsnd/dot_general | solution.py:72
  69.2 0.0 copy-start.20
  69.2 5.9 fusion.124
  75.2 0.0 copy-done.20
  75.2 5.5 fusion.147
  80.7 0.0 copy-start.21
  80.7 3.4 copy-done.21
  84.1 2.4 fusion.113
  86.5 14.5 %fusion.110 = bf16[32,256,1,1,64]{1,4,0,3,2:T(8,128)(2,1)} fusion(f32[32,256,256]{1,2,0:T(8,128)} %fusion.124, bf16[32,256,1,3,64]{1,4,3,0,2:T(8,128)(2,1)} %copy-done.3, f32[32,256,256]{1,2,0:T(8,128)} %copy-done.21, f32[32,256]{1,0:T(8,128)S(1)} %get-tuple-element.14), kind=kOutput, calls=%fused_computation.112 | convolution fusion | flops 283648256 | bytes 35717120 | tf_op jit(solution)/shard_map/bnqk,bknd->bqnd/dot_general | solution.py:53
  100.9 14.6 %fusion.107 = bf16[32,256,1,1,64]{1,4,0,3,2:T(8,128)(2,1)} fusion(f32[32,256,256]{1,2,0:T(8,128)} %fusion.124, bf16[32,256,1,3,64]{1,4,3,0,2:T(8,128)(2,1)} %copy-done.3, f32[32,256,256]{1,2,0:T(8,128)} %copy-done.21, f32[32,256]{1,0:T(8,128)S(1)} %get-tuple-element.14), kind=kOutput, calls=%fused_computation.111 | convolution fusion | flops 283648256 | bytes 35717120 | tf_op jit(solution)/shard_map/bnqk,bqnd->bknd/dot_general | solution.py:54
  115.5 4.6 fusion.116
  120.1 0.0 copy-done.16
  120.1 0.0 copy-done.12
  120.1 0.0 copy-done.14
  120.2 0.0 copy-done
  120.2 0.0 copy-start.18
  120.2 16.9 %convert_reduce_fusion.1 = (u32[256,256]{1,0:T(8,128)S(1)}, bf16[32,256,256]{2,1,0:T(8,128)(2,1)S(1)}) fusion(bf16[2048,256]{1,0:T(8,128)(2,1)S(1)} %copy-done, bf16[32,256,2048]{2,1,0:T(8,128)(2,1)} %param.8, f32[2048]{0:T(1024)S(1)} %convert_element_type.125, f32[32,256]{1,0:T(8,128)S(1)} %add_rsqrt_fusion, f32[32,256]{1,0:T(8,128)S(1)} %broadcast_multiply_fusion.2), kind=kOutput, calls=%fused_computation.74 | convolution fusion | flops 8690532352 | bytes 39133184 | tf_op jit(solution)/shard_map/bsh,hf->bsf/dot_general | solution.py:65
  137.1 0.0 copy-start.22
  137.1 1.9 copy-done.22
  139.0 0.0 copy-done.18
  139.0 33.1 %fusion.59 = bf16[32,256,256]{2,1,0:T(8,128)(2,1)} fusion(bf16[32,256,256]{2,1,0:T(8,128)(2,1)S(1)} %get-tuple-element.17, bf16[32,256,2048]{2,1,0:T(8,128)(2,1)} %param.15, bf16[256,2048]{1,0:T(8,128)(2,1)S(1)} %copy-done.18, u32[256,256]{1,0:T(8,128)S(1)} %get-tuple-element.16), kind=kOutput, calls=%fused_computation.71 | convolution fusion | flops 8751415296 | bytes 43253760 | tf_op jit(solution)/shard_map/bsh,fh->bsf/dot_general | solution.py:73
  172.2 25.4 %fusion.121 = f32[32,256,2048]{2,1,0:T(8,128)} fusion(bf16[32,256,256]{2,1,0:T(8,128)(2,1)} %fusion.59, bf16[2048,256]{1,0:T(8,128)(2,1)S(1)} %copy-done), kind=kOutput, calls=%fused_computation.120 | convolution fusion | flops 8589934592 | bytes 72351744 | tf_op jit(solution)/shard_map/bsf,hf->bsh/dot_general | solution.py:78
  197.6 0.0 copy-done.9
  197.6 23.1 %fusion.129 = f32[32,256,2048]{2,1,0:T(8,128)} fusion(bf16[32,256,64]{1,2,0:T(8,128)(2,1)S(1)} %fusion.116, bf16[1,64,2048]{2,1,0:T(8,128)(2,1)S(1)} %copy-done.9), kind=kOutput, calls=%fused_computation.128 | convolution fusion | flops 2147483648 | bytes 68419584 | tf_op jit(solution)/shard_map/bqnd,ndh->bqh/dot_general | solution.py:67
  220.7 0.0 copy-done.19
  220.8 0.0 copy-start.11
  220.8 42.5 %add_convert_fusion = bf16[32,256,2048]{2,1,0:T(8,128)(2,1)} fusion(f32[32,256,2048]{2,1,0:T(8,128)} %fusion.129, bf16[256,2048]{1,0:T(8,128)(2,1)S(1)} %copy-done.19, bf16[32,256,256]{2,1,0:T(8,128)(2,1)} %copy-done.22, u32[256,256]{1,0:T(8,128)S(1)} %get-tuple-element.16), kind=kOutput, calls=%fused_computation.25 | convolution fusion | flops 8766095360 | bytes 106168320 | tf_op jit(solution)/shard_map/bsf,fh->bsh/dot_general | solution.py:67
  263.3 0.0 copy-done.4
  263.3 0.0 copy-done.5
  263.3 0.0 copy-done.6
  263.3 0.0 copy-done.11
  263.3 32.3 %fusion.18 = bf16[32,256,2048]{2,1,0:T(8,128)(2,1)} fusion(f32[32,256,2048]{2,1,0:T(8,128)} %fusion.121, bf16[32,256,1,1,64]{1,4,0,3,2:T(8,128)(2,1)S(1)} %copy-done.4, bf16[32,256,1,1,64]{1,4,0,3,2:T(8,128)(2,1)S(1)} %copy-done.6, bf16[32,256,1,1,64]{1,4,0,3,2:T(8,128)(2,1)S(1)} %copy-done.5, bf16[2048,1,3,64]{0,3,2,1:T(8,128)(2,1)S(1)} %copy-done.11), kind=kOutput, calls=%fused_computation.24 | convolution fusion | flops 6479151104 | bytes 104595456 | tf_op jit(solution)/shard_map/bsnjd,hnjd->bsh/dot_general | solution.py:78
  295.7 0.1 all-reduce.3.cloned.1.call-update
  295.7 0.0 copy-start.7
  295.7 0.0 copy-start.13
  295.7 0.0 copy-start.15
  295.7 0.0 copy-start.17
  295.8 14.4 %fusion.90 = bf16[1,64,2048]{2,1,0:T(8,128)(2,1)} fusion(bf16[32,256,64]{1,2,0:T(8,128)(2,1)S(1)} %fusion.116, bf16[32,256,2048]{2,1,0:T(8,128)(2,1)} %param.15), kind=kOutput, calls=%fused_computation.101 | convolution fusion | flops 2147614720 | bytes 34865152 | tf_op jit(solution)/shard_map/bsnd,bsh->ndh/dot_general | solution.py:70
  310.1 0.0 copy-done.7
  310.1 0.0 copy-done.13
  310.1 0.0 copy-done.15
  310.1 0.0 copy-done.17
  310.2 0.0 copy-start.2
  310.2 18.5 %fusion.84 = bf16[2048,1,3,64]{0,3,2,1:T(8,128)(2,1)} fusion(bf16[32,256,1,1,64]{1,4,0,3,2:T(8,128)(2,1)S(1)} %copy-done.4, bf16[32,256,1,1,64]{1,4,0,3,2:T(8,128)(2,1)S(1)} %copy-done.7, bf16[32,256,1,1,64]{1,4,0,3,2:T(8,128)(2,1)S(1)} %copy-done.5, bf16[32,256,2048]{2,1,0:T(8,128)(2,1)} %param.8, f32[2048]{0:T(1024)S(1)} %copy-done.17, ...), kind=kOutput, calls=%fused_computation.98 | convolution fusion | flops 6536167424 | bytes 37560320 | tf_op jit(solution)/shard_map/bsh,bsnjd->hnjd/dot_general | solution.py:76
  328.7 0.0 copy-done.2
  328.7 20.9 %fusion.79 = bf16[2048,256]{1,0:T(8,128)(2,1)} fusion(bf16[32,256,256]{2,1,0:T(8,128)(2,1)S(1)} %copy-done.2, bf16[32,256,2048]{2,1,0:T(8,128)(2,1)} %param.8, f32[2048]{0:T(1024)S(1)} %copy-done.17, f32[32,256]{1,0:T(8,128)S(1)} %copy-done.15, f32[32,256]{1,0:T(8,128)S(1)} %copy-done.13), kind=kOutput, calls=%fused_computation.95 | convolution fusion | flops 8674344960 | bytes 38871040 | tf_op jit(solution)/shard_map/bsh,bsf->hf/dot_general | solution.py:77
  349.6 30.2 %fusion.80 = bf16[256,2048]{1,0:T(8,128)(2,1)} fusion(bf16[32,256,2048]{2,1,0:T(8,128)(2,1)} %param.15, bf16[32,256,256]{2,1,0:T(8,128)(2,1)S(1)} %copy-done.23, u32[256,256]{1,0:T(8,128)S(1)} %get-tuple-element.16), kind=kOutput, calls=%fused_computation.96 | convolution fusion | flops 8733065216 | bytes 39059456 | tf_op jit(solution)/shard_map/bsf,bsh->fh/dot_general | solution.py:71
  379.7 354.6 %all-reduce.3.cloned.1.call-done = (bf16[32,256,2048]{2,1,0:T(8,128)(2,1)}, bf16[32,256,2048]{2,1,0:T(8,128)(2,1)}) async-done(((bf16[32,256,2048]{2,1,0:T(8,128)(2,1)}, bf16[32,256,2048]{2,1,0:T(8,128)(2,1)}), (bf16[32,256,2048]{2,1,0:T(8,128)(2,1)}, bf16[32,256,2048]{2,1,0:T(8,128)(2,1)})) %all-reduce.3.cloned.1.call-update) | async-done | bytes 67108880 | tf_op jit(solution)/shard_map/psum | solution.py:68
  734.4 35.7 %fusion.16 = (bf16[2048]{0:T(1024)(128)(2,1)}, f32[32,256]{1,0:T(8,128)S(1)}, f32[32,256]{1,0:T(8,128)S(1)}) fusion(bf16[32,256,2048]{2,1,0:T(8,128)(2,1)} %param.8, bf16[32,256,2048]{2,1,0:T(8,128)(2,1)} %get-tuple-element.11, f32[32,256]{1,0:T(8,128)S(1)} %copy-done.15, f32[32,256]{1,0:T(8,128)S(1)} %copy-done.13, f32[2048]{0:T(1024)S(1)} %copy-done.17), kind=kLoop, calls=%fused_computation.21 | loop fusion | flops 167753728 | bytes 67252224 | tf_op jit(solution)/shard_map/reduce_sum | solution.py:20
  770.1 70.8 %fusion.13 = (bf16[32,256,2048]{2,1,0:T(8,128)(2,1)}, bf16[32,256,2048]{2,1,0:T(8,128)(2,1)}) fusion(bf16[32,256,2048]{2,1,0:T(8,128)(2,1)} %param.8, bf16[32,256,2048]{2,1,0:T(8,128)(2,1)} %get-tuple-element.11, bf16[32,256,2048]{2,1,0:T(8,128)(2,1)} %param.15, f32[32,256]{1,0:T(8,128)S(1)} %get-tuple-element.18, f32[32,256]{1,0:T(8,128)S(1)} %get-tuple-element.19, ...), kind=kLoop, calls=%fused_computation.18 | loop fusion | flops 251658240 | bytes 201465856 | tf_op jit(solution)/shard_map/convert_element_type | solution.py:81
  (15 shorter events, 0.1 us)
Async XLA Ops:
  7.2 113.0 %copy-start = (bf16[2048,256]{1,0:T(8,128)(2,1)S(1)}, bf16[2048,256]{1,0:T(8,128)(2,1)}, u32[]{:S(2)}) copy-start(bf16[2048,256]{1,0:T(8,128)(2,1)} %param.13) | copy-start | bytes 3145732
  7.2 727.2 %all-reduce.3.cloned.1.call-start = ((), (), s32[]{:S(2)}) async-start(), calls=%async_computation | async-start | bytes 134217728 | tf_op jit(solution)/shard_map/psum | solution.py:68
  8.1 112.1 %copy-start.16 = (f32[2048]{0:T(1024)}, f32[2048]{0:T(1024)S(1)}, u32[]{:S(2)}) copy-start(f32[2048]{0:T(1024)S(1)} %convert_element_type.125) | copy-start | bytes 24580
  19.3 100.9 %copy-start.12 = (f32[32,256]{1,0:T(8,128)}, f32[32,256]{1,0:T(8,128)S(1)}, u32[]{:S(2)}) copy-start(f32[32,256]{1,0:T(8,128)S(1)} %broadcast_multiply_fusion.2) | copy-start | bytes 98308
  19.3 13.0 %copy-start.10 = (bf16[2048,1,3,64]{0,3,2,1:T(8,128)(2,1)S(1)}, bf16[2048,1,3,64]{0,3,2,1:T(8,128)(2,1)}, u32[]{:S(2)}) copy-start(bf16[2048,1,3,64]{0,3,2,1:T(8,128)(2,1)} %param.11) | copy-start | bytes 2359300
  32.3 87.9 %copy-start.14 = (f32[32,256]{1,0:T(8,128)}, f32[32,256]{1,0:T(8,128)S(1)}, u32[]{:S(2)}) copy-start(f32[32,256]{1,0:T(8,128)S(1)} %add_rsqrt_fusion) | copy-start | bytes 98308
  49.5 1.7 copy-start.3
  51.2 1.3 copy-start.8
  69.2 6.0 copy-start.20
  80.7 3.4 copy-start.21
  120.2 18.9 %copy-start.18 = (bf16[256,2048]{1,0:T(8,128)(2,1)S(1)}, bf16[256,2048]{1,0:T(8,128)(2,1)}, u32[]{:S(2)}) copy-start(bf16[256,2048]{1,0:T(8,128)(2,1)} %param.14) | copy-start | bytes 3145732
  137.1 1.9 copy-start.22
  172.2 25.5 %copy-start.9 = (bf16[1,64,2048]{2,1,0:T(8,128)(2,1)S(1)}, bf16[1,64,2048]{2,1,0:T(8,128)(2,1)}, u32[]{:S(2)}) copy-start(bf16[1,64,2048]{2,1,0:T(8,128)(2,1)} %param.12) | copy-start | bytes 786436
  197.6 23.1 %copy-start.19 = (bf16[256,2048]{1,0:T(8,128)(2,1)S(1)}, bf16[256,2048]{1,0:T(8,128)(2,1)}, u32[]{:S(2)}) copy-start(bf16[256,2048]{1,0:T(8,128)(2,1)} %param.14) | copy-start | bytes 3145732
  220.8 42.5 %copy-start.4 = (bf16[32,256,1,1,64]{1,4,0,3,2:T(8,128)(2,1)S(1)}, bf16[32,256,1,1,64]{1,4,0,3,2:T(8,128)(2,1)}, u32[]{:S(2)}) copy-start(bf16[32,256,1,1,64]{1,4,0,3,2:T(8,128)(2,1)} %fusion.113) | copy-start | bytes 3145732
  220.8 42.5 %copy-start.5 = (bf16[32,256,1,1,64]{1,4,0,3,2:T(8,128)(2,1)S(1)}, bf16[32,256,1,1,64]{1,4,0,3,2:T(8,128)(2,1)}, u32[]{:S(2)}) copy-start(bf16[32,256,1,1,64]{1,4,0,3,2:T(8,128)(2,1)} %fusion.110) | copy-start | bytes 3145732
  220.8 42.5 %copy-start.6 = (bf16[32,256,1,1,64]{1,4,0,3,2:T(8,128)(2,1)S(1)}, bf16[32,256,1,1,64]{1,4,0,3,2:T(8,128)(2,1)}, u32[]{:S(2)}) copy-start(bf16[32,256,1,1,64]{1,4,0,3,2:T(8,128)(2,1)} %fusion.107) | copy-start | bytes 3145732
  220.8 42.5 %copy-start.11 = (bf16[2048,1,3,64]{0,3,2,1:T(8,128)(2,1)S(1)}, bf16[2048,1,3,64]{0,3,2,1:T(8,128)(2,1)}, u32[]{:S(2)}) copy-start(bf16[2048,1,3,64]{0,3,2,1:T(8,128)(2,1)} %param.11) | copy-start | bytes 2359300
  295.7 14.4 %copy-start.7 = (bf16[32,256,1,1,64]{1,4,0,3,2:T(8,128)(2,1)S(1)}, bf16[32,256,1,1,64]{1,4,0,3,2:T(8,128)(2,1)}, u32[]{:S(2)}) copy-start(bf16[32,256,1,1,64]{1,4,0,3,2:T(8,128)(2,1)} %fusion.107) | copy-start | bytes 3145732
  295.7 14.4 %copy-start.13 = (f32[32,256]{1,0:T(8,128)S(1)}, f32[32,256]{1,0:T(8,128)}, u32[]{:S(2)}) copy-start(f32[32,256]{1,0:T(8,128)} %copy-done.12) | copy-start | bytes 98308
  295.7 14.4 %copy-start.15 = (f32[32,256]{1,0:T(8,128)S(1)}, f32[32,256]{1,0:T(8,128)}, u32[]{:S(2)}) copy-start(f32[32,256]{1,0:T(8,128)} %copy-done.14) | copy-start | bytes 98308
  295.7 14.4 %copy-start.17 = (f32[2048]{0:T(1024)S(1)}, f32[2048]{0:T(1024)}, u32[]{:S(2)}) copy-start(f32[2048]{0:T(1024)} %copy-done.16) | copy-start | bytes 24580
  310.2 18.5 %copy-start.2 = (bf16[32,256,256]{2,1,0:T(8,128)(2,1)S(1)}, bf16[32,256,256]{2,1,0:T(8,128)(2,1)}, u32[]{:S(2)}) copy-start(bf16[32,256,256]{2,1,0:T(8,128)(2,1)} %fusion.59) | copy-start | bytes 12582916
  328.7 20.9 %copy-start.23 = (bf16[32,256,256]{2,1,0:T(8,128)(2,1)S(1)}, bf16[32,256,256]{2,1,0:T(8,128)(2,1)}, u32[]{:S(2)}) copy-start(bf16[32,256,256]{2,1,0:T(8,128)(2,1)} %copy-done.22) | copy-start | bytes 12582916
  770.1 70.8 %copy-start.1 = (bf16[2048,256]{1,0:T(8,128)(2,1)S(1)}, bf16[2048,256]{1,0:T(8,128)(2,1)}, u32[]{:S(2)}) copy-start(bf16[2048,256]{1,0:T(8,128)(2,1)} %param.13) | copy-start | bytes 3145732
Sparse Core Ops, SparseCore 0:
  295.8 438.4 all-reduce.2
where the time goes:
time: 856 us; the launch traced here: 848 us
  waiting for transfers between devices  355 us (41%)
  matrix products  335 us (39%)
  other arithmetic  137 us (16%)
  between operations  14.5 us (2%)
    psum x1, waiting for transfers between devices, body(): mixed = lax.psum(share.astype(jnp.bfloat16), 'model')  355 us
    convert_element_type x1, other arithmetic, body(): dx_out = (dy_in.astype(jnp.float32) + d_x).astype(jnp.bfloat16)  70.8 us
    dot_general x1, matrix products, body(): jnp.einsum('bsf,fh->bsh', hidden_act, w_down, preferred_element_type=jnp....  42.5 us
    reduce_sum x1, other arithmetic, layer_norm_bwd(): d_gain = jnp.sum(grad_f32 * normed_f32, axis=(0, 1))  35.7 us
    dot_general x1, matrix products, body(): jnp.einsum('bsh,fh->bsf', dy_in, w_down, preferred_element_type=jnp.float32)  33.1 us
    dot_general x1, matrix products, body(): jnp.einsum('bsnjd,hnjd->bsh', d_qkv, w_qkv, preferred_element_type=jnp.fl...  32.3 us
    dot_general x1, matrix products, body(): jnp.einsum('bsf,bsh->fh', hidden_act, dy_in, preferred_element_type=jnp.f...  30.2 us
    dot_general x1, matrix products, body(): jnp.einsum('bsf,hf->bsh', d_up, w_up, preferred_element_type=jnp.float32)  25.4 us
  transfers between devices with their start and end apart: 1, of which 1 were waited for; matrix products, arithmetic and copies ran while one was open for 10% of the time, Pallas kernels for 0%

commit v1 on v0

v1 whole, which is shorter than its diff:
```python
import functools

import jax
import jax.numpy as jnp
from jax import lax
from jax.experimental import pallas as pl
from jax.experimental.pallas import tpu as pltpu
from jax.sharding import PartitionSpec as P

LN_EPS = 1e-5
PAIR = 2
NT = (((1,), (1,)), ((), ()))
NN = (((1,), (0,)), ((), ()))
TN = (((0,), (0,)), ((), ()))


def dot(lhs, rhs, dims):
    return lax.dot_general(lhs, rhs, dims, preferred_element_type=jnp.float32)


def norm_rows(x_f32):
    mean_val = jnp.mean(x_f32, axis=-1, keepdims=True)
    centered = x_f32 - mean_val
    inv_std = lax.rsqrt(jnp.mean(centered * centered, axis=-1, keepdims=True) + LN_EPS)
    return centered * inv_std, inv_std


def rows_kernel(first, x_ref, dy_ref, seg_ref, gain_ref, wqkv_ref, wo_ref, w1_ref, w2_ref, *refs):
    if first:
        md_ref, acc_in, acc_out, a_scr = refs
    else:
        prev_in, prev_out, md_ref, acc_in, acc_out, a_scr = refs
    seqs, seq_len, hidden = x_ref.shape
    head_dim = wo_ref.shape[0]
    tokens = seqs * seq_len

    @pl.when(pl.program_id(0) == 0)
    def _():
        if first:
            acc_in[...] = jnp.zeros_like(acc_in)
            acc_out[...] = jnp.zeros_like(acc_out)
        else:
            acc_in[...] = prev_in[...]
            acc_out[...] = prev_out[...]

    gain = gain_ref[...].astype(jnp.float32)
    sub = 64
    for t in range(0, tokens, sub):
        s, o = t // seq_len, t % seq_len
        normed, _ = norm_rows(x_ref[s, o:o + sub, :].astype(jnp.float32))
        a_scr[t:t + sub, :] = (normed * gain).astype(jnp.bfloat16)

    a_all = a_scr[...]
    dy_all = dy_ref[...].reshape(tokens, hidden)
    qkv = dot(a_all, wqkv_ref[...], NT).astype(jnp.bfloat16)
    up = dot(a_all, w1_ref[...], NN).astype(jnp.bfloat16).astype(jnp.float32)
    d_attn = dot(dy_all, wo_ref[...], NT).astype(jnp.bfloat16)
    d_hid = dot(dy_all, w2_ref[...], NT).astype(jnp.bfloat16).astype(jnp.float32)
    cdf = 0.5 * (1.0 + lax.erf(up * (0.5 ** 0.5)))
    hid = (up * cdf).astype(jnp.bfloat16)
    slope = cdf + up * (jnp.exp(-0.5 * up * up) * 0.3989422804014327)
    d_up = (d_hid * slope).astype(jnp.bfloat16)

    scale = head_dim ** -0.5
    rows_id = lax.broadcasted_iota(jnp.int32, (seq_len, seq_len), 0)
    cols_id = lax.broadcasted_iota(jnp.int32, (seq_len, seq_len), 1)
    causal = cols_id <= rows_id
    outs, d_qkvs = [], []
    for s in range(seqs):
        lo, hi = s * seq_len, (s + 1) * seq_len
        query = qkv[lo:hi, :head_dim]
        keys = qkv[lo:hi, head_dim:2 * head_dim]
        values = qkv[lo:hi, 2 * head_dim:]
        d_o = d_attn[lo:hi]
        seg_cols = jnp.broadcast_to(seg_ref[s], (seq_len, seq_len))
        allowed = causal & (seg_cols == seg_cols.T)
        scores = jnp.where(allowed, dot(query, keys, NT) * scale, -1e30)
        expd = jnp.exp(scores - jnp.max(scores, axis=-1, keepdims=True))
        probs = expd / jnp.sum(expd, axis=-1, keepdims=True)
        probs_b = probs.astype(jnp.bfloat16)
        outs.append(dot(probs_b, values, NN).astype(jnp.bfloat16))
        d_p = dot(d_o, values, NT)
        d_s = (probs * (d_p - jnp.sum(d_p * probs, axis=-1, keepdims=True)) * scale).astype(jnp.bfloat16)
        d_q = dot(d_s, keys, NN).astype(jnp.bfloat16)
        d_k = dot(d_s, query, TN).astype(jnp.bfloat16)
        d_v = dot(probs_b, d_o, TN).astype(jnp.bfloat16)
        d_qkvs.append(jnp.concatenate([d_q, d_k, d_v], axis=-1))
    attn = jnp.concatenate(outs, axis=0)
    d_qkv = jnp.concatenate(d_qkvs, axis=0)

    devs, _, per, _ = md_ref.shape
    width_qkv = d_qkv.shape[1]
    step = 512
    for h in range(0, hidden, step):
        cols = slice(h, h + step)
        share = dot(attn, wo_ref[:, cols], NN) + dot(hid, w2_ref[:, cols], NN)
        md_ref[:, 0, :, cols] = share.astype(jnp.bfloat16).reshape(devs, per, step)
        d_share = dot(d_qkv, wqkv_ref[:, cols], NN) + dot(d_up, w1_ref[cols, :], NT)
        md_ref[:, 1, :, cols] = d_share.astype(jnp.bfloat16).reshape(devs, per, step)
        a_cols = a_scr[:, cols]
        dy_cols = dy_ref[:, :, cols].reshape(tokens, step)
        acc_in[:width_qkv, cols] += dot(d_qkv, a_cols, TN)
        acc_in[width_qkv:, cols] += dot(d_up, a_cols, TN)
        acc_out[:head_dim, cols] += dot(attn, dy_cols, TN)
        acc_out[head_dim:, cols] += dot(hid, dy_cols, TN)


def rows_call(start, count, devices, x_in, dy_in, seg, gain, wqkv, wo, w1, w2, prev):
    _, seq_len, hidden = x_in.shape
    per = count * seq_len // devices
    tokens = PAIR * seq_len
    base = start // PAIR
    width_in = wqkv.shape[0] + w1.shape[1]
    width_out = wo.shape[0] + w2.shape[0]
    row_spec = pl.BlockSpec((PAIR, seq_len, hidden), lambda i: (base + i, 0, 0))
    whole = lambda shape: pl.BlockSpec(shape, lambda i: (0,) * len(shape), pipeline_mode=pl.Buffered(1))
    acc_specs = [whole((width_in, hidden)), whole((width_out, hidden))]
    acc_shapes = [jax.ShapeDtypeStruct((width_in, hidden), jnp.float32), jax.ShapeDtypeStruct((width_out, hidden), jnp.float32)]
    args = [x_in, dy_in, seg, gain, wqkv, wo, w1, w2]
    in_specs = [row_spec, row_spec, pl.BlockSpec((PAIR, 1, seq_len), lambda i: (base + i, 0, 0)),
                whole(gain.shape), whole(wqkv.shape), whole(wo.shape), whole(w1.shape), whole(w2.shape)]
    aliases = {}
    if prev is not None:
        args += list(prev)
        in_specs += acc_specs
        aliases = {8: 1, 9: 2}
    flops = 2 * count * seq_len * hidden * (width_in * 3 + width_out * 3)
    return pl.pallas_call(
        functools.partial(rows_kernel, prev is None),
        grid=(count // PAIR,),
        in_specs=in_specs,
        out_specs=[pl.BlockSpec((tokens // per, 2, per, hidden), lambda i: (i, 0, 0, 0))] + acc_specs,
        out_shape=[jax.ShapeDtypeStruct((devices, 2, per, hidden), jnp.bfloat16)] + acc_shapes,
        input_output_aliases=aliases,
        scratch_shapes=[pltpu.VMEM((tokens, hidden), jnp.bfloat16)],
        cost_estimate=pl.CostEstimate(flops=flops, bytes_accessed=count * seq_len * hidden * 8, transcendentals=0),
        compiler_params=pltpu.CompilerParams(vmem_limit_bytes=60 * 2 ** 20),
        name=f"rows_{start}",
    )(*args)


def place_kernel(y_part, dx_part, *refs):
    y_out, dx_out = refs[-2:]
    y_out[...] = y_part[...].reshape(y_out.shape)
    dx_out[...] = dx_part[...].reshape(dx_out.shape)


def place_call(start, count, gathered, shape, dtype, prev):
    rows, seq_len, hidden = shape
    _, _, per, _ = gathered.shape
    spread = seq_len // per
    out_spec = pl.BlockSpec((1, seq_len, hidden), lambda i: (start + i, 0, 0))
    args = [gathered, gathered]
    in_specs = [pl.BlockSpec((spread, 1, per, hidden), lambda i: (i, 0, 0, 0)), pl.BlockSpec((spread, 1, per, hidden), lambda i: (i, 1, 0, 0))]
    aliases = {}
    if prev is not None:
        args += list(prev)
        in_specs += [pl.BlockSpec(memory_space=pl.ANY)] * 2
        aliases = {2: 0, 3: 1}
    return pl.pallas_call(
        place_kernel,
        grid=(count,),
        in_specs=in_specs,
        out_specs=[out_spec, out_spec],
        out_shape=[jax.ShapeDtypeStruct(shape, dtype)] * 2,
        input_output_aliases=aliases,
        cost_estimate=pl.CostEstimate(flops=count * seq_len * hidden * 64, bytes_accessed=count * seq_len * hidden * 8, transcendentals=0),
        name=f"place_{start}",
    )(*args)


def chunk_sizes(rows):
    return [rows // 8, rows // 8, rows // 4, rows // 4, rows // 4]


def solution(mesh):
    devices = mesh.shape['model']

    def body(x_in, seg_ids, ln_gain, w_qkv, w_out, w_up, w_down, dy_in):
        rows, seq_len, hidden = x_in.shape
        wqkv = w_qkv.transpose(1, 2, 3, 0).reshape(-1, hidden)
        wo = w_out.reshape(-1, hidden)
        seg = seg_ids.reshape(rows, 1, seq_len)
        gain = ln_gain.reshape(1, hidden)
        gain_f32 = ln_gain.astype(jnp.float32)
        me = lax.axis_index('model')
        x_flat = x_in.reshape(rows * seq_len, hidden)
        dy_flat = dy_in.reshape(rows * seq_len, hidden)

        acc, start, parts = None, 0, []
        for count in chunk_sizes(rows):
            shares, *acc = rows_call(start, count, devices, x_in, dy_in, seg, gain, wqkv, wo, w_up, w_down, acc)
            parts.append((start, count, lax.psum_scatter(shares, 'model', scatter_dimension=0, tiled=False)))
            start += count

        d_gain = jnp.zeros((hidden,), jnp.float32)
        local = []
        for start, count, summed in parts:
            per = summed.shape[1]
            at = start * seq_len + me * per
            x_f32 = lax.dynamic_slice_in_dim(x_flat, at, per, 0).astype(jnp.float32)
            dy_f32 = lax.dynamic_slice_in_dim(dy_flat, at, per, 0).astype(jnp.float32)
            normed, inv_std = norm_rows(x_f32)
            y_loc = (x_f32 + summed[0].astype(jnp.float32)).astype(jnp.bfloat16)
            grad = summed[1].astype(jnp.float32)
            d_gain += jnp.sum(grad * normed, axis=0)
            d_hat = grad * gain_f32
            d_x = inv_std * (d_hat - jnp.mean(d_hat, axis=-1, keepdims=True) - normed * jnp.mean(d_hat * normed, axis=-1, keepdims=True))
            dx_loc = (dy_f32 + d_x).astype(jnp.bfloat16)
            local.append((start, count, jnp.stack([y_loc, dx_loc])))
        out = None
        for start, count, pair in reversed(local):
            gathered = lax.all_gather(pair, 'model', axis=0, tiled=False)
            out = place_call(start, count, gathered, x_in.shape, x_in.dtype, out)
        d_gain = lax.psum(d_gain, 'model').astype(jnp.bfloat16)
        acc_in, acc_out = acc
        n_qkv = wqkv.shape[0]
        d_wqkv = acc_in[:n_qkv].astype(jnp.bfloat16).reshape(w_qkv.shape[1:] + (hidden,)).transpose(3, 0, 1, 2)
        d_wup = acc_in[n_qkv:].astype(jnp.bfloat16).T
        n_o = wo.shape[0]
        d_wout = acc_out[:n_o].astype(jnp.bfloat16).reshape(w_out.shape)
        d_wdown = acc_out[n_o:].astype(jnp.bfloat16)
        return out[0], out[1], d_gain, d_wqkv, d_wout, d_wup, d_wdown

    in_specs = (P('data'), P('data'), P(), P(None, 'model'), P('model'), P(None, 'model'), P('model'), P('data'))
    out_specs = (P('data'), P('data'), P('data'), P('data', 'model'), P(('data', 'model')), P('data', 'model'), P(('data', 'model')))
    return jax.shard_map(body, mesh=mesh, in_specs=in_specs, out_specs=out_specs, check_vma=False)
```

time: 856 us -> 1030 us (1.20)
  waiting for transfers between devices: 355 us -> 691 us
  matrix products: 335 us -> 0 us
  Pallas kernels: 0 us -> 240 us
  other arithmetic: 137 us -> 21 us
  blocking collectives: 0 us -> 47.8 us
    reduce_scatter x0 -> x5, waiting for transfers between devices: none -> 490 us  [body(): lax.psum_scatter(shares, 'model', scatter_dimension=0, tiled=False)]
    psum x1 -> x0, waiting for transfers between devices: 355 us -> none  [body(): mixed = lax.psum(share.astype(jnp.bfloat16), 'model')]
    dot_general x18 -> x0, matrix products: 335 us -> none  [the longest x1 42.5 us: body(): jnp.einsum('bsf,fh->bsh', hidden_act, w_down, preferred_element_type=jnp....]
    pallas_call x0 -> x10, Pallas kernels: none -> 240 us  [the longest x5 185 us: rows_call(): pl.pallas_call(functools.partial(rows_kernel, prev is None), grid=(count...]
    all_gather x0 -> x5, waiting for transfers between devices: none -> 198 us  [body(): gathered = lax.all_gather(pair, 'model', axis=0, tiled=False)]
    convert_element_type x2 -> x1, other arithmetic: 71.6 us -> 0.01 us  [body(): gain_f32 = ln_gain.astype(jnp.float32)]
    reduce_sum x3 -> x6, other arithmetic: 59.9 us -> 9.36 us  [the longest x2 4.14 us: body(): d_gain += jnp.sum(grad * normed, axis=0)]
    psum x0 -> x1, blocking collectives: none -> 47.8 us  [body(): d_gain = lax.psum(d_gain, 'model').astype(jnp.bfloat16)]
  transfers between devices with their start and end apart: 1 -> 10, of which waited for: 1 -> 10; matrix products, arithmetic and copies ran while one was open for 10% -> 3% of each run, Pallas kernels for 0% -> 5%
where the time goes in v1:
time: 1030 us
  waiting for transfers between devices  691 us (67%)
  Pallas kernels  240 us (23%)
  blocking collectives  47.8 us (5%)
  other arithmetic  21 us (2%)
  between operations  14.9 us (1%)
    reduce_scatter x5, waiting for transfers between devices, body(): lax.psum_scatter(shares, 'model', scatter_dimension=0, tiled=False)  490 us
    all_gather x5, waiting for transfers between devices, body(): gathered = lax.all_gather(pair, 'model', axis=0, tiled=False)  198 us
    pallas_call x5, Pallas kernels, rows_call(): pl.pallas_call(functools.partial(rows_kernel, prev is None), grid=(count...  185 us
    pallas_call x5, Pallas kernels, place_call(): pl.pallas_call(place_kernel, grid=(count,), in_specs=in_specs, out_specs=...  55 us
    psum x1, blocking collectives, body(): d_gain = lax.psum(d_gain, 'model').astype(jnp.bfloat16)  47.8 us
  transfers between devices with their start and end apart: 10, of which 10 were waited for; matrix products, arithmetic and copies ran while one was open for 3% of the time, Pallas kernels for 5%

profile of v1, /device:TPU:97, one launch (start us, length us, event | category | flops | bytes accessed | tf_op | source)
XLA Modules:
  0.0 1025.1 jit_solution(3044252134263668607)
XLA Ops:
  7.2 0.1 reduce-scatter.14.cloned.1.call-start
  7.2 1.4 reshape.180.seg_ref
  8.6 1.3 reshape.181.gain_ref
  9.9 24.9 %rows_0.1 = (bf16[32,2,32,2048]{3,2,1,0:T(8,128)(2,1)}, f32[448,2048]{1,0:T(8,128)}, f32[320,2048]{1,0:T(8,128)}) custom-call(bf16[32,256,2048]{2,1,0:T(8,128)(2,1)} %x_ref.9, bf16[32,256,2048]{2,1,0:T(8,128)(2,1)} %dy_ref.9, s32[32,1,256]{2,1,0:T(1,128)} %reshape.180.seg_ref, bf16[1,2048]{1,0:T(2,128)(2,1)} %reshape.181.gain_ref, ...), custom_call_target="tpu_custom_call" | custom-call | flops 9663676416 | bytes 16777216 | tf_op jit(solution)/shard_map/rows_0/pallas_call | solution.py:128
  34.8 27.3 %rows_4.1 = (bf16[32,2,32,2048]{3,2,1,0:T(8,128)(2,1)}, f32[448,2048]{1,0:T(8,128)}, f32[320,2048]{1,0:T(8,128)}) custom-call(bf16[32,256,2048]{2,1,0:T(8,128)(2,1)} %x_ref.9, bf16[32,256,2048]{2,1,0:T(8,128)(2,1)} %dy_ref.9, s32[32,1,256]{2,1,0:T(1,128)} %reshape.180.seg_ref, ...), custom_call_target="tpu_custom_call", output_to_operand_aliasing={{1}: (8, {}), {2}: (9, {})} | custom-call | flops 9663676416 | bytes 16777216 | tf_op jit(solution)/shard_map/rows_4/pallas_call | solution.py:128
  62.1 44.4 %rows_8.1 = (bf16[32,2,64,2048]{3,2,1,0:T(8,128)(2,1)}, f32[448,2048]{1,0:T(8,128)}, f32[320,2048]{1,0:T(8,128)}) custom-call(bf16[32,256,2048]{2,1,0:T(8,128)(2,1)} %x_ref.9, bf16[32,256,2048]{2,1,0:T(8,128)(2,1)} %dy_ref.9, s32[32,1,256]{2,1,0:T(1,128)} %reshape.180.seg_ref, ...), custom_call_target="tpu_custom_call", output_to_operand_aliasing={{1}: (8, {}), {2}: (9, {})} | custom-call | flops 19327352832 | bytes 33554432 | tf_op jit(solution)/shard_map/rows_8/pallas_call | solution.py:128
  106.5 44.4 %rows_16.1 = (bf16[32,2,64,2048]{3,2,1,0:T(8,128)(2,1)}, f32[448,2048]{1,0:T(8,128)}, f32[320,2048]{1,0:T(8,128)}) custom-call(bf16[32,256,2048]{2,1,0:T(8,128)(2,1)} %x_ref.9, bf16[32,256,2048]{2,1,0:T(8,128)(2,1)} %dy_ref.9, s32[32,1,256]{2,1,0:T(1,128)} %reshape.180.seg_ref, ...), custom_call_target="tpu_custom_call", output_to_operand_aliasing={{1}: (8, {}), {2}: (9, {})} | custom-call | flops 19327352832 | bytes 33554432 | tf_op jit(solution)/shard_map/rows_16/pallas_call | solution.py:128
  151.0 44.4 %rows_24.1 = (bf16[32,2,64,2048]{3,2,1,0:T(8,128)(2,1)}, f32[448,2048]{1,0:T(8,128)}, f32[320,2048]{1,0:T(8,128)}) custom-call(bf16[32,256,2048]{2,1,0:T(8,128)(2,1)} %x_ref.9, bf16[32,256,2048]{2,1,0:T(8,128)(2,1)} %dy_ref.9, s32[32,1,256]{2,1,0:T(1,128)} %reshape.180.seg_ref, ...), custom_call_target="tpu_custom_call", output_to_operand_aliasing={{1}: (8, {}), {2}: (9, {})} | custom-call | flops 19327352832 | bytes 33554432 | tf_op jit(solution)/shard_map/rows_24/pallas_call | solution.py:128
  195.4 0.1 reduce-scatter.14.cloned.1.call-update
  195.5 0.1 reduce-scatter.12.cloned.1.call-start
  195.5 0.7 reduce-scatter.12.cloned.1.call-update
  196.3 0.1 reduce-scatter.10.cloned.1.call-start
  196.4 0.7 reduce-scatter.10.cloned.1.call-update
  197.1 0.1 reduce-scatter.8.cloned.1.call-start
  197.2 0.6 reduce-scatter.8.cloned.1.call-update
  197.7 0.1 reduce-scatter.6.cloned.1.call-start
  197.8 0.6 reduce-scatter.6.cloned.1.call-update
  198.4 0.1 all-gather.19.cloned.1.call-start
  198.5 1.4 convert_reduce_fusion
  199.9 1.5 fusion.22
  201.4 104.0 %reduce-scatter.14.cloned.1.call-done = bf16[1,2,64,2048]{3,2,1,0:T(8,128)(2,1)} async-done(((bf16[32,2,64,2048]{3,2,1,0:T(8,128)(2,1)}), bf16[1,2,64,2048]{3,2,1,0:T(8,128)(2,1)}) %reduce-scatter.14.cloned.1.call-update) | async-done | bytes 524304 | tf_op jit(solution)/shard_map/reduce_scatter | solution.py:193
  305.4 111.2 %reduce-scatter.12.cloned.1.call-done = bf16[1,2,64,2048]{3,2,1,0:T(8,128)(2,1)} async-done(((bf16[32,2,64,2048]{3,2,1,0:T(8,128)(2,1)}), bf16[1,2,64,2048]{3,2,1,0:T(8,128)(2,1)}) %reduce-scatter.12.cloned.1.call-update) | async-done | bytes 524304 | tf_op jit(solution)/shard_map/reduce_scatter | solution.py:193
  416.6 111.2 %reduce-scatter.10.cloned.1.call-done = bf16[1,2,64,2048]{3,2,1,0:T(8,128)(2,1)} async-done(((bf16[32,2,64,2048]{3,2,1,0:T(8,128)(2,1)}), bf16[1,2,64,2048]{3,2,1,0:T(8,128)(2,1)}) %reduce-scatter.10.cloned.1.call-update) | async-done | bytes 524304 | tf_op jit(solution)/shard_map/reduce_scatter | solution.py:193
  527.8 2.6 fusion.38
  530.4 2.0 fusion.75
  532.4 0.8 pad_maximum_fusion.2
  533.3 0.1 all-gather.19.cloned.1.call-update
  533.3 0.1 all-gather.17.cloned.1.call-start
  533.4 0.8 pad_maximum_fusion.1
  534.2 0.1 all-gather.17.cloned.1.call-update
  534.3 0.1 all-gather.15.cloned.1.call-start
  534.4 1.5 fusion.73
  535.9 0.9 pad_maximum_fusion
  536.7 0.1 all-gather.15.cloned.1.call-update
  536.8 0.1 all-gather.13.cloned.1.call-start
  536.9 1.1 convert_reduce_fusion.3
  538.0 1.2 fusion.58
  539.2 76.3 %reduce-scatter.8.cloned.1.call-done = bf16[1,2,32,2048]{3,2,1,0:T(8,128)(2,1)} async-done(((bf16[32,2,32,2048]{3,2,1,0:T(8,128)(2,1)}), bf16[1,2,32,2048]{3,2,1,0:T(8,128)(2,1)}) %reduce-scatter.8.cloned.1.call-update) | async-done | bytes 262160 | tf_op jit(solution)/shard_map/reduce_scatter | solution.py:193
  615.5 87.7 %reduce-scatter.6.cloned.1.call-done = bf16[1,2,32,2048]{3,2,1,0:T(8,128)(2,1)} async-done(((bf16[32,2,32,2048]{3,2,1,0:T(8,128)(2,1)}), bf16[1,2,32,2048]{3,2,1,0:T(8,128)(2,1)}) %reduce-scatter.6.cloned.1.call-update) | async-done | bytes 262160 | tf_op jit(solution)/shard_map/reduce_scatter | solution.py:193
  703.2 1.5 fusion.65
  704.8 1.6 fusion.79
  706.5 0.7 pad_maximum_fusion.4
  707.2 0.1 all-gather.13.cloned.1.call-update
  707.3 0.4 all-gather.11.cloned.1.call-start
  707.6 0.7 pad_maximum_fusion.3
  708.4 0.1 all-gather.11.cloned.1.call-update
  708.4 2.3 convert.18
  710.7 1.0 slice.80
  711.7 1.1 slice_bitcast_fusion
  712.8 2.3 copy.32
  715.0 0.2 convert.19
  715.2 1.0 slice.83
  716.3 0.7 slice_bitcast_fusion.1
  717.0 47.8 %psum.7 = bf16[2048]{0:T(1024)(128)(2,1)} all-reduce(f32[2048]{0:T(1024)S(1)} %add_add_fusion), channel_id=1, replica_groups=mesh['data'=1,'model'=32] {'model'}, use_global_device_ids=true, to_apply=%region_30.0 | all-reduce | flops 2048 | bytes 12288 | tf_op jit(solution)/shard_map/psum | solution.py:215
  764.7 11.1 %all-gather.19.cloned.1.call-done = bf16[64,64,2048]{2,1,0:T(8,128)(2,1)} async-done(((bf16[2,64,2048]{2,1,0:T(8,128)(2,1)}), bf16[64,64,2048]{2,1,0:T(8,128)(2,1)}) %all-gather.19.cloned.1.call-update) | async-done | bytes 16777232 | tf_op jit(solution)/shard_map/all_gather | solution.py:213
  775.9 13.6 %place_24.1 = (bf16[32,256,2048]{2,1,0:T(8,128)(2,1)}, bf16[32,256,2048]{2,1,0:T(8,128)(2,1)}) custom-call(bf16[32,2,64,2048]{3,2,1,0:T(8,128)(2,1)} %bitcast.130, bf16[32,2,64,2048]{3,2,1,0:T(8,128)(2,1)} %bitcast.131), custom_call_target="tpu_custom_call" | custom-call | flops 268435456 | bytes 33554432 | tf_op jit(solution)/shard_map/place_24/pallas_call | solution.py:160
  789.5 54.8 %all-gather.17.cloned.1.call-done = bf16[64,64,2048]{2,1,0:T(8,128)(2,1)} async-done(((bf16[2,64,2048]{2,1,0:T(8,128)(2,1)}), bf16[64,64,2048]{2,1,0:T(8,128)(2,1)}) %all-gather.17.cloned.1.call-update) | async-done | bytes 16777232 | tf_op jit(solution)/shard_map/all_gather | solution.py:213
  844.3 13.6 %place_16.1 = (bf16[32,256,2048]{2,1,0:T(8,128)(2,1)}, bf16[32,256,2048]{2,1,0:T(8,128)(2,1)}) custom-call(bf16[32,2,64,2048]{3,2,1,0:T(8,128)(2,1)} %bitcast.132, bf16[32,2,64,2048]{3,2,1,0:T(8,128)(2,1)} %bitcast.133, bf16[32,256,2048]{2,1,0:T(8,128)(2,1)} %get-tuple-element.45.refs_0_, ...), custom_call_target="tpu_custom_call", output_to_operand_aliasing={{0}: (2, {}), {1}: (3, {})} | custom-call | flops 268435456 | bytes 33554432 | tf_op jit(solution)/shard_map/place_16/pallas_call | solution.py:160
  857.9 55.1 %all-gather.15.cloned.1.call-done = bf16[64,64,2048]{2,1,0:T(8,128)(2,1)} async-done(((bf16[2,64,2048]{2,1,0:T(8,128)(2,1)}), bf16[64,64,2048]{2,1,0:T(8,128)(2,1)}) %all-gather.15.cloned.1.call-update) | async-done | bytes 16777232 | tf_op jit(solution)/shard_map/all_gather | solution.py:213
  913.1 13.6 %place_8.1 = (bf16[32,256,2048]{2,1,0:T(8,128)(2,1)}, bf16[32,256,2048]{2,1,0:T(8,128)(2,1)}) custom-call(bf16[32,2,64,2048]{3,2,1,0:T(8,128)(2,1)} %bitcast.134, bf16[32,2,64,2048]{3,2,1,0:T(8,128)(2,1)} %bitcast.135, bf16[32,256,2048]{2,1,0:T(8,128)(2,1)} %get-tuple-element.47.refs_0_, ...), custom_call_target="tpu_custom_call", output_to_operand_aliasing={{0}: (2, {}), {1}: (3, {})} | custom-call | flops 268435456 | bytes 33554432 | tf_op jit(solution)/shard_map/place_8/pallas_call | solution.py:160
  926.7 35.2 %all-gather.13.cloned.1.call-done = bf16[64,32,2048]{2,1,0:T(8,128)(2,1)} async-done(((bf16[2,32,2048]{2,1,0:T(8,128)(2,1)}), bf16[64,32,2048]{2,1,0:T(8,128)(2,1)}) %all-gather.13.cloned.1.call-update) | async-done | bytes 8388624 | tf_op jit(solution)/shard_map/all_gather | solution.py:213
  962.0 7.0 place_4.1
  969.0 41.8 %all-gather.11.cloned.1.call-done = bf16[64,32,2048]{2,1,0:T(8,128)(2,1)} async-done(((bf16[2,32,2048]{2,1,0:T(8,128)(2,1)}), bf16[64,32,2048]{2,1,0:T(8,128)(2,1)}) %all-gather.11.cloned.1.call-update) | async-done | bytes 8388624 | tf_op jit(solution)/shard_map/all_gather | solution.py:213
  1010.8 7.0 place_0.1
  (24 shorter events, 0.1 us)
Async XLA Ops:
  7.2 298.2 %reduce-scatter.14.cloned.1.call-start = ((), (), s32[]{:S(2)}) async-start(), calls=%async_computation.9 | async-start | bytes 17301504 | tf_op jit(solution)/shard_map/reduce_scatter | solution.py:193
  195.4 3.0 copy-start.1
  195.5 221.1 %reduce-scatter.12.cloned.1.call-start = ((), (), s32[]{:S(2)}) async-start(), calls=%async_computation.8 | async-start | bytes 17301504 | tf_op jit(solution)/shard_map/reduce_scatter | solution.py:193
  196.3 518.7 %copy-start = (f32[320,2048]{1,0:T(8,128)S(1)}, f32[320,2048]{1,0:T(8,128)}, u32[]{:S(2)}) copy-start(f32[320,2048]{1,0:T(8,128)} %get-tuple-element.56) | copy-start | bytes 7864324
  196.3 331.5 %reduce-scatter.10.cloned.1.call-start = ((), (), s32[]{:S(2)}) async-start(), calls=%async_computation.7 | async-start | bytes 17301504 | tf_op jit(solution)/shard_map/reduce_scatter | solution.py:193
  197.1 418.4 %reduce-scatter.8.cloned.1.call-start = ((), (), s32[]{:S(2)}) async-start(), calls=%async_computation.6 | async-start | bytes 8650752 | tf_op jit(solution)/shard_map/reduce_scatter | solution.py:193
  197.7 505.5 %reduce-scatter.6.cloned.1.call-start = ((), (), s32[]{:S(2)}) async-start(), calls=%async_computation.5 | async-start | bytes 8650752 | tf_op jit(solution)/shard_map/reduce_scatter | solution.py:193
  198.4 577.5 %all-gather.19.cloned.1.call-start = ((), (), s32[]{:S(2)}) async-start(), calls=%async_computation.14 | async-start | bytes 17301504 | tf_op jit(solution)/shard_map/all_gather | solution.py:213
  533.3 310.9 %all-gather.17.cloned.1.call-start = ((), (), s32[]{:S(2)}) async-start(), calls=%async_computation.13 | async-start | bytes 17301504 | tf_op jit(solution)/shard_map/all_gather | solution.py:213
  534.3 378.8 %all-gather.15.cloned.1.call-start = ((), (), s32[]{:S(2)}) async-start(), calls=%async_computation.12 | async-start | bytes 17301504 | tf_op jit(solution)/shard_map/all_gather | solution.py:213
  536.8 425.2 %all-gather.13.cloned.1.call-start = ((), (), s32[]{:S(2)}) async-start(), calls=%async_computation.11 | async-start | bytes 8650752 | tf_op jit(solution)/shard_map/all_gather | solution.py:213
  707.3 303.5 %all-gather.11.cloned.1.call-start = ((), (), s32[]{:S(2)}) async-start(), calls=%async_computation.10 | async-start | bytes 8650752 | tf_op jit(solution)/shard_map/all_gather | solution.py:213
Sparse Core Ops, SparseCore 0:
  195.6 109.7 reduce-scatter.13
  309.7 106.8 reduce-scatter.11
  420.9 106.8 reduce-scatter.9
  531.2 84.2 reduce-scatter.7
  618.9 84.2 reduce-scatter.5
  705.8 70.0 all-gather.18
  778.0 66.2 all-gather.16
  846.4 66.6 all-gather.14
  915.2 46.7 all-gather.12
  963.9 46.8 all-gather.10

commit v2 on v0

v2 whole, which is shorter than its diff:
```python
import functools
import math

import jax
import jax.numpy as jnp
from jax import lax
from jax.experimental import pallas as pl
from jax.experimental.pallas import tpu as pltpu
from jax.sharding import PartitionSpec as P

LN_EPS = 1e-5
RING = 4
STAGES = 3
MESH = pl.DeviceIdType.MESH
NT = (((1,), (1,)), ((), ()))
NN = (((1,), (0,)), ((), ()))
TN = (((0,), (0,)), ((), ()))
ORDER = ((2, 2), (2, 1), (1, 2), (2, 3), (3, 2), (1, 1), (3, 3), (1, 3), (3, 1),
         (2, 0), (0, 2), (1, 0), (0, 1), (3, 0), (0, 3), (0, 0))
VMEM_LIMIT = 62 * 2 ** 20


def dot(lhs, rhs, dims):
    return lax.dot_general(lhs, rhs, dims, preferred_element_type=jnp.float32)


def norm_rows(x_f32):
    mean_val = jnp.mean(x_f32, axis=-1, keepdims=True)
    centered = x_f32 - mean_val
    inv_std = lax.rsqrt(jnp.mean(centered * centered, axis=-1, keepdims=True) + LN_EPS)
    return centered * inv_std, inv_std


class Place:
    def __init__(self):
        me = lax.axis_index('model')
        self.core = me % 2
        self.x = (me // 2) % RING
        self.y = me // (2 * RING)
        self.me = me

    def index(self, d_y, d_x, core=None):
        core = self.core if core is None else core
        return (((self.y + d_y) % RING) * RING + (self.x + d_x) % RING) * 2 + core

    def peer(self, axis, offset):
        return self.index(offset % RING, 0) if axis == 'y' else self.index(0, offset % RING)

    def sibling(self):
        return self.index(0, 0, 1 - self.core)


def remote(src, dst, send_sem, recv_sem, device):
    return pltpu.make_async_remote_copy(src_ref=src, dst_ref=dst, send_sem=send_sem, recv_sem=recv_sem,
                                        device_id={'model': device}, device_id_type=MESH)


def enter(peers):
    barrier = pltpu.get_barrier_semaphore()
    for peer in peers:
        pl.semaphore_signal(barrier, inc=1, device_id={'model': peer}, device_id_type=MESH)
    pl.semaphore_wait(barrier, len(peers))


def pick(step, values):
    out = jnp.int32(0)
    for n, value in enumerate(values):
        out = jnp.where(step == n, value, out)
    return out


def add_into(dst, *sources):
    rows = dst.shape[0]
    tile = min(rows, 32)

    def tile_add(n, carry):
        at = pl.ds(pl.multiple_of(n * tile, tile), tile)
        total = dst[at, :].astype(jnp.float32)
        for source in sources:
            total += source[at, :].astype(jnp.float32)
        dst[at, :] = total.astype(dst.dtype)
        return carry

    lax.fori_loop(0, rows // tile, tile_add, 0)


def reduce_kernel(x_hbm, dy_hbm, seg_ref, gain_ref, wqkv_hbm, w1t_hbm, wo_hbm, w2_hbm,
                  y_own, dx_own, dgain_ref, g_own, g_sib, full,
                  w_in, w_out, acc_in, acc_out, x_buf, dy_buf, a_scr, h_scr, d_scr, stage, half, tmp,
                  row_sem, w_sem, ws_sem, wr_sem, send_sem, half_sem, full_sem, tmp_sem, out_sem):
    place = Place()
    core = place.core
    _, seq_len, hidden = x_buf.shape
    mid = seq_len // 2
    n_qkv, n_up, n_o, n_dn = wqkv_hbm.shape[0], w1t_hbm.shape[0], wo_hbm.shape[0], w2_hbm.shape[0]
    head_dim = n_o
    steps = len(ORDER)

    def row_of(step):
        d_y = pick(step, [o[0] for o in ORDER])
        d_x = pick(step, [o[1] for o in ORDER])
        return place.index(d_y, d_x)

    def row_copies(step):
        row, buf = row_of(step), step % 2
        return (pltpu.make_async_copy(x_hbm.at[row], x_buf.at[buf], row_sem.at[buf, 0]),
                pltpu.make_async_copy(dy_hbm.at[row], dy_buf.at[buf], row_sem.at[buf, 1]))

    def weight_spots(side):
        return ((wqkv_hbm, w_in.at[pl.ds(pl.multiple_of(side * n_qkv, 16), n_qkv)]),
                (w1t_hbm, w_in.at[pl.ds(pl.multiple_of(2 * n_qkv + side * n_up, 16), n_up)]),
                (wo_hbm, w_out.at[pl.ds(pl.multiple_of(side * n_o, 16), n_o)]),
                (w2_hbm, w_out.at[pl.ds(pl.multiple_of(2 * n_o + side * n_dn, 16), n_dn)]))

    for copy in row_copies(0):
        copy.start()
    mine = [pltpu.make_async_copy(src, dst, w_sem.at[n]) for n, (src, dst) in enumerate(weight_spots(core))]
    for copy in mine:
        copy.start()
    enter([place.peer('x', 1), place.peer('x', -1), place.peer('y', 1), place.peer('y', -1), place.sibling()])
    swaps = [remote(src, dst, ws_sem.at[n], wr_sem.at[n], place.sibling()) for n, (src, dst) in enumerate(weight_spots(core))]
    for copy in swaps:
        copy.start()
    acc_in[...] = jnp.zeros_like(acc_in)
    acc_out[...] = jnp.zeros_like(acc_out)
    for copy in mine:
        copy.wait()
    for copy in swaps:
        copy.wait()

    gain = gain_ref[...].astype(jnp.float32)
    scale = head_dim ** -0.5
    sub = min(seq_len, 64)
    cols_step = min(hidden, 512)

    def slot_sends(slot):
        return [pltpu.make_async_copy(stage.at[slot, t, pl.ds(piece * mid, mid)], stage.at[slot, t, pl.ds(piece * mid, mid)],
                                      send_sem.at[slot, t, piece]) for t in range(2) for piece in range(2)]

    def send(slot, t, piece, dst, recv_sem, device):
        remote(stage.at[slot, t, pl.ds(piece * mid, mid)], dst, send_sem.at[slot, t, piece], recv_sem, device).start()

    def hop(slot, t, axis, offset, line):
        ahead, behind = place.peer(axis, 1), place.peer(axis, -1)
        spot = stage.at[slot, t]
        if offset == 2:
            send(slot, t, 0, half.at[t, line, 0], half_sem.at[t, line, 0], ahead)
            send(slot, t, 1, half.at[t, line, 1], half_sem.at[t, line, 1], behind)
            return
        if offset in (1, 3):
            piece = 0 if offset == 1 else 1
            came = half.at[t, line, piece]
            pltpu.make_async_copy(came, came, half_sem.at[t, line, piece]).wait()
            add_into(spot.at[pl.ds(piece * mid, mid)], came)
            for n in range(2):
                send(slot, t, n, full.at[t, line, piece, pl.ds(n * mid, mid)], full_sem.at[t, line, piece, n],
                     ahead if offset == 1 else behind)
            return
        loads = []
        for side in range(2):
            for n in range(2):
                came = full.at[t, line, side, pl.ds(n * mid, mid)]
                pltpu.make_async_copy(came, came, full_sem.at[t, line, side, n]).wait()
            load = pltpu.make_async_copy(full.at[t, line, side], tmp.at[side], tmp_sem.at[side])
            load.start()
            loads.append(load)
        for load in loads:
            load.wait()
        add_into(spot, tmp.at[0], tmp.at[1])

    def row_step(step, carry):
        buf = step % 2
        slot = step % STAGES
        for copy in row_copies(step):
            copy.wait()

        @pl.when(step + 1 < steps)
        def _():
            for copy in row_copies(step + 1):
                copy.start()

        for t in range(0, seq_len, sub):
            normed, _ = norm_rows(x_buf[buf, t:t + sub, :].astype(jnp.float32))
            a_scr[t:t + sub, :] = (normed * gain).astype(jnp.bfloat16)

        proj = dot(w_in[...], a_scr[...], NT)
        qkv = proj[:2 * n_qkv].astype(jnp.bfloat16)
        up = proj[2 * n_qkv:].astype(jnp.bfloat16).astype(jnp.float32)
        d_proj = dot(w_out[...], dy_buf[buf], NT).astype(jnp.bfloat16)
        d_attn = d_proj[:2 * n_o]
        d_hid = d_proj[2 * n_o:].astype(jnp.float32)
        cdf = 0.5 * (1.0 + lax.erf(up * (0.5 ** 0.5)))
        h_scr[2 * n_o:, :] = (up * cdf).astype(jnp.bfloat16)
        slope = cdf + up * (jnp.exp(-0.5 * up * up) * 0.3989422804014327)
        d_scr[2 * n_qkv:, :] = (d_hid * slope).astype(jnp.bfloat16)

        seg_row = seg_ref[row_of(step)]
        classes = lax.broadcasted_iota(jnp.int32, (16, seq_len), 0)
        one_hot = (classes == jnp.broadcast_to(seg_row, (16, seq_len))).astype(jnp.bfloat16)
        same = dot(one_hot, one_hot, TN) > 0.5
        key_id = lax.broadcasted_iota(jnp.int32, (seq_len, seq_len), 0)
        query_id = lax.broadcasted_iota(jnp.int32, (seq_len, seq_len), 1)
        allowed = (key_id <= query_id) & same
        for head in range(2):
            at = head * n_qkv
            query = qkv[at:at + head_dim]
            keys = qkv[at + head_dim:at + 2 * head_dim]
            values = qkv[at + 2 * head_dim:at + 3 * head_dim]
            d_o = d_attn[head * head_dim:(head + 1) * head_dim]
            scores = jnp.where(allowed, dot(keys, query, TN) * scale, -1e30)
            expd = jnp.exp(scores - jnp.max(scores, axis=0, keepdims=True))
            probs = expd / jnp.sum(expd, axis=0, keepdims=True)
            probs_b = probs.astype(jnp.bfloat16)
            h_scr[head * head_dim:(head + 1) * head_dim, :] = dot(values, probs_b, NN).astype(jnp.bfloat16)
            d_p = dot(values, d_o, TN)
            d_s = (probs * (d_p - jnp.sum(d_p * probs, axis=0, keepdims=True)) * scale).astype(jnp.bfloat16)
            d_scr[at:at + head_dim, :] = dot(keys, d_s, NN).astype(jnp.bfloat16)
            d_scr[at + head_dim:at + 2 * head_dim, :] = dot(query, d_s, NT).astype(jnp.bfloat16)
            d_scr[at + 2 * head_dim:at + 3 * head_dim, :] = dot(d_o, probs_b, NT).astype(jnp.bfloat16)

        @pl.when(step >= STAGES)
        def _():
            for copy in slot_sends(slot):
                copy.wait()

        for h in range(0, hidden, cols_step):
            cols = slice(h, h + cols_step)
            stage[slot, 0, :, cols] = dot(h_scr[...], w_out[:, cols], TN).astype(jnp.bfloat16)
            stage[slot, 1, :, cols] = dot(d_scr[...], w_in[:, cols], TN).astype(jnp.bfloat16)
            acc_in[:, cols] += dot(d_scr[...], a_scr[:, cols], NN)
            acc_out[:, cols] += dot(h_scr[...], dy_buf[buf, :, cols], NN)

        for n, (d_y, d_x) in enumerate(ORDER):
            @pl.when(step == n)
            def _():
                at = n % STAGES
                for t, first, second in ((0, ('x', d_x), ('y', d_y)), (1, ('y', d_y), ('x', d_x))):
                    hop(at, t, *first, second[1])
                    if first[1] == 0:
                        hop(at, t, *second, RING)
        return carry

    lax.fori_loop(0, steps, row_step, 0)

    outs = []
    for n, (side, dst) in enumerate(((core, g_own), (1 - core, g_sib))):
        to = 0
        for m, (acc, at, count) in enumerate(((acc_in, side * n_qkv, n_qkv), (acc_in, 2 * n_qkv + side * n_up, n_up),
                                              (acc_out, side * n_o, n_o), (acc_out, 2 * n_o + side * n_dn, n_dn))):
            outs.append(pltpu.make_async_copy(acc.at[pl.ds(pl.multiple_of(at, 16), count)], dst.at[pl.ds(to, count)], out_sem.at[4 * n + m]))
            to += count
    for copy in outs:
        copy.start()
    for n in range(max(0, steps - STAGES), steps - 1):
        for copy in slot_sends(n % STAGES):
            copy.wait()

    last, buf = (steps - 1) % STAGES, (steps - 1) % 2
    d_gain = jnp.zeros((1, hidden), jnp.float32)
    fine = min(seq_len, 32)

    def finish(n, d_gain):
        at = pl.ds(pl.multiple_of(n * fine, fine), fine)
        x_f32 = x_buf[buf, at, :].astype(jnp.float32)
        normed, inv_std = norm_rows(x_f32)
        grad = stage[last, 1, at, :].astype(jnp.float32)
        stage[last, 0, at, :] = (x_f32 + stage[last, 0, at, :].astype(jnp.float32)).astype(jnp.bfloat16)
        d_hat = grad * gain
        d_x = inv_std * (d_hat - jnp.mean(d_hat, axis=-1, keepdims=True) - normed * jnp.mean(d_hat * normed, axis=-1, keepdims=True))
        stage[last, 1, at, :] = (dy_buf[buf, at, :].astype(jnp.float32) + d_x).astype(jnp.bfloat16)
        return d_gain + jnp.sum(grad * normed, axis=0, keepdims=True)

    dgain_ref[...] = lax.fori_loop(0, seq_len // fine, finish, d_gain)
    ends = [pltpu.make_async_copy(stage.at[last, t], dst, tmp_sem.at[t]) for t, dst in ((0, y_own), (1, dx_own))]
    for copy in ends:
        copy.start()
    for copy in ends + outs:
        copy.wait()


def gather_kernel(y_own, dx_own, dgain_ref, g_sib, y_all, dx_all, g_recv, dgain_out, gain_scr,
                  send_sem, link_sem, pair_sem, pair_recv, own_sem, g_sem, dg_send, dg_recv):
    place = Place()
    seq_len = y_all.shape[1]
    mid = seq_len // 2
    outs = (y_all, dx_all)
    owns = (y_own, dx_own)
    links = (('x', 1), ('x', -1), ('y', 1), ('y', -1))
    enter([place.peer(a, o) for a in ('x', 'y') for o in (1, 2, 3)] + [place.sibling()])

    issued = {link: [] for link in links}
    sends = []

    def row_index(t, d_1, d_2):
        return place.index(d_1, d_2) if t == 0 else place.index(d_2, d_1)

    def issue(link, t, d_1, d_2, piece):
        n = len(issued[link])
        row = row_index(t, d_1 % RING, d_2 % RING)
        spot = outs[t].at[row, pl.ds(piece * mid, mid)]
        src = owns[t].at[pl.ds(piece * mid, mid)] if (d_1, d_2) == (0, 0) else spot
        which = links.index(link)
        copy = remote(src, spot, send_sem.at[which, n], link_sem.at[which, n], place.peer(*link))
        copy.start()
        sends.append(copy)
        issued[link].append((t, d_1, d_2, piece))

    def pair(t, d_1, d_2, piece):
        row = row_index(t, d_1 % RING, d_2 % RING)
        spot = outs[t].at[row, pl.ds(piece * mid, mid)]
        src = owns[t].at[pl.ds(piece * mid, mid)] if (d_1, d_2) == (0, 0) else spot
        slot = ((d_1 % RING) * RING + d_2 % RING) * 2 + piece
        copy = remote(src, spot, pair_sem.at[t, slot], pair_recv.at[t], place.sibling())
        copy.start()
        sends.append(copy)

    axes = (('y', 'x'), ('x', 'y'))
    for piece in range(2):
        for t in range(2):
            for way in (1, -1):
                issue((axes[t][0], way), t, 0, 0, piece)
    for piece in range(2):
        for t in range(2):
            for way in (1, -1):
                issue((axes[t][1], way), t, 0, 0, piece)
    locals_ = []
    for t in range(2):
        for piece in range(2):
            pair(t, 0, 0, piece)
        copy = pltpu.make_async_copy(owns[t], outs[t].at[place.me], own_sem.at[t])
        copy.start()
        locals_.append(copy)
    g_copy = remote(g_sib, g_recv, g_sem.at[0], g_sem.at[1], place.sibling())
    g_copy.start()

    total = dgain_ref[...]
    for n, (axis, offsets) in enumerate((('core', (1,)), ('x', (1, 2, 3)), ('y', (1, 2, 3)))):
        spot = {'core': place.core, 'x': place.x, 'y': place.y}[axis]
        gain_scr[n, spot] = total
        copies = []
        for m, offset in enumerate(offsets):
            device = place.sibling() if axis == 'core' else place.peer(axis, offset)
            copies.append(remote(gain_scr.at[n, spot], gain_scr.at[n, spot], dg_send.at[n, m], dg_recv.at[n, m], device))
        for copy in copies:
            copy.start()
        for copy in copies:
            copy.wait()
        total = gain_scr[n, 0]
        for m in range(1, len(offsets) + 1):
            total = total + gain_scr[n, m]
    dgain_out[...] = total.astype(dgain_out.dtype)

    rounds = 4 * (RING * RING - 1) // 4
    for n in range(rounds):
        for link in links:
            t, d_1, d_2, piece = issued[link][n]
            axis, way = link
            on_first = axis == axes[t][0]
            d_1, d_2 = (d_1 - way, d_2) if on_first else (d_1, d_2 - way)
            row = row_index(t, d_1 % RING, d_2 % RING)
            spot = outs[t].at[row, pl.ds(piece * mid, mid)]
            pltpu.make_async_copy(spot, spot, link_sem.at[links.index(link), n]).wait()
            along = d_1 if on_first else d_2
            if abs(along) == 1 and piece == (0 if way == 1 else 1):
                issue(link, t, d_1, d_2, piece)
            if on_first:
                for other in (1, -1):
                    issue((axes[t][1], other), t, d_1, d_2, piece)
            pair(t, d_1, d_2, piece)

    for t in range(2):
        theirs = outs[t].at[pl.ds(0, RING * RING)]
        pltpu.make_async_copy(theirs, theirs, pair_recv.at[t]).wait()
    for copy in sends:
        copy.wait_send()
    for copy in locals_:
        copy.wait()
    g_copy.wait()


def solution(mesh):
    devices = mesh.shape['model']
    assert devices == 2 * RING * RING and math.isqrt(devices // 2) == RING

    def body(x_in, seg_ids, ln_gain, w_qkv, w_out, w_up, w_down, dy_in):
        rows, seq_len, hidden = x_in.shape
        assert rows == devices
        wqkv = w_qkv.transpose(1, 2, 3, 0).reshape(-1, hidden)
        w1t = w_up.T
        wo = w_out.reshape(-1, hidden)
        n_qkv, n_up, n_o, n_dn = wqkv.shape[0], w1t.shape[0], wo.shape[0], w_down.shape[0]
        n_in, n_out = n_qkv + n_up, n_o + n_dn
        bf16, f32 = jnp.bfloat16, jnp.float32
        vmem, anywhere = pl.BlockSpec(memory_space=pltpu.VMEM), pl.BlockSpec(memory_space=pl.ANY)
        dma = pltpu.SemaphoreType.DMA
        shape = jax.ShapeDtypeStruct
        mid = seq_len // 2
        y_own, dx_own, d_gain, g_own, g_sib, _ = pl.pallas_call(
            reduce_kernel,
            in_specs=[anywhere, anywhere, vmem, vmem] + [anywhere] * 4,
            out_specs=[anywhere, anywhere, vmem, anywhere, anywhere, anywhere],
            out_shape=[shape((seq_len, hidden), bf16), shape((seq_len, hidden), bf16), shape((1, hidden), f32),
                       shape((n_in + n_out, hidden), f32), shape((n_in + n_out, hidden), f32),
                       shape((2, RING + 1, 2, seq_len, hidden), bf16)],
            scratch_shapes=[
                pltpu.VMEM((2 * n_in, hidden), bf16), pltpu.VMEM((2 * n_out, hidden), bf16),
                pltpu.VMEM((2 * n_in, hidden), f32), pltpu.VMEM((2 * n_out, hidden), f32),
                pltpu.VMEM((2, seq_len, hidden), bf16), pltpu.VMEM((2, seq_len, hidden), bf16),
                pltpu.VMEM((seq_len, hidden), bf16),
                pltpu.VMEM((2 * n_out, seq_len), bf16), pltpu.VMEM((2 * n_in, seq_len), bf16),
                pltpu.VMEM((STAGES, 2, seq_len, hidden), bf16),
                pltpu.VMEM((2, RING + 1, 2, mid, hidden), bf16),
                pltpu.VMEM((2, seq_len, hidden), bf16),
                dma((2, 2)), dma((4,)), dma((4,)), dma((4,)), dma((STAGES, 2, 2)),
                dma((2, RING + 1, 2)), dma((2, RING + 1, 2, 2)), dma((2,)), dma((8,)),
            ],
            compiler_params=pltpu.CompilerParams(collective_id=0, has_side_effects=True, vmem_limit_bytes=VMEM_LIMIT),
            name="rows_reduce",
        )(x_in, dy_in, seg_ids.reshape(rows, 1, seq_len), ln_gain.reshape(1, hidden), wqkv, w1t, wo, w_down)

        per_link = RING * RING - 1
        y_out, dx_out, g_recv, d_gain = pl.pallas_call(
            gather_kernel,
            in_specs=[anywhere, anywhere, vmem, anywhere],
            out_specs=[anywhere, anywhere, anywhere, vmem],
            out_shape=[shape(x_in.shape, bf16), shape(x_in.shape, bf16), shape(g_sib.shape, f32), shape((1, hidden), bf16)],
            scratch_shapes=[
                pltpu.VMEM((3, RING, 1, hidden), f32),
                dma((4, per_link)), dma((4, per_link)), dma((2, 2 * RING * RING)), dma((2,)), dma((2,)), dma((2,)),
                dma((3, 3)), dma((3, 3)),
            ],
            compiler_params=pltpu.CompilerParams(collective_id=1, has_side_effects=True, vmem_limit_bytes=VMEM_LIMIT),
            name="rows_gather",
        )(y_own, dx_own, d_gain, g_sib)

        grads = (g_own + g_recv).astype(bf16)
        d_wqkv = grads[:n_qkv].reshape(w_qkv.shape[1:] + (hidden,)).transpose(3, 0, 1, 2)
        d_wup = grads[n_qkv:n_in].T
        d_wout = grads[n_in:n_in + n_o].reshape(w_out.shape)
        d_wdown = grads[n_in + n_o:]
        return y_out, dx_out, d_gain.reshape(hidden), d_wqkv, d_wout, d_wup, d_wdown

    in_specs = (P('data'), P('data'), P(), P(None, 'model'), P('model'), P(None, 'model'), P('model'), P('data'))
    out_specs = (P('data'), P('data'), P('data'), P('data', 'model'), P(('data', 'model')), P('data', 'model'), P(('data', 'model')))
    return jax.shard_map(body, mesh=mesh, in_specs=in_specs, out_specs=out_specs, check_vma=False)
```

time: 856 us -> 499 us (0.58)
  Pallas kernels: 0 us -> 435 us
  waiting for transfers between devices: 355 us -> 0 us
  matrix products: 335 us -> 0 us
  other arithmetic: 137 us -> 6.26 us
  local copies, waits for them, and re-layouts: 7.07 us -> 56.1 us
  between operations: 14.5 us -> 0.68 us
    pallas_call x0 -> x2, Pallas kernels: none -> 435 us  [the longest x1 248 us: body(): pl.pallas_call(reduce_kernel, in_specs=[anywhere, anywhere, vmem, vmem] +...]
    psum x1 -> x0, waiting for transfers between devices: 355 us -> none  [body(): mixed = lax.psum(share.astype(jnp.bfloat16), 'model')]
    dot_general x18 -> x0, matrix products: 335 us -> none  [the longest x1 42.5 us: body(): jnp.einsum('bsf,fh->bsh', hidden_act, w_down, preferred_element_type=jnp....]
    convert_element_type x2 -> x1, other arithmetic: 71.6 us -> 5.64 us  [body(): grads = (g_own + g_recv).astype(bf16)]
    reduce_sum x3 -> x0, other arithmetic: 59.9 us -> none  [the longest x1 35.7 us: layer_norm_bwd(): d_gain = jnp.sum(grad_f32 * normed_f32, axis=(0, 1))]
    unnamed x48 -> x6, local copies, waits for them, and re-layouts: 7.07 us -> 50.3 us
  transfers between devices with their start and end apart: 1 -> 0, of which waited for: 1 -> 0; matrix products, arithmetic and copies ran while one was open for 10% -> 0% of each run, Pallas kernels for 0% -> 0%
where the time goes in v2:
time: 499 us; the launch traced here: 498 us
  Pallas kernels  435 us (87%)
  local copies, waits for them, and re-layouts  56.1 us (11%)
  other arithmetic  6.26 us (1%)
    pallas_call x1, Pallas kernels, body(): pl.pallas_call(reduce_kernel, in_specs=[anywhere, anywhere, vmem, vmem] +...  248 us
    pallas_call x1, Pallas kernels, body(): pl.pallas_call(gather_kernel, in_specs=[anywhere, anywhere, vmem, anywher...  187 us
    unnamed x6, local copies, waits for them, and re-layouts  50.3 us

profile of v2, /device:TPU:97, one launch (start us, length us, event | category | flops | bytes accessed | tf_op | source)
XLA Modules:
  0.0 497.9 jit_solution(9344410855228263070)
XLA Ops:
  0.6 1.3 reshape.36.gain_ref
  1.9 1.4 reshape.35.seg_ref
  3.3 2.3 copy.15
  5.6 248.1 %rows_reduce.1 = (bf16[256,2048]{1,0:T(8,128)(2,1)}, bf16[256,2048]{1,0:T(8,128)(2,1)}, f32[1,2048]{1,0:T(1,128)}, f32[768,2048]{1,0:T(8,128)}, f32[768,2048]{1,...) custom-call(bf16[32,256,2048]{2,1,0:T(8,128)(2,1)} %x_hbm.1, bf16[32,256,2048]{2,1,0:T(8,128)(2,1)} %dy_hbm.1, ...), custom_call_target="tpu_custom_call" | custom-call | tf_op jit(solution)/shard_map/rows_reduce/pallas_call | solution.py:398
  253.7 186.7 %rows_gather.1 = (bf16[32,256,2048]{2,1,0:T(8,128)(2,1)}, bf16[32,256,2048]{2,1,0:T(8,128)(2,1)}, f32[768,2048]{1,0:T(8,128)}, bf16[1,2048]{1,0:T(2,128)(2,1)}) custom-call(bf16[256,2048]{1,0:T(8,128)(2,1)} %get-tuple-element.16.y_own, bf16[256,2048]{1,0:T(8,128)(2,1)} %get-tuple-element.17.dx_own, f32[1,2048]{1,0:T(1,128)} %get-tuple-element.18.dgain_ref, ...), custom_call_target="tpu_custom_call" | custom-call | tf_op jit(solution)/shard_map/rows_gather/pallas_call | solution.py:422
  440.4 0.0 copy-start
  440.4 5.6 %add_convert_fusion = bf16[768,2048]{1,0:T(8,128)(2,1)S(1)} fusion(f32[768,2048]{1,0:T(8,128)} %get-tuple-element.23, f32[768,2048]{1,0:T(8,128)} %get-tuple-element.24), kind=kLoop, calls=%fused_computation | loop fusion | flops 3145728 | bytes 15728640 | tf_op jit(solution)/shard_map/convert_element_type | solution.py:436
  446.1 0.0 copy-done
  446.1 0.6 reduce
  446.7 0.7 slice_bitcast_fusion.1
  447.4 0.9 slice.16
  448.4 1.5 fusion
  449.8 2.3 copy.16
  452.1 22.9 %copy.19 = bf16[32,256,2048]{2,1,0:T(8,128)(2,1)} copy(bf16[32,256,2048]{2,1,0:T(8,128)(2,1)} %get-tuple-element.41) | data formatting | bytes 67108864
  475.0 22.9 %copy.20 = bf16[32,256,2048]{2,1,0:T(8,128)(2,1)} copy(bf16[32,256,2048]{2,1,0:T(8,128)(2,1)} %get-tuple-element.42) | data formatting | bytes 67108864
Async XLA Ops:
  440.4 5.7 %copy-start = (bf16[1,2048]{1,0:T(2,128)(2,1)S(1)}, bf16[1,2048]{1,0:T(2,128)(2,1)}, u32[]{:S(2)}) copy-start(bf16[1,2048]{1,0:T(2,128)(2,1)} %get-tuple-element.22) | copy-start | bytes 12292

commit v3 on v2

v3 whole, which is shorter than its diff:
```python
import functools
import math

import jax
import jax.numpy as jnp
from jax import lax
from jax.experimental import pallas as pl
from jax.experimental.pallas import tpu as pltpu
from jax.sharding import PartitionSpec as P

LN_EPS = 1e-5
RING = 4
MESH = pl.DeviceIdType.MESH
NT = (((1,), (1,)), ((), ()))
NN = (((1,), (0,)), ((), ()))
TN = (((0,), (0,)), ((), ()))
ORDER = ((2, 2), (1, 2), (2, 3), (3, 2), (2, 1), (0, 1), (1, 1), (3, 3),
         (2, 0), (0, 2), (3, 0), (1, 3), (3, 1), (0, 3), (1, 0), (0, 0))
SLOT = (0, 1, 2, 3, 4, 0, 1, 2, 3, 4, 2, 1, 3, 4, 1, 3)
SLOTS = max(SLOT) + 1
EVENTS = (
    ((0, 0, 0, 1), (0, 0, 1, 1), (0, 1, 0, 1), (0, 1, 1, 1)),
    ((1, 0, 0, 1), (1, 0, 1, 1), (1, 1, 1, 1)),
    ((2, 0, 0, 1), (2, 1, 0, 1), (2, 1, 1, 1), (1, 1, 0, 1), (2, 0, 1, 1)),
    ((3, 0, 0, 1), (3, 0, 1, 1), (3, 1, 0, 1), (3, 1, 1, 1)),
    ((4, 0, 1, 1), (4, 1, 0, 1), (4, 1, 1, 1), (4, 0, 0, 1)),
    ((5, 0, 1, 1),),
    ((6, 0, 1, 1), (6, 1, 1, 1), (6, 0, 0, 1)),
    ((7, 0, 0, 1), (7, 1, 0, 1), (7, 1, 1, 1)),
    ((8, 1, 0, 1), (8, 1, 1, 1), (8, 0, 1, 1), (8, 0, 1, 2), (6, 1, 0, 1), (7, 0, 1, 1), (8, 0, 0, 1), (8, 0, 0, 2)),
    ((9, 0, 0, 1), (9, 0, 1, 1), (9, 1, 0, 1), (9, 1, 0, 2), (9, 1, 1, 1), (9, 1, 1, 2)),
    ((10, 1, 0, 1),),
    ((11, 0, 0, 1), (11, 1, 1, 1), (11, 0, 1, 1), (11, 1, 0, 1), (10, 1, 1, 1)),
    ((12, 0, 1, 1), (12, 1, 0, 1), (12, 0, 0, 1), (12, 1, 1, 1), (5, 0, 0, 1)),
    ((13, 0, 0, 1), (13, 0, 1, 1), (13, 1, 1, 1), (13, 1, 1, 2)),
    ((14, 1, 1, 1), (14, 1, 0, 1), (14, 0, 0, 1), (14, 0, 0, 2), (10, 0, 1, 1), (10, 0, 1, 2), (13, 1, 0, 1), (13, 1, 0, 2), (14, 0, 1, 1), (14, 0, 1, 2), (10, 0, 0, 1), (10, 0, 0, 2), (5, 1, 0, 1), (5, 1, 0, 2)),
    ((15, 1, 1, 1), (15, 0, 0, 1), (15, 0, 1, 1), (5, 1, 1, 1), (5, 1, 1, 2), (15, 1, 0, 1), (15, 1, 0, 2), (15, 1, 1, 2), (15, 0, 0, 2), (15, 0, 1, 2)),
)
VMEM_LIMIT = 62 * 2 ** 20


def dot(lhs, rhs, dims):
    return lax.dot_general(lhs, rhs, dims, preferred_element_type=jnp.float32)


def norm_rows(x_f32):
    mean_val = jnp.mean(x_f32, axis=-1, keepdims=True)
    centered = x_f32 - mean_val
    inv_std = lax.rsqrt(jnp.mean(centered * centered, axis=-1, keepdims=True) + LN_EPS)
    return centered * inv_std, inv_std


class Place:
    def __init__(self):
        me = lax.axis_index('model')
        self.core = me % 2
        self.x = (me // 2) % RING
        self.y = me // (2 * RING)
        self.me = me

    def index(self, d_y, d_x, core=None):
        core = self.core if core is None else core
        return (((self.y + d_y) % RING) * RING + (self.x + d_x) % RING) * 2 + core

    def peer(self, axis, offset):
        return self.index(offset % RING, 0) if axis == 'y' else self.index(0, offset % RING)

    def sibling(self):
        return self.index(0, 0, 1 - self.core)


def remote(src, dst, send_sem, recv_sem, device):
    return pltpu.make_async_remote_copy(src_ref=src, dst_ref=dst, send_sem=send_sem, recv_sem=recv_sem,
                                        device_id={'model': device}, device_id_type=MESH)


def enter(peers):
    barrier = pltpu.get_barrier_semaphore()
    for peer in peers:
        pl.semaphore_signal(barrier, inc=1, device_id={'model': peer}, device_id_type=MESH)
    pl.semaphore_wait(barrier, len(peers))


def pick(step, values):
    out = jnp.int32(0)
    for n, value in enumerate(values):
        out = jnp.where(step == n, value, out)
    return out


def add_into(dst, *sources):
    rows = dst.shape[0]
    tile = min(rows, 32)

    def tile_add(n, carry):
        at = pl.ds(pl.multiple_of(n * tile, tile), tile)
        total = dst[at, :].astype(jnp.float32)
        for source in sources:
            total += source[at, :].astype(jnp.float32)
        dst[at, :] = total.astype(dst.dtype)
        return carry

    lax.fori_loop(0, rows // tile, tile_add, 0)


def reduce_kernel(x_hbm, dy_hbm, seg_ref, gain_ref, wqkv_hbm, w1_hbm, wo_hbm, w2_hbm,
                  y_own, dx_own, dgain_ref, g_own, g_sib, full,
                  w_in, w_out, w1_raw, acc_in, acc_out, x_buf, dy_buf, a_scr, h_scr, d_scr, stage, half, last_full, tmp,
                  row_sem, w_sem, ws_sem, wr_sem, send_sem, half_sem, full_sem, tmp_sem, out_sem):
    place = Place()
    core = place.core
    _, seq_len, hidden = x_buf.shape
    mid = seq_len // 2
    n_qkv, n_up, n_o, n_dn = wqkv_hbm.shape[0], w1_hbm.shape[1], wo_hbm.shape[0], w2_hbm.shape[0]
    head_dim = n_o
    steps = len(ORDER)

    def row_of(step):
        d_y = pick(step, [o[0] for o in ORDER])
        d_x = pick(step, [o[1] for o in ORDER])
        return place.index(d_y, d_x)

    def row_copies(step):
        row, buf = row_of(step), step % 2
        return (pltpu.make_async_copy(x_hbm.at[row], x_buf.at[buf], row_sem.at[buf, 0]),
                pltpu.make_async_copy(dy_hbm.at[row], dy_buf.at[buf], row_sem.at[buf, 1]))

    def rows_at(ref, at, count):
        return ref.at[pl.ds(pl.multiple_of(at, 16), count)]

    up_spot = rows_at(w_in, 2 * n_qkv + core * n_up, n_up)
    spots = ((wqkv_hbm, rows_at(w_in, core * n_qkv, n_qkv)), (wo_hbm, rows_at(w_out, core * n_o, n_o)),
             (w2_hbm, rows_at(w_out, 2 * n_o + core * n_dn, n_dn)))

    raw = pltpu.make_async_copy(w1_hbm, w1_raw, w_sem.at[3])
    raw.start()
    for copy in row_copies(0):
        copy.start()
    mine = [pltpu.make_async_copy(src, dst, w_sem.at[n]) for n, (src, dst) in enumerate(spots)]
    for copy in mine:
        copy.start()
    enter([place.peer('x', 1), place.peer('x', -1), place.peer('y', 1), place.peer('y', -1), place.sibling()])
    swaps = [remote(src, dst, ws_sem.at[n], wr_sem.at[n], place.sibling()) for n, (src, dst) in enumerate(spots)]
    for copy in swaps:
        copy.start()
    raw.wait()
    turn = min(hidden, 256)
    for h in range(0, hidden, turn):
        up_spot[:, h:h + turn] = w1_raw[h:h + turn, :].T
    acc_in[...] = jnp.zeros_like(acc_in)
    acc_out[...] = jnp.zeros_like(acc_out)
    swaps.append(remote(up_spot, up_spot, ws_sem.at[3], wr_sem.at[3], place.sibling()))
    swaps[3].start()
    for copy in mine:
        copy.wait()
    for copy in swaps:
        copy.wait()

    gain = gain_ref[...].astype(jnp.float32)
    scale = head_dim ** -0.5
    sub = min(seq_len, 64)
    cols_step = min(hidden, 512)

    def piece_of(ref, piece):
        return ref.at[pl.ds(piece * mid, mid)]

    def landed(ref, sem):
        pltpu.make_async_copy(ref, ref, sem).wait()

    def slot_sends(slot):
        return [pltpu.make_async_copy(piece_of(stage.at[slot, t], piece), piece_of(stage.at[slot, t], piece),
                                      send_sem.at[slot, t, piece]) for t in range(2) for piece in range(2)]

    def event(n, t, piece, ring):
        d_y, d_x = ORDER[n]
        first, second = (('x', d_x), ('y', d_y)) if t == 0 else (('y', d_y), ('x', d_x))
        (axis, offset), line = (first, second[1]) if ring == 1 else (second, RING)
        ahead, behind = place.peer(axis, 1), place.peer(axis, -1)
        spot = piece_of(stage.at[SLOT[n], t], piece)

        def arrival(side):
            return piece_of(last_full.at[t, side] if line == RING else full.at[t, line, side], piece)

        def send(dst, recv_sem, device):
            remote(spot, dst, send_sem.at[SLOT[n], t, piece], recv_sem, device).start()

        if offset == 2:
            send(half.at[t, line, piece], half_sem.at[t, line, piece], ahead if piece == 0 else behind)
        elif offset in (1, 3):
            side = 0 if offset == 1 else 1
            if side == piece:
                landed(half.at[t, line, piece], half_sem.at[t, line, piece])
                add_into(spot, half.at[t, line, piece])
            send(arrival(side), full_sem.at[t, line, side, piece], ahead if side == 0 else behind)
        elif line == RING:
            for side in range(2):
                landed(arrival(side), full_sem.at[t, line, side, piece])
            add_into(spot, arrival(0), arrival(1))
        else:
            loads = [pltpu.make_async_copy(arrival(side), tmp.at[piece, side], tmp_sem.at[piece, side]) for side in range(2)]
            for side in range(2):
                landed(arrival(side), full_sem.at[t, line, side, piece])
                loads[side].start()
            for load in loads:
                load.wait()
            add_into(spot, tmp.at[piece, 0], tmp.at[piece, 1])

    def grad_copies():
        copies = []
        for n, (side, dst) in enumerate(((core, g_own), (1 - core, g_sib))):
            to = 0
            for m, (acc, at, count) in enumerate(((acc_in, side * n_qkv, n_qkv), (acc_in, 2 * n_qkv + side * n_up, n_up),
                                                  (acc_out, side * n_o, n_o), (acc_out, 2 * n_o + side * n_dn, n_dn))):
                copies.append(pltpu.make_async_copy(rows_at(acc, at, count), dst.at[pl.ds(to, count)], out_sem.at[4 * n + m]))
                to += count
        return copies

    def row_step(step, carry):
        buf = step % 2
        slot = pick(step, SLOT)
        for copy in row_copies(step):
            copy.wait()

        @pl.when(step + 1 < steps)
        def _():
            for copy in row_copies(step + 1):
                copy.start()

        for t in range(0, seq_len, sub):
            normed, _ = norm_rows(x_buf[buf, t:t + sub, :].astype(jnp.float32))
            a_scr[t:t + sub, :] = (normed * gain).astype(jnp.bfloat16)

        proj = dot(w_in[...], a_scr[...], NT)
        qkv = proj[:2 * n_qkv].astype(jnp.bfloat16)
        up = proj[2 * n_qkv:].astype(jnp.bfloat16).astype(jnp.float32)
        d_proj = dot(w_out[...], dy_buf[buf], NT).astype(jnp.bfloat16)
        d_attn = d_proj[:2 * n_o]
        d_hid = d_proj[2 * n_o:].astype(jnp.float32)
        cdf = 0.5 * (1.0 + lax.erf(up * (0.5 ** 0.5)))
        h_scr[2 * n_o:, :] = (up * cdf).astype(jnp.bfloat16)
        slope = cdf + up * (jnp.exp(-0.5 * up * up) * 0.3989422804014327)
        d_scr[2 * n_qkv:, :] = (d_hid * slope).astype(jnp.bfloat16)

        seg_row = seg_ref[pl.ds(row_of(step), 1), :]
        classes = lax.broadcasted_iota(jnp.int32, (16, seq_len), 0)
        one_hot = (classes == jnp.broadcast_to(seg_row, (16, seq_len))).astype(jnp.bfloat16)
        same = dot(one_hot, one_hot, TN) > 0.5
        key_id = lax.broadcasted_iota(jnp.int32, (seq_len, seq_len), 0)
        query_id = lax.broadcasted_iota(jnp.int32, (seq_len, seq_len), 1)
        allowed = (key_id <= query_id) & same
        for head in range(2):
            at = head * n_qkv
            query = qkv[at:at + head_dim]
            keys = qkv[at + head_dim:at + 2 * head_dim]
            values = qkv[at + 2 * head_dim:at + 3 * head_dim]
            d_o = d_attn[head * head_dim:(head + 1) * head_dim]
            scores = jnp.where(allowed, dot(keys, query, TN) * scale, -1e30)
            expd = jnp.exp(scores - jnp.max(scores, axis=0, keepdims=True))
            probs = expd / jnp.sum(expd, axis=0, keepdims=True)
            probs_b = probs.astype(jnp.bfloat16)
            h_scr[head * head_dim:(head + 1) * head_dim, :] = dot(values, probs_b, NN).astype(jnp.bfloat16)
            d_p = dot(values, d_o, TN)
            d_s = (probs * (d_p - jnp.sum(d_p * probs, axis=0, keepdims=True)) * scale).astype(jnp.bfloat16)
            d_scr[at:at + head_dim, :] = dot(keys, d_s, NN).astype(jnp.bfloat16)
            d_scr[at + head_dim:at + 2 * head_dim, :] = dot(query, d_s, NT).astype(jnp.bfloat16)
            d_scr[at + 2 * head_dim:at + 3 * head_dim, :] = dot(d_o, probs_b, NT).astype(jnp.bfloat16)

        @pl.when(pick(step, [int(SLOT[n] in SLOT[:n]) for n in range(steps)]) == 1)
        def _():
            for copy in slot_sends(slot):
                copy.wait()

        for h in range(0, hidden, cols_step):
            cols = slice(h, h + cols_step)
            stage[slot, 0, :, cols] = dot(h_scr[...], w_out[:, cols], TN).astype(jnp.bfloat16)
            stage[slot, 1, :, cols] = dot(d_scr[...], w_in[:, cols], TN).astype(jnp.bfloat16)
            acc_in[:, cols] += dot(d_scr[...], a_scr[:, cols], NN)
            acc_out[:, cols] += dot(h_scr[...], dy_buf[buf, :, cols], NN)

        for n in range(steps):
            @pl.when(step == n)
            def _():
                if n == steps - 1:
                    for copy in grad_copies():
                        copy.start()
                for work in EVENTS[n]:
                    event(*work)
        return carry

    lax.fori_loop(0, steps, row_step, 0)
    last, buf = SLOT[-1], (steps - 1) % 2
    for slot in range(SLOTS):
        if slot != last:
            for copy in slot_sends(slot):
                copy.wait()

    fine = min(seq_len, 32)

    def finish(n, d_gain):
        at = pl.ds(pl.multiple_of(n * fine, fine), fine)
        x_f32 = x_buf[buf, at, :].astype(jnp.float32)
        normed, inv_std = norm_rows(x_f32)
        grad = stage[last, 1, at, :].astype(jnp.float32)
        stage[last, 0, at, :] = (x_f32 + stage[last, 0, at, :].astype(jnp.float32)).astype(jnp.bfloat16)
        d_hat = grad * gain
        d_x = inv_std * (d_hat - jnp.mean(d_hat, axis=-1, keepdims=True) - normed * jnp.mean(d_hat * normed, axis=-1, keepdims=True))
        stage[last, 1, at, :] = (dy_buf[buf, at, :].astype(jnp.float32) + d_x).astype(jnp.bfloat16)
        return d_gain + jnp.sum(grad * normed, axis=0, keepdims=True)

    dgain_ref[...] = lax.fori_loop(0, seq_len // fine, finish, jnp.zeros((1, hidden), jnp.float32))
    ends = [pltpu.make_async_copy(stage.at[last, t], dst, tmp_sem.at[0, t]) for t, dst in ((0, y_own), (1, dx_own))]
    for copy in ends:
        copy.start()
    for copy in ends + grad_copies():
        copy.wait()


def gather_kernel(y_own, dx_own, dgain_ref, g_own, g_sib, y_lo, y_hi, dx_all, g_recv, dgain_out, grads, d_up,
                  gain_scr, g_buf, t_buf, send_sem, link_sem, pair_sem, pair_recv, own_sem, g_sem, gb_sem, dg_send, dg_recv):
    place = Place()
    _, seq_len, hidden = dx_all.shape
    mid = seq_len // 2
    links = (('x', 1), ('x', -1), ('y', 1), ('y', -1))
    enter([place.peer(a, o) for a in ('x', 'y') for o in (1, 2, 3)] + [place.sibling()])

    issued = {link: [] for link in links}
    sends = []

    def row_index(t, d_1, d_2):
        return place.index(d_1 % RING, d_2 % RING) if t == 0 else place.index(d_2 % RING, d_1 % RING)

    def spot_of(t, row, piece):
        if t == 1:
            return dx_all.at[row, pl.ds(piece * mid, mid)]
        return (y_lo, y_hi)[piece].at[row]

    def source(t, d_1, d_2, piece):
        if (d_1, d_2) == (0, 0):
            return (y_own, dx_own)[t].at[pl.ds(piece * mid, mid)]
        return spot_of(t, row_index(t, d_1, d_2), piece)

    def issue(link, t, d_1, d_2, piece):
        n = len(issued[link])
        which = links.index(link)
        copy = remote(source(t, d_1, d_2, piece), spot_of(t, row_index(t, d_1, d_2), piece),
                      send_sem.at[which, n], link_sem.at[which, n], place.peer(*link))
        copy.start()
        sends.append(copy)
        issued[link].append((t, d_1, d_2, piece))

    def pair(t, d_1, d_2, piece):
        slot = ((d_1 % RING) * RING + d_2 % RING) * 2 + piece
        copy = remote(source(t, d_1, d_2, piece), spot_of(t, row_index(t, d_1, d_2), piece),
                      pair_sem.at[t, slot], pair_recv.at[t, piece], place.sibling())
        copy.start()
        sends.append(copy)

    axes = (('y', 'x'), ('x', 'y'))
    for ring in range(2):
        for piece in range(2):
            for t in range(2):
                for way in (1, -1):
                    issue((axes[t][ring], way), t, 0, 0, piece)
    locals_ = []
    for t in range(2):
        for piece in range(2):
            pair(t, 0, 0, piece)
            copy = pltpu.make_async_copy(source(t, 0, 0, piece), spot_of(t, place.me, piece), own_sem.at[t, piece])
            copy.start()
            locals_.append(copy)
    g_copy = remote(g_sib, g_recv, g_sem.at[0], g_sem.at[1], place.sibling())
    g_copy.start()

    total = dgain_ref[...]
    for n, (axis, offsets) in enumerate((('core', (1,)), ('x', (1, 2, 3)), ('y', (1, 2, 3)))):
        spot = {'core': place.core, 'x': place.x, 'y': place.y}[axis]
        gain_scr[n, spot] = total
        copies = []
        for m, offset in enumerate(offsets):
            device = place.sibling() if axis == 'core' else place.peer(axis, offset)
            copies.append(remote(gain_scr.at[n, spot], gain_scr.at[n, spot], dg_send.at[n, m], dg_recv.at[n, m], device))
        for copy in copies:
            copy.start()
        for copy in copies:
            copy.wait()
        total = gain_scr[n, 0]
        for m in range(1, len(offsets) + 1):
            total = total + gain_scr[n, m]
    dgain_out[...] = total.astype(dgain_out.dtype)

    tile, turn = g_buf.shape[1], t_buf.shape[2]
    n_up = d_up.shape[1]
    n_qkv = 3 * tile

    def grad_tile(at, to):
        loads = [pltpu.make_async_copy(g.at[pl.ds(at, tile)], g_buf.at[n], gb_sem.at[n]) for n, g in enumerate((g_own, g_recv))]
        for load in loads:
            load.start()
        for load in loads:
            load.wait()
        grads[to:to + tile, :] = (g_buf[0] + g_buf[1]).astype(grads.dtype)

    def up_tile(h):
        loads = [pltpu.make_async_copy(g.at[pl.ds(n_qkv, n_up), pl.ds(h, turn)], t_buf.at[n], gb_sem.at[n]) for n, g in enumerate((g_own, g_recv))]
        for load in loads:
            load.start()
        for load in loads:
            load.wait()
        d_up[h:h + turn, :] = (t_buf[0] + t_buf[1]).T.astype(d_up.dtype)

    jobs = [functools.partial(grad_tile, at, at) for at in range(0, n_qkv, tile)]
    jobs += [functools.partial(grad_tile, at, at - n_up) for at in range(n_qkv + n_up, g_own.shape[0], tile)]
    jobs += [functools.partial(up_tile, h) for h in range(0, hidden, turn)]

    rounds = RING * RING - 1
    for n in range(rounds):
        for link in links:
            t, d_1, d_2, piece = issued[link][n]
            axis, way = link
            on_first = axis == axes[t][0]
            d_1, d_2 = (d_1 - way, d_2) if on_first else (d_1, d_2 - way)
            spot = spot_of(t, row_index(t, d_1, d_2), piece)
            pltpu.make_async_copy(spot, spot, link_sem.at[links.index(link), n]).wait()
            along = d_1 if on_first else d_2
            if abs(along) == 1 and piece == (0 if way == 1 else 1):
                issue(link, t, d_1, d_2, piece)
            if on_first:
                for other in (1, -1):
                    issue((axes[t][1], other), t, d_1, d_2, piece)
            pair(t, d_1, d_2, piece)
        if n == 2:
            g_copy.wait()
        if n >= 2:
            for job in jobs[(n - 2) * len(jobs) // (rounds - 2):(n - 1) * len(jobs) // (rounds - 2)]:
                job()

    for t in range(2):
        for piece in range(2):
            theirs = dx_all.at[pl.ds(0, RING * RING), pl.ds(piece * mid, mid)] if t else (y_lo, y_hi)[piece].at[pl.ds(0, RING * RING)]
            pltpu.make_async_copy(theirs, theirs, pair_recv.at[t, piece]).wait()
    for copy in sends:
        copy.wait_send()
    for copy in locals_:
        copy.wait()


def place_kernel(y_lo, y_hi, dx_all, grads, d_up, y_out, dx_out, d_wqkv, d_wout, d_wdown, d_wup, bounce, in_sem, out_sem, sem):
    rows, mid, _ = y_lo.shape
    n_qkv, n_o, n_dn = d_wqkv.shape[0], d_wout.shape[0], d_wdown.shape[0]
    bufs, per = bounce.shape[0], bounce.shape[1]
    count = rows // per
    loads = [pltpu.make_async_copy(y_hi.at[pl.ds(n * per, per)], bounce.at[n % bufs], in_sem.at[n % bufs]) for n in range(count)]
    stores = [pltpu.make_async_copy(bounce.at[n % bufs], y_out.at[pl.ds(n * per, per), pl.ds(mid, mid)], out_sem.at[n % bufs]) for n in range(count)]
    for n in range(min(bufs, count)):
        loads[n].start()
    direct = [(y_lo, y_out.at[:, pl.ds(0, mid)]), (dx_all, dx_out), (grads.at[pl.ds(0, n_qkv)], d_wqkv),
              (grads.at[pl.ds(n_qkv, n_o)], d_wout), (grads.at[pl.ds(n_qkv + n_o, n_dn)], d_wdown), (d_up, d_wup)]
    copies = [pltpu.make_async_copy(src, dst, sem.at[n]) for n, (src, dst) in enumerate(direct)]
    for copy in copies:
        copy.start()
    for n in range(count):
        loads[n].wait()
        stores[n].start()
        if n >= 1 and n - 1 + bufs < count:
            stores[n - 1].wait()
            loads[n - 1 + bufs].start()
    for n in range(max(0, count - bufs), count):
        stores[n].wait()
    for copy in copies:
        copy.wait()


def solution(mesh):
    devices = mesh.shape['model']
    assert devices == 2 * RING * RING and math.isqrt(devices // 2) == RING

    def body(x_in, seg_ids, ln_gain, w_qkv, w_out, w_up, w_down, dy_in):
        rows, seq_len, hidden = x_in.shape
        assert rows == devices
        wqkv = w_qkv.transpose(1, 2, 3, 0).reshape(-1, hidden)
        wo = w_out.reshape(-1, hidden)
        n_qkv, n_up, n_o, n_dn = wqkv.shape[0], w_up.shape[1], wo.shape[0], w_down.shape[0]
        n_in, n_out = n_qkv + n_up, n_o + n_dn
        bf16, f32 = jnp.bfloat16, jnp.float32
        vmem, anywhere = pl.BlockSpec(memory_space=pltpu.VMEM), pl.BlockSpec(memory_space=pl.ANY)
        dma = pltpu.SemaphoreType.DMA
        shape = jax.ShapeDtypeStruct
        mid = seq_len // 2
        y_own, dx_own, d_gain, g_own, g_sib, _ = pl.pallas_call(
            reduce_kernel,
            in_specs=[anywhere, anywhere, vmem, vmem] + [anywhere] * 4,
            out_specs=[anywhere, anywhere, vmem, anywhere, anywhere, anywhere],
            out_shape=[shape((seq_len, hidden), bf16), shape((seq_len, hidden), bf16), shape((1, hidden), f32),
                       shape((n_in + n_out, hidden), f32), shape((n_in + n_out, hidden), f32),
                       shape((2, RING, 2, seq_len, hidden), bf16)],
            scratch_shapes=[
                pltpu.VMEM((2 * n_in, hidden), bf16), pltpu.VMEM((2 * n_out, hidden), bf16), pltpu.VMEM((hidden, n_up), bf16),
                pltpu.VMEM((2 * n_in, hidden), f32), pltpu.VMEM((2 * n_out, hidden), f32),
                pltpu.VMEM((2, seq_len, hidden), bf16), pltpu.VMEM((2, seq_len, hidden), bf16),
                pltpu.VMEM((seq_len, hidden), bf16),
                pltpu.VMEM((2 * n_out, seq_len), bf16), pltpu.VMEM((2 * n_in, seq_len), bf16),
                pltpu.VMEM((SLOTS, 2, seq_len, hidden), bf16),
                pltpu.VMEM((2, RING + 1, 2, mid, hidden), bf16),
                pltpu.VMEM((2, 2, seq_len, hidden), bf16),
                pltpu.VMEM((2, 2, mid, hidden), bf16),
                dma((2, 2)), dma((4,)), dma((4,)), dma((4,)), dma((SLOTS, 2, 2)),
                dma((2, RING + 1, 2)), dma((2, RING + 1, 2, 2)), dma((2, 2)), dma((8,)),
            ],
            compiler_params=pltpu.CompilerParams(collective_id=0, has_side_effects=True, vmem_limit_bytes=VMEM_LIMIT),
            name="rows_reduce",
        )(x_in, dy_in, seg_ids, ln_gain.reshape(1, hidden), wqkv, w_up, wo, w_down)

        per_link = RING * RING - 1
        y_lo, y_hi, dx_all, _, d_gain, grads, d_up = pl.pallas_call(
            gather_kernel,
            in_specs=[anywhere, anywhere, vmem, anywhere, anywhere],
            out_specs=[vmem, anywhere, vmem, anywhere, vmem, vmem, vmem],
            out_shape=[pltpu.VMEM((rows, mid, hidden), bf16), shape((rows, mid, hidden), bf16), pltpu.VMEM((rows, seq_len, hidden), bf16),
                       shape(g_sib.shape, f32), shape((1, hidden), bf16),
                       pltpu.VMEM((n_qkv + n_out, hidden), bf16), pltpu.VMEM((hidden, n_up), bf16)],
            scratch_shapes=[
                pltpu.VMEM((3, RING, 1, hidden), f32), pltpu.VMEM((2, n_o, hidden), f32), pltpu.VMEM((2, n_up, min(hidden, 256)), f32),
                dma((4, per_link)), dma((4, per_link)), dma((2, 2 * RING * RING)), dma((2, 2)), dma((2, 2)), dma((2,)), dma((2,)),
                dma((3, 3)), dma((3, 3)),
            ],
            compiler_params=pltpu.CompilerParams(collective_id=1, has_side_effects=True, vmem_limit_bytes=6 * 2 ** 20),
            name="rows_gather",
        )(y_own, dx_own, d_gain, g_own, g_sib)

        bufs = 4
        fixed = lambda array: pltpu.with_memory_space_constraint(array, pltpu.VMEM)
        y_out, dx_out, d_wqkv, d_wout, d_wdown, d_wup = pl.pallas_call(
            place_kernel,
            in_specs=[vmem, anywhere, vmem, vmem, vmem],
            out_specs=[anywhere] * 6,
            out_shape=[shape(x_in.shape, bf16), shape(x_in.shape, bf16), shape(wqkv.shape, bf16), shape(wo.shape, bf16),
                       shape(w_down.shape, bf16), shape(w_up.shape, bf16)],
            scratch_shapes=[pltpu.VMEM((bufs, 2, mid, hidden), bf16), dma((bufs,)), dma((bufs,)), dma((6,))],
            compiler_params=pltpu.CompilerParams(vmem_limit_bytes=6 * 2 ** 20),
            name="rows_place",
        )(fixed(y_lo), pltpu.with_memory_space_constraint(y_hi, pltpu.HBM), fixed(dx_all), fixed(grads), fixed(d_up))
        d_wqkv = d_wqkv.reshape(w_qkv.shape[1:] + (hidden,)).transpose(3, 0, 1, 2)
        return y_out, dx_out, d_gain.reshape(hidden), d_wqkv, d_wout.reshape(w_out.shape), d_wup, d_wdown

    in_specs = (P('data'), P('data'), P(), P(None, 'model'), P('model'), P(None, 'model'), P('model'), P('data'))
    out_specs = (P('data'), P('data'), P('data'), P('data', 'model'), P(('data', 'model')), P('data', 'model'), P(('data', 'model')))
    return jax.shard_map(body, mesh=mesh, in_specs=in_specs, out_specs=out_specs, check_vma=False)
```

time: 499 us -> 420 us (0.84)
  local copies, waits for them, and re-layouts: 56.1 us -> 1.3 us
  Pallas kernels: 435 us -> 416 us
  other arithmetic: 6.26 us -> 0.63 us
    unnamed x6 -> x2, local copies, waits for them, and re-layouts: 50.3 us -> 0.01 us
    pallas_call x1, Pallas kernels: 248 us -> 203 us  [body(): pl.pallas_call(reduce_kernel, in_specs=[anywhere, anywhere, vmem, vmem] +...]
    pallas_call x0 -> x1, Pallas kernels: none -> 28.8 us  [body(): pl.pallas_call(place_kernel, in_specs=[vmem, anywhere, vmem, vmem, vmem],...]
    convert_element_type x1 -> x0, other arithmetic: 5.64 us -> none  [body(): grads = (g_own + g_recv).astype(bf16)]
where the time goes in v3:
time: 420 us; the launch traced here: 419 us
  Pallas kernels  416 us (99%)
    pallas_call x1, Pallas kernels, body(): pl.pallas_call(reduce_kernel, in_specs=[anywhere, anywhere, vmem, vmem] +...  203 us
    pallas_call x1, Pallas kernels, body(): pl.pallas_call(gather_kernel, in_specs=[anywhere, anywhere, vmem, anywher...  184 us
    pallas_call x1, Pallas kernels, body(): pl.pallas_call(place_kernel, in_specs=[vmem, anywhere, vmem, vmem, vmem],...  28.8 us

profile of v3, /device:TPU:97, one launch (start us, length us, event | category | flops | bytes accessed | tf_op | source)
XLA Modules:
  0.0 418.8 jit_solution(9473756201700351439)
XLA Ops:
  0.6 1.3 reshape.32.gain_ref
  1.9 203.1 %rows_reduce.1 = (bf16[256,2048]{1,0:T(8,128)(2,1)}, bf16[256,2048]{1,0:T(8,128)(2,1)}, f32[1,2048]{1,0:T(1,128)}, f32[768,2048]{1,0:T(8,128)}, f32[768,2048]{1,...) custom-call(bf16[32,256,2048]{2,1,0:T(8,128)(2,1)} %x_hbm.1, bf16[32,256,2048]{2,1,0:T(8,128)(2,1)} %dy_hbm.1, ...), custom_call_target="tpu_custom_call" | custom-call | tf_op jit(solution)/shard_map/rows_reduce/pallas_call | solution.py:489
  205.1 184.2 %rows_gather.1 = (bf16[32,128,2048]{2,1,0:T(8,128)(2,1)S(1)}, bf16[32,128,2048]{2,1,0:T(8,128)(2,1)}, bf16[32,256,2048]{2,1,0:T(8,128)(2,1)S(1)}, f32[768,2048]{...) custom-call(bf16[256,2048]{1,0:T(8,128)(2,1)} %get-tuple-element.24.y_own, ...), custom_call_target="tpu_custom_call" | custom-call | tf_op jit(solution)/shard_map/rows_gather/pallas_call | solution.py:514
  389.3 0.0 copy-start
  389.3 28.8 %rows_place.1 = (bf16[32,256,2048]{2,1,0:T(8,128)(2,1)}, bf16[32,256,2048]{2,1,0:T(8,128)(2,1)}, bf16[192,2048]{1,0:T(8,128)(2,1)}, bf16[64,2048]{1,0:T(8,128)(2...) custom-call(bf16[32,128,2048]{2,1,0:T(8,128)(2,1)S(1)} %get-tuple-element.29.y_lo, ...), custom_call_target="tpu_custom_call" | custom-call | tf_op jit(solution)/shard_map/rows_place/pallas_call | solution.py:532
  418.2 0.0 copy-done
  418.2 0.6 reduce
Async XLA Ops:
  389.3 28.8 %copy-start = (bf16[1,2048]{1,0:T(2,128)(2,1)S(1)}, bf16[1,2048]{1,0:T(2,128)(2,1)}, u32[]{:S(2)}) copy-start(bf16[1,2048]{1,0:T(2,128)(2,1)} %get-tuple-element.36) | copy-start | bytes 12292

commit v4 on v3

--- a/solution.py
+++ b/solution.py
@@ -14,29 +14,29 @@
 NT = (((1,), (1,)), ((), ()))
 NN = (((1,), (0,)), ((), ()))
 TN = (((0,), (0,)), ((), ()))
-ORDER = ((2, 2), (1, 2), (2, 3), (3, 2), (2, 1), (0, 1), (1, 1), (3, 3),
-         (2, 0), (0, 2), (3, 0), (1, 3), (3, 1), (0, 3), (1, 0), (0, 0))
-SLOT = (0, 1, 2, 3, 4, 0, 1, 2, 3, 4, 2, 1, 3, 4, 1, 3)
+ORDER = ((2, 2), (3, 2), (2, 1), (2, 3), (1, 2), (0, 2), (2, 0), (3, 3),
+         (1, 1), (3, 1), (0, 3), (1, 3), (1, 0), (3, 0), (0, 1), (0, 0))
+SLOT = (0, 1, 2, 3, 4, 0, 1, 2, 3, 4, 0, 1, 2, 3, 4, 1)
 SLOTS = max(SLOT) + 1
 EVENTS = (
-    ((0, 0, 0, 1), (0, 0, 1, 1), (0, 1, 0, 1), (0, 1, 1, 1)),
-    ((1, 0, 0, 1), (1, 0, 1, 1), (1, 1, 1, 1)),
-    ((2, 0, 0, 1), (2, 1, 0, 1), (2, 1, 1, 1), (1, 1, 0, 1), (2, 0, 1, 1)),
-    ((3, 0, 0, 1), (3, 0, 1, 1), (3, 1, 0, 1), (3, 1, 1, 1)),
-    ((4, 0, 1, 1), (4, 1, 0, 1), (4, 1, 1, 1), (4, 0, 0, 1)),
-    ((5, 0, 1, 1),),
-    ((6, 0, 1, 1), (6, 1, 1, 1), (6, 0, 0, 1)),
-    ((7, 0, 0, 1), (7, 1, 0, 1), (7, 1, 1, 1)),
-    ((8, 1, 0, 1), (8, 1, 1, 1), (8, 0, 1, 1), (8, 0, 1, 2), (6, 1, 0, 1), (7, 0, 1, 1), (8, 0, 0, 1), (8, 0, 0, 2)),
-    ((9, 0, 0, 1), (9, 0, 1, 1), (9, 1, 0, 1), (9, 1, 0, 2), (9, 1, 1, 1), (9, 1, 1, 2)),
-    ((10, 1, 0, 1),),
-    ((11, 0, 0, 1), (11, 1, 1, 1), (11, 0, 1, 1), (11, 1, 0, 1), (10, 1, 1, 1)),
-    ((12, 0, 1, 1), (12, 1, 0, 1), (12, 0, 0, 1), (12, 1, 1, 1), (5, 0, 0, 1)),
-    ((13, 0, 0, 1), (13, 0, 1, 1), (13, 1, 1, 1), (13, 1, 1, 2)),
-    ((14, 1, 1, 1), (14, 1, 0, 1), (14, 0, 0, 1), (14, 0, 0, 2), (10, 0, 1, 1), (10, 0, 1, 2), (13, 1, 0, 1), (13, 1, 0, 2), (14, 0, 1, 1), (14, 0, 1, 2), (10, 0, 0, 1), (10, 0, 0, 2), (5, 1, 0, 1), (5, 1, 0, 2)),
-    ((15, 1, 1, 1), (15, 0, 0, 1), (15, 0, 1, 1), (5, 1, 1, 1), (5, 1, 1, 2), (15, 1, 0, 1), (15, 1, 0, 2), (15, 1, 1, 2), (15, 0, 0, 2), (15, 0, 1, 2)),
+    (((0, 0, 0, 1), (0, 0, 1, 1), (0, 1, 0, 1), (0, 1, 1, 1)), ()),
+    (((1, 0, 0, 1), (1, 0, 1, 1), (1, 1, 0, 1)), ()),
+    (((2, 0, 1, 1), (2, 1, 0, 1), (2, 1, 1, 1), (1, 1, 1, 1), (2, 0, 0, 1)), ()),
+    (((3, 0, 0, 1), (3, 1, 0, 1), (3, 1, 1, 1), (3, 0, 1, 1)), ()),
+    (((4, 0, 0, 1), (4, 0, 1, 1), (4, 1, 1, 1), (4, 1, 0, 1)), ()),
+    (((5, 0, 0, 1), (5, 0, 1, 1)), ()),
+    (((6, 1, 0, 1), (6, 1, 1, 1), (6, 0, 0, 1), (6, 0, 0, 2), (6, 0, 1, 1), (6, 0, 1, 2)), ((5, 1, 1, 1), (5, 1, 1, 2))),
+    (((7, 0, 0, 1), (7, 1, 0, 1), (7, 0, 1, 1), (7, 1, 1, 1)), ((5, 1, 0, 1), (5, 1, 0, 2))),
+    (((8, 0, 1, 1), (8, 1, 1, 1), (8, 1, 0, 1), (8, 0, 0, 1)), ()),
+    (((9, 0, 1, 1), (9, 1, 0, 1), (9, 0, 0, 1), (9, 1, 1, 1)), ()),
+    (((10, 0, 0, 1), (10, 0, 1, 1)), ()),
+    (((11, 0, 0, 1), (11, 1, 1, 1), (11, 1, 0, 1), (11, 0, 1, 1)), ()),
+    (((12, 1, 1, 1), (12, 1, 0, 1)), ()),
+    (((13, 1, 0, 1), (13, 1, 1, 1), (13, 0, 1, 1), (13, 0, 1, 2)), ((10, 1, 1, 1), (10, 1, 1, 2))),
+    (((14, 0, 1, 1), (14, 0, 0, 1), (14, 1, 0, 1), (14, 1, 0, 2), (13, 0, 0, 1), (13, 0, 0, 2), (14, 1, 1, 1), (14, 1, 1, 2), (10, 1, 0, 1), (10, 1, 0, 2)), ((12, 0, 0, 1), (12, 0, 0, 2))),
+    ((), ((15, 0, 1, 1), (15, 1, 1, 1), (12, 0, 1, 1), (12, 0, 1, 2), (15, 0, 0, 1), (15, 1, 0, 1), (15, 0, 0, 2), (15, 1, 0, 2), (15, 1, 1, 2), (15, 0, 1, 2))),
 )
-VMEM_LIMIT = 62 * 2 ** 20
+VMEM_LIMIT = 60 * 2 ** 20
 
 
 def dot(lhs, rhs, dims):
@@ -120,10 +120,8 @@
         d_x = pick(step, [o[1] for o in ORDER])
         return place.index(d_y, d_x)
 
-    def row_copies(step):
-        row, buf = row_of(step), step % 2
-        return (pltpu.make_async_copy(x_hbm.at[row], x_buf.at[buf], row_sem.at[buf, 0]),
-                pltpu.make_async_copy(dy_hbm.at[row], dy_buf.at[buf], row_sem.at[buf, 1]))
+    def row_copy(step, buf, n):
+        return pltpu.make_async_copy((x_hbm, dy_hbm)[n].at[row_of(step)], (x_buf, dy_buf)[n].at[buf], row_sem.at[buf, n])
 
     def rows_at(ref, at, count):
         return ref.at[pl.ds(pl.multiple_of(at, 16), count)]
@@ -132,33 +130,43 @@
     spots = ((wqkv_hbm, rows_at(w_in, core * n_qkv, n_qkv)), (wo_hbm, rows_at(w_out, core * n_o, n_o)),
              (w2_hbm, rows_at(w_out, 2 * n_o + core * n_dn, n_dn)))
 
+    gain = gain_ref[...].astype(jnp.float32)[None, :]
+    sub = min(seq_len, 16)
+
+    def norm_row(buf):
+        for t in range(0, seq_len, sub):
+            normed, _ = norm_rows(x_buf[buf, t:t + sub, :].astype(jnp.float32))
+            a_scr[t:t + sub, :] = (normed * gain).astype(jnp.bfloat16)
+
+    peers = [place.peer('x', 1), place.peer('x', -1), place.peer('y', 1), place.peer('y', -1), place.sibling()]
+    barrier = pltpu.get_barrier_semaphore()
+    for peer in peers:
+        pl.semaphore_signal(barrier, inc=1, device_id={'model': peer}, device_id_type=MESH)
     raw = pltpu.make_async_copy(w1_hbm, w1_raw, w_sem.at[3])
     raw.start()
-    for copy in row_copies(0):
-        copy.start()
+    for n in range(2):
+        row_copy(0, 0, n).start()
     mine = [pltpu.make_async_copy(src, dst, w_sem.at[n]) for n, (src, dst) in enumerate(spots)]
     for copy in mine:
-        copy.start()
-    enter([place.peer('x', 1), place.peer('x', -1), place.peer('y', 1), place.peer('y', -1), place.sibling()])
-    swaps = [remote(src, dst, ws_sem.at[n], wr_sem.at[n], place.sibling()) for n, (src, dst) in enumerate(spots)]
-    for copy in swaps:
         copy.start()
     raw.wait()
     turn = min(hidden, 256)
     for h in range(0, hidden, turn):
         up_spot[:, h:h + turn] = w1_raw[h:h + turn, :].T
+    pl.semaphore_wait(barrier, len(peers))
+    swaps = [remote(src, dst, ws_sem.at[n], wr_sem.at[n], place.sibling()) for n, (src, dst) in enumerate(spots)]
+    swaps.append(remote(up_spot, up_spot, ws_sem.at[3], wr_sem.at[3], place.sibling()))
+    for n in (0, 3, 1, 2):
+        swaps[n].start()
+    row_copy(0, 0, 0).wait()
+    norm_row(0)
     acc_in[...] = jnp.zeros_like(acc_in)
     acc_out[...] = jnp.zeros_like(acc_out)
-    swaps.append(remote(up_spot, up_spot, ws_sem.at[3], wr_sem.at[3], place.sibling()))
-    swaps[3].start()
-    for copy in mine:
-        copy.wait()
-    for copy in swaps:
-        copy.wait()
-
-    gain = gain_ref[...].astype(jnp.float32)
+    mine[0].wait()
+    for n in (0, 3):
+        swaps[n].wait()
+
     scale = head_dim ** -0.5
-    sub = min(seq_len, 64)
     cols_step = min(hidden, 512)
 
     def piece_of(ref, piece):
@@ -215,25 +223,54 @@
                 to += count
         return copies
 
+    def grad_cols(buf, h):
+        cols = slice(h, h + cols_step)
+        acc_in[:, cols] += dot(d_scr[...], a_scr[:, cols], NN)
+        acc_out[:, cols] += dot(h_scr[...], dy_buf[buf, :, cols], NN)
+
+    def attend(head, qkv, d_attn, allowed):
+        at = head * n_qkv
+        query = qkv[at:at + head_dim]
+        keys = qkv[at + head_dim:at + 2 * head_dim]
+        values = qkv[at + 2 * head_dim:at + 3 * head_dim]
+        d_o = d_attn[head * head_dim:(head + 1) * head_dim]
+        scores = jnp.where(allowed, dot(keys, query, TN) * scale, -1e30)
+        expd = jnp.exp(scores - jnp.max(scores, axis=0, keepdims=True))
+        probs = expd / jnp.sum(expd, axis=0, keepdims=True)
+        probs_b = probs.astype(jnp.bfloat16)
+        h_scr[head * head_dim:(head + 1) * head_dim, :] = dot(values, probs_b, NN).astype(jnp.bfloat16)
+        d_p = dot(values, d_o, TN)
+        d_s = (probs * (d_p - jnp.sum(d_p * probs, axis=0, keepdims=True)) * scale).astype(jnp.bfloat16)
+        d_scr[at:at + head_dim, :] = dot(keys, d_s, NN).astype(jnp.bfloat16)
+        d_scr[at + head_dim:at + 2 * head_dim, :] = dot(query, d_s, NT).astype(jnp.bfloat16)
+        d_scr[at + 2 * head_dim:at + 3 * head_dim, :] = dot(d_o, probs_b, NT).astype(jnp.bfloat16)
+
     def row_step(step, carry):
         buf = step % 2
         slot = pick(step, SLOT)
-        for copy in row_copies(step):
-            copy.wait()
+        tiles = range(0, hidden, cols_step)
+
+        @pl.when(step > 0)
+        def _():
+            row_copy(step, buf, 0).wait()
+            norm_row(buf)
+
+        row_copy(step, buf, 1).wait()
 
         @pl.when(step + 1 < steps)
         def _():
-            for copy in row_copies(step + 1):
-                copy.start()
-
-        for t in range(0, seq_len, sub):
-            normed, _ = norm_rows(x_buf[buf, t:t + sub, :].astype(jnp.float32))
-            a_scr[t:t + sub, :] = (normed * gain).astype(jnp.bfloat16)
+            for n in range(2):
+                row_copy(step + 1, 1 - buf, n).start()
+
+        @pl.when(step == 0)
+        def _():
+            for copy in mine[1:] + swaps[1:3]:
+                copy.wait()
 
         proj = dot(w_in[...], a_scr[...], NT)
+        d_proj = dot(w_out[...], dy_buf[buf], NT).astype(jnp.bfloat16)
         qkv = proj[:2 * n_qkv].astype(jnp.bfloat16)
         up = proj[2 * n_qkv:].astype(jnp.bfloat16).astype(jnp.float32)
-        d_proj = dot(w_out[...], dy_buf[buf], NT).astype(jnp.bfloat16)
         d_attn = d_proj[:2 * n_o]
         d_hid = d_proj[2 * n_o:].astype(jnp.float32)
         cdf = 0.5 * (1.0 + lax.erf(up * (0.5 ** 0.5)))
@@ -249,68 +286,69 @@
         query_id = lax.broadcasted_iota(jnp.int32, (seq_len, seq_len), 1)
         allowed = (key_id <= query_id) & same
         for head in range(2):
-            at = head * n_qkv
-            query = qkv[at:at + head_dim]
-            keys = qkv[at + head_dim:at + 2 * head_dim]
-            values = qkv[at + 2 * head_dim:at + 3 * head_dim]
-            d_o = d_attn[head * head_dim:(head + 1) * head_dim]
-            scores = jnp.where(allowed, dot(keys, query, TN) * scale, -1e30)
-            expd = jnp.exp(scores - jnp.max(scores, axis=0, keepdims=True))
-            probs = expd / jnp.sum(expd, axis=0, keepdims=True)
-            probs_b = probs.astype(jnp.bfloat16)
-            h_scr[head * head_dim:(head + 1) * head_dim, :] = dot(values, probs_b, NN).astype(jnp.bfloat16)
-            d_p = dot(values, d_o, TN)
-            d_s = (probs * (d_p - jnp.sum(d_p * probs, axis=0, keepdims=True)) * scale).astype(jnp.bfloat16)
-            d_scr[at:at + head_dim, :] = dot(keys, d_s, NN).astype(jnp.bfloat16)
-            d_scr[at + head_dim:at + 2 * head_dim, :] = dot(query, d_s, NT).astype(jnp.bfloat16)
-            d_scr[at + 2 * head_dim:at + 3 * head_dim, :] = dot(d_o, probs_b, NT).astype(jnp.bfloat16)
+            attend(head, qkv, d_attn, allowed)
 
         @pl.when(pick(step, [int(SLOT[n] in SLOT[:n]) for n in range(steps)]) == 1)
         def _():
             for copy in slot_sends(slot):
                 copy.wait()
 
-        for h in range(0, hidden, cols_step):
+        for h in tiles:
             cols = slice(h, h + cols_step)
             stage[slot, 0, :, cols] = dot(h_scr[...], w_out[:, cols], TN).astype(jnp.bfloat16)
             stage[slot, 1, :, cols] = dot(d_scr[...], w_in[:, cols], TN).astype(jnp.bfloat16)
-            acc_in[:, cols] += dot(d_scr[...], a_scr[:, cols], NN)
-            acc_out[:, cols] += dot(h_scr[...], dy_buf[buf, :, cols], NN)
-
-        for n in range(steps):
-            @pl.when(step == n)
-            def _():
-                if n == steps - 1:
-                    for copy in grad_copies():
-                        copy.start()
-                for work in EVENTS[n]:
-                    event(*work)
+
+        def pass_on(when):
+            for n in range(steps - 1):
+                if EVENTS[n][when]:
+                    @pl.when(step == n)
+                    def _():
+                        for work in EVENTS[n][when]:
+                            event(*work)
+
+        pass_on(0)
+        for h in tiles:
+            grad_cols(buf, h)
+        pass_on(1)
         return carry
 
     lax.fori_loop(0, steps, row_step, 0)
     last, buf = SLOT[-1], (steps - 1) % 2
+    for copy in grad_copies():
+        copy.start()
+    dgain_ref[...] = jnp.zeros_like(dgain_ref)
+    fine = min(mid, 32)
+
+    def finish(piece):
+        def tile(n, d_gain):
+            at = pl.ds(pl.multiple_of(piece * mid + n * fine, fine), fine)
+            x_f32 = x_buf[buf, at, :].astype(jnp.float32)
+            normed, inv_std = norm_rows(x_f32)
+            grad = stage[last, 1, at, :].astype(jnp.float32)
+            stage[last, 0, at, :] = (x_f32 + stage[last, 0, at, :].astype(jnp.float32)).astype(jnp.bfloat16)
+            d_hat = grad * gain
+            d_x = inv_std * (d_hat - jnp.mean(d_hat, axis=-1, keepdims=True) - normed * jnp.mean(d_hat * normed, axis=-1, keepdims=True))
+            stage[last, 1, at, :] = (dy_buf[buf, at, :].astype(jnp.float32) + d_x).astype(jnp.bfloat16)
+            return d_gain + jnp.sum(grad * normed, axis=0, keepdims=True)
+
+        dgain_ref[...] += lax.fori_loop(0, mid // fine, tile, jnp.zeros((1, hidden), jnp.float32))
+        for t, dst in ((0, y_own), (1, dx_own)):
+            ends.append(pltpu.make_async_copy(piece_of(stage.at[last, t], piece), piece_of(dst, piece), tmp_sem.at[piece, t]))
+            ends[-1].start()
+
+    ends = []
+    ended = {0: 0, 1: 0}
+    for work in EVENTS[-1][1]:
+        event(*work)
+        n, _, piece, ring = work
+        if n == steps - 1 and ring == 2:
+            ended[piece] += 1
+            if ended[piece] == 2:
+                finish(piece)
     for slot in range(SLOTS):
         if slot != last:
             for copy in slot_sends(slot):
                 copy.wait()
-
-    fine = min(seq_len, 32)
-
-    def finish(n, d_gain):
-        at = pl.ds(pl.multiple_of(n * fine, fine), fine)
-        x_f32 = x_buf[buf, at, :].astype(jnp.float32)
-        normed, inv_std = norm_rows(x_f32)
-        grad = stage[last, 1, at, :].astype(jnp.float32)
-        stage[last, 0, at, :] = (x_f32 + stage[last, 0, at, :].astype(jnp.float32)).astype(jnp.bfloat16)
-        d_hat = grad * gain
-        d_x = inv_std * (d_hat - jnp.mean(d_hat, axis=-1, keepdims=True) - normed * jnp.mean(d_hat * normed, axis=-1, keepdims=True))
-        stage[last, 1, at, :] = (dy_buf[buf, at, :].astype(jnp.float32) + d_x).astype(jnp.bfloat16)
-        return d_gain + jnp.sum(grad * normed, axis=0, keepdims=True)
-
-    dgain_ref[...] = lax.fori_loop(0, seq_len // fine, finish, jnp.zeros((1, hidden), jnp.float32))
-    ends = [pltpu.make_async_copy(stage.at[last, t], dst, tmp_sem.at[0, t]) for t, dst in ((0, y_own), (1, dx_own))]
-    for copy in ends:
-        copy.start()
     for copy in ends + grad_copies():
         copy.wait()
 
@@ -386,7 +424,7 @@
         total = gain_scr[n, 0]
         for m in range(1, len(offsets) + 1):
             total = total + gain_scr[n, m]
-    dgain_out[...] = total.astype(dgain_out.dtype)
+    dgain_out[...] = jnp.sum(total, axis=0).astype(dgain_out.dtype)
 
     tile, turn = g_buf.shape[1], t_buf.shape[2]
     n_up = d_up.shape[1]
@@ -431,7 +469,7 @@
         if n == 2:
             g_copy.wait()
         if n >= 2:
-            for job in jobs[(n - 2) * len(jobs) // (rounds - 2):(n - 1) * len(jobs) // (rounds - 2)]:
+            for job in jobs[2 * (n - 2):2 * (n - 1)]:
                 job()
 
     for t in range(2):
@@ -444,7 +482,7 @@
         copy.wait()
 
 
-def place_kernel(y_lo, y_hi, dx_all, grads, d_up, y_out, dx_out, d_wqkv, d_wout, d_wdown, d_wup, bounce, in_sem, out_sem, sem):
+def place_kernel(y_lo, y_hi, dx_all, grads, d_up, dgain, y_out, dx_out, d_wqkv, d_wout, d_wdown, d_wup, dgain_out, bounce, in_sem, out_sem, sem):
     rows, mid, _ = y_lo.shape
     n_qkv, n_o, n_dn = d_wqkv.shape[0], d_wout.shape[0], d_wdown.shape[0]
     bufs, per = bounce.shape[0], bounce.shape[1]
@@ -458,6 +496,7 @@
     copies = [pltpu.make_async_copy(src, dst, sem.at[n]) for n, (src, dst) in enumerate(direct)]
     for copy in copies:
         copy.start()
+    dgain_out[...] = dgain[...]
     for n in range(count):
         loads[n].wait()
         stores[n].start()
@@ -486,6 +525,7 @@
         dma = pltpu.SemaphoreType.DMA
         shape = jax.ShapeDtypeStruct
         mid = seq_len // 2
+        fixed = lambda array: pltpu.with_memory_space_constraint(array, pltpu.VMEM)
         y_own, dx_own, d_gain, g_own, g_sib, _ = pl.pallas_call(
             reduce_kernel,
             in_specs=[anywhere, anywhere, vmem, vmem] + [anywhere] * 4,
@@ -508,7 +548,7 @@
             ],
             compiler_params=pltpu.CompilerParams(collective_id=0, has_side_effects=True, vmem_limit_bytes=VMEM_LIMIT),
             name="rows_reduce",
-        )(x_in, dy_in, seg_ids, ln_gain.reshape(1, hidden), wqkv, w_up, wo, w_down)
+        )(x_in, dy_in, seg_ids, ln_gain, wqkv, w_up, wo, w_down)
 
         per_link = RING * RING - 1
         y_lo, y_hi, dx_all, _, d_gain, grads, d_up = pl.pallas_call(
@@ -516,7 +556,7 @@
             in_specs=[anywhere, anywhere, vmem, anywhere, anywhere],
             out_specs=[vmem, anywhere, vmem, anywhere, vmem, vmem, vmem],
             out_shape=[pltpu.VMEM((rows, mid, hidden), bf16), shape((rows, mid, hidden), bf16), pltpu.VMEM((rows, seq_len, hidden), bf16),
-                       shape(g_sib.shape, f32), shape((1, hidden), bf16),
+                       shape(g_sib.shape, f32), pltpu.VMEM((hidden,), bf16),
                        pltpu.VMEM((n_qkv + n_out, hidden), bf16), pltpu.VMEM((hidden, n_up), bf16)],
             scratch_shapes=[
                 pltpu.VMEM((3, RING, 1, hidden), f32), pltpu.VMEM((2, n_o, hidden), f32), pltpu.VMEM((2, n_up, min(hidden, 256)), f32),
@@ -528,19 +568,18 @@
         )(y_own, dx_own, d_gain, g_own, g_sib)
 
         bufs = 4
-        fixed = lambda array: pltpu.with_memory_space_constraint(array, pltpu.VMEM)
-        y_out, dx_out, d_wqkv, d_wout, d_wdown, d_wup = pl.pallas_call(
+        y_out, dx_out, d_wqkv, d_wout, d_wdown, d_wup, d_gain = pl.pallas_call(
             place_kernel,
-            in_specs=[vmem, anywhere, vmem, vmem, vmem],
-            out_specs=[anywhere] * 6,
+            in_specs=[vmem, anywhere, vmem, vmem, vmem, vmem],
+            out_specs=[anywhere] * 6 + [vmem],
             out_shape=[shape(x_in.shape, bf16), shape(x_in.shape, bf16), shape(wqkv.shape, bf16), shape(wo.shape, bf16),
-                       shape(w_down.shape, bf16), shape(w_up.shape, bf16)],
+                       shape(w_down.shape, bf16), shape(w_up.shape, bf16), shape((hidden,), bf16)],
             scratch_shapes=[pltpu.VMEM((bufs, 2, mid, hidden), bf16), dma((bufs,)), dma((bufs,)), dma((6,))],
             compiler_params=pltpu.CompilerParams(vmem_limit_bytes=6 * 2 ** 20),
             name="rows_place",
-        )(fixed(y_lo), pltpu.with_memory_space_constraint(y_hi, pltpu.HBM), fixed(dx_all), fixed(grads), fixed(d_up))
+        )(fixed(y_lo), pltpu.with_memory_space_constraint(y_hi, pltpu.HBM), fixed(dx_all), fixed(grads), fixed(d_up), fixed(d_gain))
         d_wqkv = d_wqkv.reshape(w_qkv.shape[1:] + (hidden,)).transpose(3, 0, 1, 2)
-        return y_out, dx_out, d_gain.reshape(hidden), d_wqkv, d_wout.reshape(w_out.shape), d_wup, d_wdown
+        return y_out, dx_out, d_gain, d_wqkv, d_wout.reshape(w_out.shape), d_wup, d_wdown
 
     in_specs = (P('data'), P('data'), P(), P(None, 'model'), P('model'), P(None, 'model'), P('model'), P('data'))
     out_specs = (P('data'), P('data'), P('data'), P('data', 'model'), P(('data', 'model')), P('data', 'model'), P(('data', 'model')))

time: 420 us -> 415 us (0.988)
  no operation moved by 1% of the time
where the time goes in v4:
time: 415 us; the launch traced here: 414 us
  Pallas kernels  413 us (100%)
    pallas_call x1, Pallas kernels, body(): pl.pallas_call(reduce_kernel, in_specs=[anywhere, anywhere, vmem, vmem] +...  200 us
    pallas_call x1, Pallas kernels, body(): pl.pallas_call(gather_kernel, in_specs=[anywhere, anywhere, vmem, anywher...  184 us
    pallas_call x1, Pallas kernels, body(): pl.pallas_call(place_kernel, in_specs=[vmem, anywhere, vmem, vmem, vmem,...  29.4 us

profile of v4, /device:TPU:97, one launch (start us, length us, event | category | flops | bytes accessed | tf_op | source)
XLA Modules:
  0.0 414.1 jit_solution(6813117661378658302)
XLA Ops:
  0.6 200.0 %rows_reduce.1 = (bf16[256,2048]{1,0:T(8,128)(2,1)}, bf16[256,2048]{1,0:T(8,128)(2,1)}, f32[1,2048]{1,0:T(1,128)}, f32[768,2048]{1,0:T(8,128)}, f32[768,2048]{1,...) custom-call(bf16[32,256,2048]{2,1,0:T(8,128)(2,1)} %x_hbm.1, bf16[32,256,2048]{2,1,0:T(8,128)(2,1)} %dy_hbm.1, ...), custom_call_target="tpu_custom_call" | custom-call | tf_op jit(solution)/shard_map/rows_reduce/pallas_call | solution.py:529
  200.6 183.9 %rows_gather.1 = (bf16[32,128,2048]{2,1,0:T(8,128)(2,1)S(1)}, bf16[32,128,2048]{2,1,0:T(8,128)(2,1)}, bf16[32,256,2048]{2,1,0:T(8,128)(2,1)S(1)}, f32[768,2048]{...) custom-call(bf16[256,2048]{1,0:T(8,128)(2,1)} %get-tuple-element.25.y_own, ...), custom_call_target="tpu_custom_call" | custom-call | tf_op jit(solution)/shard_map/rows_gather/pallas_call | solution.py:554
  384.5 29.4 %rows_place.1 = (bf16[32,256,2048]{2,1,0:T(8,128)(2,1)}, bf16[32,256,2048]{2,1,0:T(8,128)(2,1)}, bf16[192,2048]{1,0:T(8,128)(2,1)}, bf16[64,2048]{1,0:T(8,128)(2...) custom-call(bf16[32,128,2048]{2,1,0:T(8,128)(2,1)S(1)} %get-tuple-element.30.y_lo, ...), custom_call_target="tpu_custom_call" | custom-call | tf_op jit(solution)/shard_map/rows_place/pallas_call | solution.py:571

commit v5 on v4

v5 whole, which is shorter than its diff:
```python
import jax
import jax.numpy as jnp
from jax import lax
from jax.experimental import pallas as pl
from jax.experimental.pallas import tpu as pltpu
from jax.sharding import PartitionSpec as P

LN_EPS = 1e-5
RING = 4
MESH = pl.DeviceIdType.MESH
NT = (((1,), (1,)), ((), ()))
NN = (((1,), (0,)), ((), ()))
TN = (((0,), (0,)), ((), ()))
ORDER = ((2, 2), (1, 2), (2, 3), (3, 2), (1, 1), (3, 3), (2, 1), (2, 0),
         (0, 2), (3, 1), (1, 3), (3, 0), (0, 3), (1, 0), (0, 1), (0, 0))
SLOT = (0, 1, 2, 3, 4, 0, 1, 3, 2, 0, 1, 4, 2, 3, 1, 0)
SLOTS = max(SLOT) + 1
EVENTS = (
    ((0, 0, 0, 1), (0, 0, 1, 1), (0, 1, 0, 1), (0, 1, 1, 1)),
    ((1, 0, 0, 1), (1, 0, 1, 1), (1, 1, 1, 1)),
    ((2, 0, 0, 1), (2, 1, 0, 1), (2, 1, 1, 1)),
    ((3, 0, 0, 1), (3, 0, 1, 1), (3, 1, 0, 1), (1, 1, 0, 1), (2, 0, 1, 1), (3, 1, 1, 1)),
    ((4, 0, 1, 1), (4, 1, 1, 1), (4, 0, 0, 1)),
    ((5, 0, 0, 1), (5, 1, 0, 1), (5, 1, 1, 1)),
    ((6, 0, 1, 1), (6, 1, 0, 1), (6, 1, 1, 1), (6, 0, 0, 1), (5, 0, 1, 1)),
    ((7, 1, 0, 1), (7, 1, 1, 1)),
    ((8, 0, 0, 1), (8, 0, 1, 1), (8, 1, 0, 1), (8, 1, 0, 2), (8, 1, 1, 1), (8, 1, 1, 2), (4, 1, 0, 1), (7, 0, 1, 1), (7, 0, 1, 2)),
    ((9, 0, 1, 1), (9, 1, 0, 1), (9, 0, 0, 1), (7, 0, 0, 1), (7, 0, 0, 2), (9, 1, 1, 1)),
    ((10, 0, 0, 1), (10, 1, 1, 1), (10, 0, 1, 1), (10, 1, 0, 1)),
    ((11, 1, 0, 1), (11, 1, 1, 1)),
    ((12, 0, 0, 1), (12, 0, 1, 1)),
    ((13, 1, 1, 1), (13, 1, 0, 1), (11, 0, 1, 1), (11, 0, 1, 2), (12, 1, 1, 1), (12, 1, 1, 2), (13, 0, 0, 1), (13, 0, 0, 2)),
    ((14, 0, 1, 1), (14, 0, 0, 1), (14, 1, 0, 1), (14, 1, 0, 2), (11, 0, 0, 1), (11, 0, 0, 2), (12, 1, 0, 1), (12, 1, 0, 2), (13, 0, 1, 1), (13, 0, 1, 2), (14, 1, 1, 1), (14, 1, 1, 2)),
    ((15, 0, 1, 1), (15, 1, 0, 1), (15, 1, 1, 1), (15, 0, 0, 1), (15, 0, 1, 2), (15, 1, 0, 2), (15, 0, 0, 2), (15, 1, 1, 2)),
)
VMEM_LIMIT = 60 * 2 ** 20
LANDING_LIMIT = 8 * 2 ** 20


def dot(lhs, rhs, dims):
    return lax.dot_general(lhs, rhs, dims, preferred_element_type=jnp.float32)


def norm_rows(x_f32):
    mean_val = jnp.mean(x_f32, axis=-1, keepdims=True)
    centered = x_f32 - mean_val
    inv_std = lax.rsqrt(jnp.mean(centered * centered, axis=-1, keepdims=True) + LN_EPS)
    return centered * inv_std, inv_std


class Place:
    def __init__(self):
        me = lax.axis_index('model')
        self.core = me % 2
        self.x = (me // 2) % RING
        self.y = me // (2 * RING)
        self.me = me

    def index(self, d_y, d_x, core=None):
        core = self.core if core is None else core
        return (((self.y + d_y) % RING) * RING + (self.x + d_x) % RING) * 2 + core

    def peer(self, axis, offset):
        return self.index(offset % RING, 0) if axis == 'y' else self.index(0, offset % RING)

    def sibling(self):
        return self.index(0, 0, 1 - self.core)


def remote(src, dst, send_sem, recv_sem, device):
    return pltpu.make_async_remote_copy(src_ref=src, dst_ref=dst, send_sem=send_sem, recv_sem=recv_sem,
                                        device_id={'model': device}, device_id_type=MESH)


def greet(peers):
    barrier = pltpu.get_barrier_semaphore()
    for peer in peers:
        pl.semaphore_signal(barrier, inc=1, device_id={'model': peer}, device_id_type=MESH)
    return barrier


def pick(step, values):
    out = jnp.int32(0)
    for n, value in enumerate(values):
        out = jnp.where(step == n, value, out)
    return out


def rows_at(ref, at, count):
    return ref.at[pl.ds(pl.multiple_of(at, 16), count)]


def landed(ref, sem):
    pltpu.make_async_copy(ref, ref, sem).wait()


def add_into(dst, *sources):
    rows = dst.shape[0]
    tile = min(rows, 32)

    def tile_add(n, carry):
        at = pl.ds(pl.multiple_of(n * tile, tile), tile)
        total = dst[at, :].astype(jnp.float32)
        for source in sources:
            total += source[at, :].astype(jnp.float32)
        dst[at, :] = total.astype(dst.dtype)
        return carry

    lax.fori_loop(0, rows // tile, tile_add, 0)


def reduce_kernel(x_hbm, dy_hbm, seg_ref, gain_ref, wqkv_hbm, w1_hbm, wo_hbm, w2_hbm,
                  y_own, dx_own, dgain_ref, a_all, hd_all,
                  w_in, w_out, w1_raw, x_buf, dy_buf, a_scr, hd_scr, stage, half, full,
                  row_sem, w_sem, ws_sem, wr_sem, send_sem, half_sem, full_sem, end_sem, save_sem):
    place = Place()
    core = place.core
    _, seq_len, hidden = x_buf.shape
    mid = seq_len // 2
    n_qkv, n_up, n_o, n_dn = wqkv_hbm.shape[0], w1_hbm.shape[1], wo_hbm.shape[0], w2_hbm.shape[0]
    n_d = 2 * (n_qkv + n_up)
    steps = len(ORDER)

    def row_of(step):
        return place.index(pick(step, [o[0] for o in ORDER]), pick(step, [o[1] for o in ORDER]))

    def row_copy(step, buf, n):
        return pltpu.make_async_copy((x_hbm, dy_hbm)[n].at[row_of(step)], (x_buf, dy_buf)[n].at[buf], row_sem.at[buf, n])

    def save(step, n):
        return pltpu.make_async_copy((a_scr, hd_scr)[n], (a_all, hd_all)[n].at[row_of(step) // 2], save_sem.at[n])

    up_spot = rows_at(w_in, 2 * n_qkv + core * n_up, n_up)
    spots = ((wqkv_hbm, rows_at(w_in, core * n_qkv, n_qkv)), (wo_hbm, rows_at(w_out, core * n_o, n_o)),
             (w2_hbm, rows_at(w_out, 2 * n_o + core * n_dn, n_dn)))

    gain = gain_ref[...].astype(jnp.float32)[None, :]
    sub = min(seq_len, 16)

    def norm_row(buf):
        for t in range(0, seq_len, sub):
            normed, _ = norm_rows(x_buf[buf, t:t + sub, :].astype(jnp.float32))
            a_scr[t:t + sub, :] = (normed * gain).astype(jnp.bfloat16)

    peers = [place.peer('x', 1), place.peer('x', -1), place.peer('y', 1), place.peer('y', -1), place.sibling()]
    barrier = greet(peers)
    raw = pltpu.make_async_copy(w1_hbm, w1_raw, w_sem.at[3])
    raw.start()
    for n in range(2):
        row_copy(0, 0, n).start()
    mine = [pltpu.make_async_copy(src, dst, w_sem.at[n]) for n, (src, dst) in enumerate(spots)]
    for copy in mine:
        copy.start()
    raw.wait()
    turn = min(hidden, 256)
    for h in range(0, hidden, turn):
        up_spot[:, h:h + turn] = w1_raw[h:h + turn, :].T
    pl.semaphore_wait(barrier, len(peers))
    swaps = [remote(src, dst, ws_sem.at[n], wr_sem.at[n], place.sibling()) for n, (src, dst) in enumerate(spots)]
    swaps.append(remote(up_spot, up_spot, ws_sem.at[3], wr_sem.at[3], place.sibling()))
    for n in (0, 3, 1, 2):
        swaps[n].start()
    row_copy(0, 0, 0).wait()
    norm_row(0)
    mine[0].wait()
    for n in (0, 3):
        swaps[n].wait()

    scale = n_o ** -0.5
    cols_step = min(hidden, 512)

    def piece_of(ref, piece):
        return ref.at[pl.ds(piece * mid, mid)]

    def slot_sends(slot):
        return [pltpu.make_async_copy(piece_of(stage.at[slot, t], piece), piece_of(stage.at[slot, t], piece),
                                      send_sem.at[slot, t, piece]) for t in range(2) for piece in range(2)]

    def event(n, t, piece, ring):
        d_y, d_x = ORDER[n]
        first, second = (('x', d_x), ('y', d_y)) if t == 0 else (('y', d_y), ('x', d_x))
        (axis, offset), line = (first, second[1]) if ring == 1 else (second, RING)
        ahead, behind = place.peer(axis, 1), place.peer(axis, -1)
        spot = piece_of(stage.at[SLOT[n], t], piece)

        def send(dst, recv_sem, device):
            remote(spot, dst, send_sem.at[SLOT[n], t, piece], recv_sem, device).start()

        if offset == 2:
            send(half.at[t, line, piece], half_sem.at[t, line, piece], ahead if piece == 0 else behind)
        elif offset in (1, 3):
            side = 0 if offset == 1 else 1
            if side == piece:
                landed(half.at[t, line, piece], half_sem.at[t, line, piece])
                add_into(spot, half.at[t, line, piece])
            send(piece_of(full.at[t, line, side], piece), full_sem.at[t, line, side, piece], ahead if side == 0 else behind)
        else:
            came = [piece_of(full.at[t, line, side], piece) for side in range(2)]
            for side in range(2):
                landed(came[side], full_sem.at[t, line, side, piece])
            add_into(spot, *came)

    def attend(head, qkv, d_attn, allowed):
        at = head * n_qkv
        query, keys, values = qkv[at:at + n_o], qkv[at + n_o:at + 2 * n_o], qkv[at + 2 * n_o:at + 3 * n_o]
        d_o = d_attn[head * n_o:(head + 1) * n_o]
        scores = jnp.where(allowed, dot(keys, query, TN) * scale, -1e30)
        expd = jnp.exp(scores - jnp.max(scores, axis=0, keepdims=True))
        probs = expd / jnp.sum(expd, axis=0, keepdims=True)
        probs_b = probs.astype(jnp.bfloat16)
        hd_scr[n_d + head * n_o:n_d + (head + 1) * n_o, :] = dot(values, probs_b, NN).astype(jnp.bfloat16)
        d_p = dot(values, d_o, TN)
        d_s = (probs * (d_p - jnp.sum(d_p * probs, axis=0, keepdims=True)) * scale).astype(jnp.bfloat16)
        hd_scr[at:at + n_o, :] = dot(keys, d_s, NN).astype(jnp.bfloat16)
        hd_scr[at + n_o:at + 2 * n_o, :] = dot(query, d_s, NT).astype(jnp.bfloat16)
        hd_scr[at + 2 * n_o:at + 3 * n_o, :] = dot(d_o, probs_b, NT).astype(jnp.bfloat16)

    def row_step(step, carry):
        buf = step % 2
        slot = pick(step, SLOT)

        @pl.when(step > 0)
        def _():
            for n in range(2):
                save(step - 1, n).wait()
            row_copy(step, buf, 0).wait()
            norm_row(buf)

        row_copy(step, buf, 1).wait()
        save(step, 0).start()

        @pl.when(step + 1 < steps)
        def _():
            for n in range(2):
                row_copy(step + 1, 1 - buf, n).start()

        @pl.when(step == 0)
        def _():
            for copy in mine[1:] + swaps[1:3]:
                copy.wait()

        proj = dot(w_in[...], a_scr[...], NT)
        d_proj = dot(w_out[...], dy_buf[buf], NT).astype(jnp.bfloat16)
        qkv = proj[:2 * n_qkv].astype(jnp.bfloat16)
        up = proj[2 * n_qkv:].astype(jnp.bfloat16).astype(jnp.float32)
        d_attn = d_proj[:2 * n_o]
        d_hid = d_proj[2 * n_o:].astype(jnp.float32)
        cdf = 0.5 * (1.0 + lax.erf(up * (0.5 ** 0.5)))
        hd_scr[n_d + 2 * n_o:, :] = (up * cdf).astype(jnp.bfloat16)
        slope = cdf + up * (jnp.exp(-0.5 * up * up) * 0.3989422804014327)
        hd_scr[2 * n_qkv:n_d, :] = (d_hid * slope).astype(jnp.bfloat16)

        seg_row = seg_ref[pl.ds(row_of(step), 1), :]
        classes = lax.broadcasted_iota(jnp.int32, (16, seq_len), 0)
        one_hot = (classes == jnp.broadcast_to(seg_row, (16, seq_len))).astype(jnp.bfloat16)
        same = dot(one_hot, one_hot, TN) > 0.5
        key_id = lax.broadcasted_iota(jnp.int32, (seq_len, seq_len), 0)
        query_id = lax.broadcasted_iota(jnp.int32, (seq_len, seq_len), 1)
        allowed = (key_id <= query_id) & same
        for head in range(2):
            attend(head, qkv, d_attn, allowed)
        save(step, 1).start()

        @pl.when(pick(step, [int(SLOT[n] in SLOT[:n]) for n in range(steps)]) == 1)
        def _():
            for copy in slot_sends(slot):
                copy.wait()

        for h in range(0, hidden, cols_step):
            cols = slice(h, h + cols_step)
            stage[slot, 0, :, cols] = dot(hd_scr[n_d:, :], w_out[:, cols], TN).astype(jnp.bfloat16)
            stage[slot, 1, :, cols] = dot(hd_scr[:n_d, :], w_in[:, cols], TN).astype(jnp.bfloat16)

        for n in range(steps - 1):
            @pl.when(step == n)
            def _():
                for work in EVENTS[n]:
                    event(*work)
        return carry

    lax.fori_loop(0, steps, row_step, 0)
    last, buf = SLOT[-1], (steps - 1) % 2
    dgain_ref[...] = jnp.zeros_like(dgain_ref)
    fine = min(mid, 32)

    def finish(piece):
        def tile(n, d_gain):
            at = pl.ds(pl.multiple_of(piece * mid + n * fine, fine), fine)
            x_f32 = x_buf[buf, at, :].astype(jnp.float32)
            normed, inv_std = norm_rows(x_f32)
            grad = stage[last, 1, at, :].astype(jnp.float32)
            stage[last, 0, at, :] = (x_f32 + stage[last, 0, at, :].astype(jnp.float32)).astype(jnp.bfloat16)
            d_hat = grad * gain
            d_x = inv_std * (d_hat - jnp.mean(d_hat, axis=-1, keepdims=True) - normed * jnp.mean(d_hat * normed, axis=-1, keepdims=True))
            stage[last, 1, at, :] = (dy_buf[buf, at, :].astype(jnp.float32) + d_x).astype(jnp.bfloat16)
            return d_gain + jnp.sum(grad * normed, axis=0, keepdims=True)

        dgain_ref[...] += lax.fori_loop(0, mid // fine, tile, jnp.zeros((1, hidden), jnp.float32))
        copies = [pltpu.make_async_copy(piece_of(stage.at[last, t], piece), piece_of(dst, piece), end_sem.at[piece, t])
                  for t, dst in ((0, y_own), (1, dx_own))]
        for copy in copies:
            copy.start()
        return copies

    ends = []
    ended = {0: 0, 1: 0}
    for work in EVENTS[-1]:
        event(*work)
        n, _, piece, ring = work
        if n == steps - 1 and ring == 2:
            ended[piece] += 1
            if ended[piece] == 2:
                ends += finish(piece)
    for slot in range(SLOTS):
        if slot != last:
            for copy in slot_sends(slot):
                copy.wait()
    for copy in ends + [save(steps - 1, n) for n in range(2)]:
        copy.wait()


def gather_kernel(n_parts, y_own, dx_own, dgain_ref, dy_hbm, a_all, hd_all, y_lo, y_hi, dx_all, dgain_out, grads, d_up,
                  gain_scr, acc, g_recv, a_buf, dy_buf, hd_buf, send_sem, link_sem, pair_sem, pair_recv, own_sem,
                  load_sem, g_send, g_land, dg_send, dg_recv):
    place = Place()
    core = place.core
    _, seq_len, hidden = dx_all.shape
    mid = seq_len // 2
    links = (('x', 1), ('x', -1), ('y', 1), ('y', -1))
    peers = [place.peer(a, o) for a in ('x', 'y') for o in (1, 2, 3)] + [place.sibling()]
    pl.semaphore_wait(greet(peers), len(peers))

    issued = {link: [] for link in links}
    sends = []

    def row_index(t, d_1, d_2):
        return place.index(d_1 % RING, d_2 % RING) if t == 0 else place.index(d_2 % RING, d_1 % RING)

    def spot_of(t, row, piece):
        if t == 1:
            return dx_all.at[row, pl.ds(piece * mid, mid)]
        return (y_lo, y_hi)[piece].at[row]

    def source(t, d_1, d_2, piece):
        if (d_1, d_2) == (0, 0):
            return (y_own, dx_own)[t].at[pl.ds(piece * mid, mid)]
        return spot_of(t, row_index(t, d_1, d_2), piece)

    def issue(link, t, d_1, d_2, piece):
        n = len(issued[link])
        which = links.index(link)
        copy = remote(source(t, d_1, d_2, piece), spot_of(t, row_index(t, d_1, d_2), piece),
                      send_sem.at[which, n], link_sem.at[which, n], place.peer(*link))
        copy.start()
        sends.append(copy)
        issued[link].append((t, d_1, d_2, piece))

    def pair(t, d_1, d_2, piece):
        slot = ((d_1 % RING) * RING + d_2 % RING) * 2 + piece
        copy = remote(source(t, d_1, d_2, piece), spot_of(t, row_index(t, d_1, d_2), piece),
                      pair_sem.at[t, slot], pair_recv.at[t, piece], place.sibling())
        copy.start()
        sends.append(copy)

    axes = (('y', 'x'), ('x', 'y'))
    for ring in range(2):
        for piece in range(2):
            for t in range(2):
                for way in (1, -1):
                    issue((axes[t][ring], way), t, 0, 0, piece)
    locals_ = []
    for t in range(2):
        for piece in range(2):
            pair(t, 0, 0, piece)
            copy = pltpu.make_async_copy(source(t, 0, 0, piece), spot_of(t, place.me, piece), own_sem.at[t, piece])
            copy.start()
            locals_.append(copy)

    depth, _, group = a_buf.shape
    rows = a_all.shape[0]
    n_qkv, n_up, n_o, n_dn = n_parts
    n_d = 2 * (n_qkv + n_up)
    segments, at, to = [], 0, 0
    for size in n_parts:
        segments.append((at, to, size))
        at, to = at + 2 * size, to + size

    def loads(r, h):
        slot = r % depth
        cols = pl.ds(h, group)
        return (pltpu.make_async_copy(a_all.at[r, :, cols], a_buf.at[slot], load_sem.at[slot, 0]),
                pltpu.make_async_copy(dy_hbm.at[2 * r + core, :, cols], dy_buf.at[slot], load_sem.at[slot, 1]),
                pltpu.make_async_copy(hd_all.at[r], hd_buf.at[slot], load_sem.at[slot, 2]))

    def swap_grads(n):
        return [remote(rows_at(acc, at + (1 - core) * size, size), g_recv.at[n % 2, pl.ds(to, size)],
                       g_send.at[m], g_land.at[n % 2, m], place.sibling()) for m, (at, to, size) in enumerate(segments)]

    def sum_rows(n):
        h = n * group
        acc[...] = jnp.zeros_like(acc)
        for r in range(depth - 1):
            for copy in loads(r, h):
                copy.start()

        def add_row(r, carry):
            slot = r % depth
            for copy in loads(r, h):
                copy.wait()

            @pl.when(r + depth - 1 < rows)
            def _():
                for copy in loads(r + depth - 1, h):
                    copy.start()

            acc[:n_d, :] += dot(hd_buf[slot, :n_d, :], a_buf[slot], NN)
            acc[n_d:, :] += dot(hd_buf[slot, n_d:, :], dy_buf[slot], NN)
            return carry

        lax.fori_loop(0, rows, add_row, 0)
        for copy in swap_grads(n):
            copy.start()

    def end_rows(n):
        for copy in swap_grads(n):
            copy.wait()
        for m, (at, to, size) in enumerate(segments):
            total = rows_at(acc, at + core * size, size)[...] + g_recv[n % 2, to:to + size, :]
            if m == 1:
                d_up[n * group:(n + 1) * group, :] = total.T.astype(d_up.dtype)
            else:
                spot = to if m == 0 else to - n_up
                grads[spot:spot + size, n * group:(n + 1) * group] = total.astype(grads.dtype)

    total = dgain_ref[...]
    for n, (axis, offsets) in enumerate((('core', (1,)), ('x', (1, 2, 3)), ('y', (1, 2, 3)))):
        spot = {'core': core, 'x': place.x, 'y': place.y}[axis]
        gain_scr[n, spot] = total
        copies = []
        for m, offset in enumerate(offsets):
            device = place.sibling() if axis == 'core' else place.peer(axis, offset)
            copies.append(remote(gain_scr.at[n, spot], gain_scr.at[n, spot], dg_send.at[n, m], dg_recv.at[n, m], device))
        for copy in copies:
            copy.start()
        for copy in copies:
            copy.wait()
        total = gain_scr[n, 0]
        for m in range(1, len(offsets) + 1):
            total = total + gain_scr[n, m]
    dgain_out[...] = jnp.sum(total, axis=0).astype(dgain_out.dtype)

    groups = hidden // group
    rounds = RING * RING - 1
    assert groups <= rounds
    for n in range(rounds):
        if n < groups:
            sum_rows(n)
        for link in links:
            t, d_1, d_2, piece = issued[link][n]
            axis, way = link
            on_first = axis == axes[t][0]
            d_1, d_2 = (d_1 - way, d_2) if on_first else (d_1, d_2 - way)
            landed(spot_of(t, row_index(t, d_1, d_2), piece), link_sem.at[links.index(link), n])
            along = d_1 if on_first else d_2
            if abs(along) == 1 and piece == (0 if way == 1 else 1):
                issue(link, t, d_1, d_2, piece)
            if on_first:
                for other in (1, -1):
                    issue((axes[t][1], other), t, d_1, d_2, piece)
            pair(t, d_1, d_2, piece)
        if n < groups:
            end_rows(n)

    for t in range(2):
        for piece in range(2):
            theirs = dx_all.at[pl.ds(0, RING * RING), pl.ds(piece * mid, mid)] if t else (y_lo, y_hi)[piece].at[pl.ds(0, RING * RING)]
            landed(theirs, pair_recv.at[t, piece])
    for copy in sends:
        copy.wait_send()
    for copy in locals_:
        copy.wait()


def place_kernel(y_lo, y_hi, dx_all, grads, d_up, dgain, y_out, dx_out, d_wqkv, d_wout, d_wdown, d_wup, dgain_out, bounce, in_sem, out_sem, sem):
    rows, mid, _ = y_lo.shape
    n_qkv, n_o, n_dn = d_wqkv.shape[0], d_wout.shape[0], d_wdown.shape[0]
    bufs, per = bounce.shape[0], bounce.shape[1]
    count = rows // per
    loads = [pltpu.make_async_copy(y_hi.at[pl.ds(n * per, per)], bounce.at[n % bufs], in_sem.at[n % bufs]) for n in range(count)]
    stores = [pltpu.make_async_copy(bounce.at[n % bufs], y_out.at[pl.ds(n * per, per), pl.ds(mid, mid)], out_sem.at[n % bufs]) for n in range(count)]
    for n in range(min(bufs, count)):
        loads[n].start()
    direct = [(y_lo, y_out.at[:, pl.ds(0, mid)]), (dx_all, dx_out), (grads.at[pl.ds(0, n_qkv)], d_wqkv),
              (grads.at[pl.ds(n_qkv, n_o)], d_wout), (grads.at[pl.ds(n_qkv + n_o, n_dn)], d_wdown), (d_up, d_wup)]
    copies = [pltpu.make_async_copy(src, dst, sem.at[n]) for n, (src, dst) in enumerate(direct)]
    for copy in copies:
        copy.start()
    dgain_out[...] = dgain[...]
    for n in range(count):
        loads[n].wait()
        stores[n].start()
        if n >= 1 and n - 1 + bufs < count:
            stores[n - 1].wait()
            loads[n - 1 + bufs].start()
    for n in range(max(0, count - bufs), count):
        stores[n].wait()
    for copy in copies:
        copy.wait()


def solution(mesh):
    devices = mesh.shape['model']
    assert devices == 2 * RING * RING

    def body(x_in, seg_ids, ln_gain, w_qkv, w_out, w_up, w_down, dy_in):
        rows, seq_len, hidden = x_in.shape
        assert rows == devices
        wqkv = w_qkv.transpose(1, 2, 3, 0).reshape(-1, hidden)
        wo = w_out.reshape(-1, hidden)
        n_parts = (wqkv.shape[0], w_up.shape[1], wo.shape[0], w_down.shape[0])
        n_in, n_out = n_parts[0] + n_parts[1], n_parts[2] + n_parts[3]
        n_all, n_up = n_in + n_out, n_parts[1]
        bf16, f32 = jnp.bfloat16, jnp.float32
        vmem, anywhere = pl.BlockSpec(memory_space=pltpu.VMEM), pl.BlockSpec(memory_space=pl.ANY)
        dma = pltpu.SemaphoreType.DMA
        shape = jax.ShapeDtypeStruct
        chips, mid, group = RING * RING, seq_len // 2, hidden // 8
        fixed = lambda array: pltpu.with_memory_space_constraint(array, pltpu.VMEM)
        y_own, dx_own, d_gain, a_all, hd_all = pl.pallas_call(
            reduce_kernel,
            in_specs=[anywhere, anywhere, vmem, vmem] + [anywhere] * 4,
            out_specs=[anywhere, anywhere, vmem, anywhere, anywhere],
            out_shape=[shape((seq_len, hidden), bf16), shape((seq_len, hidden), bf16), shape((1, hidden), f32),
                       shape((chips, seq_len, hidden), bf16), shape((chips, 2 * n_all, seq_len), bf16)],
            scratch_shapes=[
                pltpu.VMEM((2 * n_in, hidden), bf16), pltpu.VMEM((2 * n_out, hidden), bf16), pltpu.VMEM((hidden, n_up), bf16),
                pltpu.VMEM((2, seq_len, hidden), bf16), pltpu.VMEM((2, seq_len, hidden), bf16),
                pltpu.VMEM((seq_len, hidden), bf16), pltpu.VMEM((2 * n_all, seq_len), bf16),
                pltpu.VMEM((SLOTS, 2, seq_len, hidden), bf16),
                pltpu.VMEM((2, RING + 1, 2, mid, hidden), bf16),
                pltpu.VMEM((2, RING + 1, 2, seq_len, hidden), bf16),
                dma((2, 2)), dma((4,)), dma((4,)), dma((4,)), dma((SLOTS, 2, 2)),
                dma((2, RING + 1, 2)), dma((2, RING + 1, 2, 2)), dma((2, 2)), dma((2,)),
            ],
            compiler_params=pltpu.CompilerParams(collective_id=0, has_side_effects=True, vmem_limit_bytes=VMEM_LIMIT),
            name="rows_reduce",
        )(x_in, dy_in, seg_ids, ln_gain, wqkv, w_up, wo, w_down)

        per_link, depth = chips - 1, 4
        y_lo, y_hi, dx_all, d_gain, grads, d_up = pl.pallas_call(
            lambda *refs: gather_kernel(n_parts, *refs),
            in_specs=[anywhere, anywhere, vmem, anywhere, anywhere, anywhere],
            out_specs=[vmem, anywhere, vmem, vmem, vmem, vmem],
            out_shape=[pltpu.VMEM((rows, mid, hidden), bf16), shape((rows, mid, hidden), bf16), pltpu.VMEM((rows, seq_len, hidden), bf16),
                       pltpu.VMEM((hidden,), bf16), pltpu.VMEM((n_all - n_up, hidden), bf16), pltpu.VMEM((hidden, n_up), bf16)],
            scratch_shapes=[
                pltpu.VMEM((3, RING, 1, hidden), f32), pltpu.VMEM((2 * n_all, group), f32), pltpu.VMEM((2, n_all, group), f32),
                pltpu.VMEM((depth, seq_len, group), bf16), pltpu.VMEM((depth, seq_len, group), bf16), pltpu.VMEM((depth, 2 * n_all, seq_len), bf16),
                dma((4, per_link)), dma((4, per_link)), dma((2, 2 * chips)), dma((2, 2)), dma((2, 2)),
                dma((depth, 3)), dma((4,)), dma((2, 4)), dma((3, 3)), dma((3, 3)),
            ],
            compiler_params=pltpu.CompilerParams(collective_id=1, has_side_effects=True, vmem_limit_bytes=LANDING_LIMIT),
            name="rows_gather",
        )(y_own, dx_own, d_gain, dy_in, a_all, hd_all)

        bufs = 6
        y_out, dx_out, d_wqkv, d_wout, d_wdown, d_wup, d_gain = pl.pallas_call(
            place_kernel,
            in_specs=[vmem, anywhere, vmem, vmem, vmem, vmem],
            out_specs=[anywhere] * 6 + [vmem],
            out_shape=[shape(x_in.shape, bf16), shape(x_in.shape, bf16), shape(wqkv.shape, bf16), shape(wo.shape, bf16),
                       shape(w_down.shape, bf16), shape(w_up.shape, bf16), shape((hidden,), bf16)],
            scratch_shapes=[pltpu.VMEM((bufs, 2, mid, hidden), bf16), dma((bufs,)), dma((bufs,)), dma((6,))],
            compiler_params=pltpu.CompilerParams(vmem_limit_bytes=LANDING_LIMIT),
            name="rows_place",
        )(fixed(y_lo), pltpu.with_memory_space_constraint(y_hi, pltpu.HBM), fixed(dx_all), fixed(grads), fixed(d_up), fixed(d_gain))
        d_wqkv = d_wqkv.reshape(w_qkv.shape[1:] + (hidden,)).transpose(3, 0, 1, 2)
        return y_out, dx_out, d_gain, d_wqkv, d_wout.reshape(w_out.shape), d_wup, d_wdown

    in_specs = (P('data'), P('data'), P(), P(None, 'model'), P('model'), P(None, 'model'), P('model'), P('data'))
    out_specs = (P('data'), P('data'), P('data'), P('data', 'model'), P(('data', 'model')), P('data', 'model'), P(('data', 'model')))
    return jax.shard_map(body, mesh=mesh, in_specs=in_specs, out_specs=out_specs, check_vma=False)
```

time: 415 us -> 421 us (1.014)
  Pallas kernels: 413 us -> 419 us
    pallas_call x1, Pallas kernels: 184 us -> 194 us  [body(): pl.pallas_call(lambda *refs: gather_kernel(n_parts, *refs), in_specs=[any...]
where the time goes in v5:
time: 421 us; the launch traced here: 420 us
  Pallas kernels  419 us (100%)
    pallas_call x1, Pallas kernels, body(): pl.pallas_call(reduce_kernel, in_specs=[anywhere, anywhere, vmem, vmem] +...  196 us
    pallas_call x1, Pallas kernels, body(): pl.pallas_call(lambda *refs: gather_kernel(n_parts, *refs), in_specs=[any...  194 us
    pallas_call x1, Pallas kernels, body(): pl.pallas_call(place_kernel, in_specs=[vmem, anywhere, vmem, vmem, vmem,...  29.3 us

profile of v5, /device:TPU:97, one launch (start us, length us, event | category | flops | bytes accessed | tf_op | source)
XLA Modules:
  0.0 420.2 jit_solution(4083919008954128946)
XLA Ops:
  0.6 196.3 %rows_reduce.1 = (bf16[256,2048]{1,0:T(8,128)(2,1)}, bf16[256,2048]{1,0:T(8,128)(2,1)}, f32[1,2048]{1,0:T(1,128)}, bf16[16,256,2048]{2,1,0:T(8,128)(2,1)}, bf16[16,1536,256]{2,1,0:T(8,128)(2,1)}) custom-call(bf16[32,256,2048]{2,1,0:T(8,128)(2,1)} %x_hbm.1, bf16[32,256,2048]{2,1,0:T(8,128)(2,1)} %refs_3_.1, s32[32,256]{1,0:T(8,128)} %seg_ref.1, ...), custom_call_target="tpu_custom_call" | custom-call | tf_op jit(solution)/shard_map/rows_reduce/pallas_call | solution.py:529
  196.9 193.8 %rows_gather.1 = (bf16[32,128,2048]{2,1,0:T(8,128)(2,1)S(1)}, bf16[32,128,2048]{2,1,0:T(8,128)(2,1)}, bf16[32,256,2048]{2,1,0:T(8,128)(2,1)S(1)}, bf16[2048]{0:T...) custom-call(bf16[256,2048]{1,0:T(8,128)(2,1)} %get-tuple-element.25.refs_0_, ...), custom_call_target="tpu_custom_call" | custom-call | tf_op jit(solution)/shard_map/rows_gather/pallas_call | solution.py:550
  390.7 29.3 %rows_place.1 = (bf16[32,256,2048]{2,1,0:T(8,128)(2,1)}, bf16[32,256,2048]{2,1,0:T(8,128)(2,1)}, bf16[192,2048]{1,0:T(8,128)(2,1)}, bf16[64,2048]{1,0:T(8,128)(2...) custom-call(bf16[32,128,2048]{2,1,0:T(8,128)(2,1)S(1)} %get-tuple-element.30.y_lo, ...), custom_call_target="tpu_custom_call" | custom-call | tf_op jit(solution)/shard_map/rows_place/pallas_call | solution.py:567

commit v6 on v5

--- a/solution.py
+++ b/solution.py
@@ -327,7 +327,7 @@
     _, seq_len, hidden = dx_all.shape
     mid = seq_len // 2
     links = (('x', 1), ('x', -1), ('y', 1), ('y', -1))
-    peers = [place.peer(a, o) for a in ('x', 'y') for o in (1, 2, 3)] + [place.sibling()]
+    peers = [place.peer(a, o) for a in ('x', 'y') for o in (1, -1)] + [place.sibling()]
     pl.semaphore_wait(greet(peers), len(peers))
 
     issued = {link: [] for link in links}
@@ -364,10 +364,10 @@
 
     axes = (('y', 'x'), ('x', 'y'))
     for ring in range(2):
-        for piece in range(2):
+        for n in range(2):
             for t in range(2):
                 for way in (1, -1):
-                    issue((axes[t][ring], way), t, 0, 0, piece)
+                    issue((axes[t][ring], way), t, 0, 0, n if way == 1 else 1 - n)
     locals_ = []
     for t in range(2):
         for piece in range(2):
@@ -376,8 +376,9 @@
             copy.start()
             locals_.append(copy)
 
-    depth, _, group = a_buf.shape
-    rows = a_all.shape[0]
+    depth, _, _, group = a_buf.shape
+    pairs = a_all.shape[0] // 2
+    groups = hidden // group
     n_qkv, n_up, n_o, n_dn = n_parts
     n_d = 2 * (n_qkv + n_up)
     segments, at, to = [], 0, 0
@@ -385,39 +386,45 @@
         segments.append((at, to, size))
         at, to = at + 2 * size, to + size
 
-    def loads(r, h):
-        slot = r % depth
-        cols = pl.ds(h, group)
-        return (pltpu.make_async_copy(a_all.at[r, :, cols], a_buf.at[slot], load_sem.at[slot, 0]),
-                pltpu.make_async_copy(dy_hbm.at[2 * r + core, :, cols], dy_buf.at[slot], load_sem.at[slot, 1]),
-                pltpu.make_async_copy(hd_all.at[r], hd_buf.at[slot], load_sem.at[slot, 2]))
+    def loads(count):
+        slot = count % depth
+        first = 2 * (count % pairs)
+        cols = pl.ds(pl.multiple_of(count // pairs * group, group), group)
+        copies = []
+        for m in range(2):
+            r = first + m
+            copies += [pltpu.make_async_copy(a_all.at[r, :, cols], a_buf.at[slot, m], load_sem.at[slot, m, 0]),
+                       pltpu.make_async_copy(dy_hbm.at[2 * r + core, :, cols], dy_buf.at[slot, m], load_sem.at[slot, m, 1]),
+                       pltpu.make_async_copy(hd_all.at[r], hd_buf.at[slot, m], load_sem.at[slot, m, 2])]
+        return copies
 
     def swap_grads(n):
         return [remote(rows_at(acc, at + (1 - core) * size, size), g_recv.at[n % 2, pl.ds(to, size)],
                        g_send.at[m], g_land.at[n % 2, m], place.sibling()) for m, (at, to, size) in enumerate(segments)]
 
+    for count in range(depth - 1):
+        for copy in loads(count):
+            copy.start()
+
     def sum_rows(n):
-        h = n * group
         acc[...] = jnp.zeros_like(acc)
-        for r in range(depth - 1):
-            for copy in loads(r, h):
-                copy.start()
-
-        def add_row(r, carry):
-            slot = r % depth
-            for copy in loads(r, h):
+
+        def add_pair(i, carry):
+            count = n * pairs + i
+            slot = count % depth
+            for copy in loads(count):
                 copy.wait()
 
-            @pl.when(r + depth - 1 < rows)
+            @pl.when(count + depth - 1 < groups * pairs)
             def _():
-                for copy in loads(r + depth - 1, h):
+                for copy in loads(count + depth - 1):
                     copy.start()
 
-            acc[:n_d, :] += dot(hd_buf[slot, :n_d, :], a_buf[slot], NN)
-            acc[n_d:, :] += dot(hd_buf[slot, n_d:, :], dy_buf[slot], NN)
+            acc[:n_d, :] += dot(hd_buf[slot, 0, :n_d, :], a_buf[slot, 0], NN) + dot(hd_buf[slot, 1, :n_d, :], a_buf[slot, 1], NN)
+            acc[n_d:, :] += dot(hd_buf[slot, 0, n_d:, :], dy_buf[slot, 0], NN) + dot(hd_buf[slot, 1, n_d:, :], dy_buf[slot, 1], NN)
             return carry
 
-        lax.fori_loop(0, rows, add_row, 0)
+        lax.fori_loop(0, pairs, add_pair, 0)
         for copy in swap_grads(n):
             copy.start()
 
@@ -433,23 +440,17 @@
                 grads[spot:spot + size, n * group:(n + 1) * group] = total.astype(grads.dtype)
 
     total = dgain_ref[...]
-    for n, (axis, offsets) in enumerate((('core', (1,)), ('x', (1, 2, 3)), ('y', (1, 2, 3)))):
-        spot = {'core': core, 'x': place.x, 'y': place.y}[axis]
-        gain_scr[n, spot] = total
-        copies = []
-        for m, offset in enumerate(offsets):
-            device = place.sibling() if axis == 'core' else place.peer(axis, offset)
-            copies.append(remote(gain_scr.at[n, spot], gain_scr.at[n, spot], dg_send.at[n, m], dg_recv.at[n, m], device))
-        for copy in copies:
-            copy.start()
-        for copy in copies:
-            copy.wait()
-        total = gain_scr[n, 0]
-        for m in range(1, len(offsets) + 1):
-            total = total + gain_scr[n, m]
+    for n, axis in enumerate(('core', 'x', 'x', 'y', 'y')):
+        at = {'core': core, 'x': place.x, 'y': place.y}[axis]
+        other = (RING - 1 - at) if n in (2, 4) else at + 1 - 2 * (at % 2)
+        device = place.sibling() if axis == 'core' else place.peer(axis, other - at)
+        gain_scr[n, 0] = total
+        copy = remote(gain_scr.at[n, 0], gain_scr.at[n, 1], dg_send.at[n], dg_recv.at[n], device)
+        copy.start()
+        copy.wait()
+        total = gain_scr[n, 0] + gain_scr[n, 1]
     dgain_out[...] = jnp.sum(total, axis=0).astype(dgain_out.dtype)
 
-    groups = hidden // group
     rounds = RING * RING - 1
     assert groups <= rounds
     for n in range(rounds):
@@ -490,8 +491,14 @@
     stores = [pltpu.make_async_copy(bounce.at[n % bufs], y_out.at[pl.ds(n * per, per), pl.ds(mid, mid)], out_sem.at[n % bufs]) for n in range(count)]
     for n in range(min(bufs, count)):
         loads[n].start()
-    direct = [(y_lo, y_out.at[:, pl.ds(0, mid)]), (dx_all, dx_out), (grads.at[pl.ds(0, n_qkv)], d_wqkv),
-              (grads.at[pl.ds(n_qkv, n_o)], d_wout), (grads.at[pl.ds(n_qkv + n_o, n_dn)], d_wdown), (d_up, d_wup)]
+    split = 4
+    part = rows // split
+    direct = []
+    for n in range(split):
+        at = pl.ds(n * part, part)
+        direct += [(dx_all.at[at], dx_out.at[at]), (y_lo.at[at], y_out.at[at, pl.ds(0, mid)])]
+    direct += [(grads.at[pl.ds(0, n_qkv)], d_wqkv),
+               (grads.at[pl.ds(n_qkv, n_o)], d_wout), (grads.at[pl.ds(n_qkv + n_o, n_dn)], d_wdown), (d_up, d_wup)]
     copies = [pltpu.make_async_copy(src, dst, sem.at[n]) for n, (src, dst) in enumerate(direct)]
     for copy in copies:
         copy.start()
@@ -546,7 +553,7 @@
             name="rows_reduce",
         )(x_in, dy_in, seg_ids, ln_gain, wqkv, w_up, wo, w_down)
 
-        per_link, depth = chips - 1, 4
+        per_link, depth = chips - 1, 2
         y_lo, y_hi, dx_all, d_gain, grads, d_up = pl.pallas_call(
             lambda *refs: gather_kernel(n_parts, *refs),
             in_specs=[anywhere, anywhere, vmem, anywhere, anywhere, anywhere],
@@ -554,10 +561,11 @@
             out_shape=[pltpu.VMEM((rows, mid, hidden), bf16), shape((rows, mid, hidden), bf16), pltpu.VMEM((rows, seq_len, hidden), bf16),
                        pltpu.VMEM((hidden,), bf16), pltpu.VMEM((n_all - n_up, hidden), bf16), pltpu.VMEM((hidden, n_up), bf16)],
             scratch_shapes=[
-                pltpu.VMEM((3, RING, 1, hidden), f32), pltpu.VMEM((2 * n_all, group), f32), pltpu.VMEM((2, n_all, group), f32),
-                pltpu.VMEM((depth, seq_len, group), bf16), pltpu.VMEM((depth, seq_len, group), bf16), pltpu.VMEM((depth, 2 * n_all, seq_len), bf16),
+                pltpu.VMEM((5, 2, 1, hidden), f32), pltpu.VMEM((2 * n_all, group), f32), pltpu.VMEM((2, n_all, group), f32),
+                pltpu.VMEM((depth, 2, seq_len, group), bf16), pltpu.VMEM((depth, 2, seq_len, group), bf16),
+                pltpu.VMEM((depth, 2, 2 * n_all, seq_len), bf16),
                 dma((4, per_link)), dma((4, per_link)), dma((2, 2 * chips)), dma((2, 2)), dma((2, 2)),
-                dma((depth, 3)), dma((4,)), dma((2, 4)), dma((3, 3)), dma((3, 3)),
+                dma((depth, 2, 3)), dma((4,)), dma((2, 4)), dma((5,)), dma((5,)),
             ],
             compiler_params=pltpu.CompilerParams(collective_id=1, has_side_effects=True, vmem_limit_bytes=LANDING_LIMIT),
             name="rows_gather",
@@ -570,7 +578,7 @@
             out_specs=[anywhere] * 6 + [vmem],
             out_shape=[shape(x_in.shape, bf16), shape(x_in.shape, bf16), shape(wqkv.shape, bf16), shape(wo.shape, bf16),
                        shape(w_down.shape, bf16), shape(w_up.shape, bf16), shape((hidden,), bf16)],
-            scratch_shapes=[pltpu.VMEM((bufs, 2, mid, hidden), bf16), dma((bufs,)), dma((bufs,)), dma((6,))],
+            scratch_shapes=[pltpu.VMEM((bufs, 2, mid, hidden), bf16), dma((bufs,)), dma((bufs,)), dma((12,))],
             compiler_params=pltpu.CompilerParams(vmem_limit_bytes=LANDING_LIMIT),
             name="rows_place",
         )(fixed(y_lo), pltpu.with_memory_space_constraint(y_hi, pltpu.HBM), fixed(dx_all), fixed(grads), fixed(d_up), fixed(d_gain))

time: 421 us -> 447 us (1.062)
  Pallas kernels: 419 us -> 444 us
    pallas_call x1, Pallas kernels: 194 us -> 219 us  [body(): pl.pallas_call(lambda *refs: gather_kernel(n_parts, *refs), in_specs=[any...]
where the time goes in v6:
time: 447 us; the launch traced here: 445 us
  Pallas kernels  444 us (99%)
    pallas_call x1, Pallas kernels, body(): pl.pallas_call(lambda *refs: gather_kernel(n_parts, *refs), in_specs=[any...  219 us
    pallas_call x1, Pallas kernels, body(): pl.pallas_call(reduce_kernel, in_specs=[anywhere, anywhere, vmem, vmem] +...  196 us
    pallas_call x1, Pallas kernels, body(): pl.pallas_call(place_kernel, in_specs=[vmem, anywhere, vmem, vmem, vmem,...  29.2 us

profile of v6, /device:TPU:97, one launch (start us, length us, event | category | flops | bytes accessed | tf_op | source)
XLA Modules:
  0.0 445.3 jit_solution(4012139218595889757)
XLA Ops:
  0.6 196.3 %rows_reduce.1 = (bf16[256,2048]{1,0:T(8,128)(2,1)}, bf16[256,2048]{1,0:T(8,128)(2,1)}, f32[1,2048]{1,0:T(1,128)}, bf16[16,256,2048]{2,1,0:T(8,128)(2,1)}, bf16[16,1536,256]{2,1,0:T(8,128)(2,1)}) custom-call(bf16[32,256,2048]{2,1,0:T(8,128)(2,1)} %x_hbm.1, bf16[32,256,2048]{2,1,0:T(8,128)(2,1)} %refs_3_.1, s32[32,256]{1,0:T(8,128)} %seg_ref.1, ...), custom_call_target="tpu_custom_call" | custom-call | tf_op jit(solution)/shard_map/rows_reduce/pallas_call | solution.py:536
  196.9 219.0 %rows_gather.1 = (bf16[32,128,2048]{2,1,0:T(8,128)(2,1)S(1)}, bf16[32,128,2048]{2,1,0:T(8,128)(2,1)}, bf16[32,256,2048]{2,1,0:T(8,128)(2,1)S(1)}, bf16[2048]{0:T...) custom-call(bf16[256,2048]{1,0:T(8,128)(2,1)} %get-tuple-element.25.refs_0_, ...), custom_call_target="tpu_custom_call" | custom-call | tf_op jit(solution)/shard_map/rows_gather/pallas_call | solution.py:557
  415.9 29.2 %rows_place.1 = (bf16[32,256,2048]{2,1,0:T(8,128)(2,1)}, bf16[32,256,2048]{2,1,0:T(8,128)(2,1)}, bf16[192,2048]{1,0:T(8,128)(2,1)}, bf16[64,2048]{1,0:T(8,128)(2...) custom-call(bf16[32,128,2048]{2,1,0:T(8,128)(2,1)S(1)} %get-tuple-element.30.y_lo, ...), custom_call_target="tpu_custom_call" | custom-call | tf_op jit(solution)/shard_map/rows_place/pallas_call | solution.py:575

commit v7 on v6

--- a/solution.py
+++ b/solution.py
@@ -34,7 +34,7 @@
     ((15, 0, 1, 1), (15, 1, 0, 1), (15, 1, 1, 1), (15, 0, 0, 1), (15, 0, 1, 2), (15, 1, 0, 2), (15, 0, 0, 2), (15, 1, 1, 2)),
 )
 VMEM_LIMIT = 60 * 2 ** 20
-LANDING_LIMIT = 8 * 2 ** 20
+LANDING_LIMIT = 41 * 2 ** 18
 
 
 def dot(lhs, rhs, dims):
@@ -321,7 +321,7 @@
 
 def gather_kernel(n_parts, y_own, dx_own, dgain_ref, dy_hbm, a_all, hd_all, y_lo, y_hi, dx_all, dgain_out, grads, d_up,
                   gain_scr, acc, g_recv, a_buf, dy_buf, hd_buf, send_sem, link_sem, pair_sem, pair_recv, own_sem,
-                  load_sem, g_send, g_land, dg_send, dg_recv):
+                  load_sem, g_send, g_land, g_free, dg_send, dg_recv):
     place = Place()
     core = place.core
     _, seq_len, hidden = dx_all.shape
@@ -376,8 +376,8 @@
             copy.start()
             locals_.append(copy)
 
-    depth, _, _, group = a_buf.shape
-    pairs = a_all.shape[0] // 2
+    depth, _, group = a_buf.shape
+    rows = a_all.shape[0]
     groups = hidden // group
     n_qkv, n_up, n_o, n_dn = n_parts
     n_d = 2 * (n_qkv + n_up)
@@ -387,57 +387,60 @@
         at, to = at + 2 * size, to + size
 
     def loads(count):
-        slot = count % depth
-        first = 2 * (count % pairs)
-        cols = pl.ds(pl.multiple_of(count // pairs * group, group), group)
-        copies = []
-        for m in range(2):
-            r = first + m
-            copies += [pltpu.make_async_copy(a_all.at[r, :, cols], a_buf.at[slot, m], load_sem.at[slot, m, 0]),
-                       pltpu.make_async_copy(dy_hbm.at[2 * r + core, :, cols], dy_buf.at[slot, m], load_sem.at[slot, m, 1]),
-                       pltpu.make_async_copy(hd_all.at[r], hd_buf.at[slot, m], load_sem.at[slot, m, 2])]
-        return copies
+        slot, r = count % depth, count % rows
+        cols = pl.ds(pl.multiple_of(count // rows * group, group), group)
+        return (pltpu.make_async_copy(a_all.at[r, :, cols], a_buf.at[slot], load_sem.at[slot, 0]),
+                pltpu.make_async_copy(dy_hbm.at[2 * r + core, :, cols], dy_buf.at[slot], load_sem.at[slot, 1]),
+                pltpu.make_async_copy(hd_all.at[r, pl.ds(0, n_d)], hd_buf.at[slot, pl.ds(0, n_d)], load_sem.at[slot, 2]),
+                pltpu.make_async_copy(hd_all.at[r, pl.ds(n_d, hd_all.shape[1] - n_d)],
+                                      hd_buf.at[slot, pl.ds(n_d, hd_all.shape[1] - n_d)], load_sem.at[slot, 3]))
 
     def swap_grads(n):
-        return [remote(rows_at(acc, at + (1 - core) * size, size), g_recv.at[n % 2, pl.ds(to, size)],
-                       g_send.at[m], g_land.at[n % 2, m], place.sibling()) for m, (at, to, size) in enumerate(segments)]
+        return [remote(rows_at(acc, at + (1 - core) * size, size), g_recv.at[pl.ds(to, size)],
+                       g_send.at[m], g_land.at[m], place.sibling()) for m, (at, to, size) in enumerate(segments)]
 
     for count in range(depth - 1):
         for copy in loads(count):
             copy.start()
 
-    def sum_rows(n):
-        acc[...] = jnp.zeros_like(acc)
-
-        def add_pair(i, carry):
-            count = n * pairs + i
+    def sum_rows(n, half):
+        if half == 0:
+            acc[...] = jnp.zeros_like(acc)
+
+        def add_row(i, carry):
+            count = n * rows + i
             slot = count % depth
             for copy in loads(count):
                 copy.wait()
 
-            @pl.when(count + depth - 1 < groups * pairs)
+            @pl.when(count + depth - 1 < groups * rows)
             def _():
                 for copy in loads(count + depth - 1):
                     copy.start()
 
-            acc[:n_d, :] += dot(hd_buf[slot, 0, :n_d, :], a_buf[slot, 0], NN) + dot(hd_buf[slot, 1, :n_d, :], a_buf[slot, 1], NN)
-            acc[n_d:, :] += dot(hd_buf[slot, 0, n_d:, :], dy_buf[slot, 0], NN) + dot(hd_buf[slot, 1, n_d:, :], dy_buf[slot, 1], NN)
+            acc[:n_d, :] += dot(hd_buf[slot, :n_d, :], a_buf[slot], NN)
+            acc[n_d:, :] += dot(hd_buf[slot, n_d:, :], dy_buf[slot], NN)
             return carry
 
-        lax.fori_loop(0, pairs, add_pair, 0)
-        for copy in swap_grads(n):
-            copy.start()
+        lax.fori_loop(half * (rows // 2), (half + 1) * (rows // 2), add_row, 0)
+        if half == 1:
+            if n > 0:
+                pl.semaphore_wait(g_free, 1)
+            for copy in swap_grads(n):
+                copy.start()
 
     def end_rows(n):
         for copy in swap_grads(n):
             copy.wait()
         for m, (at, to, size) in enumerate(segments):
-            total = rows_at(acc, at + core * size, size)[...] + g_recv[n % 2, to:to + size, :]
+            total = rows_at(acc, at + core * size, size)[...] + g_recv[to:to + size, :]
             if m == 1:
                 d_up[n * group:(n + 1) * group, :] = total.T.astype(d_up.dtype)
             else:
                 spot = to if m == 0 else to - n_up
                 grads[spot:spot + size, n * group:(n + 1) * group] = total.astype(grads.dtype)
+        if n + 1 < groups:
+            pl.semaphore_signal(g_free, inc=1, device_id={'model': place.sibling()}, device_id_type=MESH)
 
     total = dgain_ref[...]
     for n, axis in enumerate(('core', 'x', 'x', 'y', 'y')):
@@ -452,10 +455,12 @@
     dgain_out[...] = jnp.sum(total, axis=0).astype(dgain_out.dtype)
 
     rounds = RING * RING - 1
-    assert groups <= rounds
+    assert 2 * groups < rounds
     for n in range(rounds):
-        if n < groups:
-            sum_rows(n)
+        if n > 0 and n % 2 == 0 and n <= 2 * groups:
+            end_rows(n // 2 - 1)
+        if n < 2 * groups:
+            sum_rows(n // 2, n % 2)
         for link in links:
             t, d_1, d_2, piece = issued[link][n]
             axis, way = link
@@ -469,8 +474,6 @@
                 for other in (1, -1):
                     issue((axes[t][1], other), t, d_1, d_2, piece)
             pair(t, d_1, d_2, piece)
-        if n < groups:
-            end_rows(n)
 
     for t in range(2):
         for piece in range(2):
@@ -531,7 +534,7 @@
         vmem, anywhere = pl.BlockSpec(memory_space=pltpu.VMEM), pl.BlockSpec(memory_space=pl.ANY)
         dma = pltpu.SemaphoreType.DMA
         shape = jax.ShapeDtypeStruct
-        chips, mid, group = RING * RING, seq_len // 2, hidden // 8
+        chips, mid, group = RING * RING, seq_len // 2, hidden // 4
         fixed = lambda array: pltpu.with_memory_space_constraint(array, pltpu.VMEM)
         y_own, dx_own, d_gain, a_all, hd_all = pl.pallas_call(
             reduce_kernel,
@@ -553,7 +556,7 @@
             name="rows_reduce",
         )(x_in, dy_in, seg_ids, ln_gain, wqkv, w_up, wo, w_down)
 
-        per_link, depth = chips - 1, 2
+        per_link, depth = chips - 1, 3
         y_lo, y_hi, dx_all, d_gain, grads, d_up = pl.pallas_call(
             lambda *refs: gather_kernel(n_parts, *refs),
             in_specs=[anywhere, anywhere, vmem, anywhere, anywhere, anywhere],
@@ -561,11 +564,11 @@
             out_shape=[pltpu.VMEM((rows, mid, hidden), bf16), shape((rows, mid, hidden), bf16), pltpu.VMEM((rows, seq_len, hidden), bf16),
                        pltpu.VMEM((hidden,), bf16), pltpu.VMEM((n_all - n_up, hidden), bf16), pltpu.VMEM((hidden, n_up), bf16)],
             scratch_shapes=[
-                pltpu.VMEM((5, 2, 1, hidden), f32), pltpu.VMEM((2 * n_all, group), f32), pltpu.VMEM((2, n_all, group), f32),
-                pltpu.VMEM((depth, 2, seq_len, group), bf16), pltpu.VMEM((depth, 2, seq_len, group), bf16),
-                pltpu.VMEM((depth, 2, 2 * n_all, seq_len), bf16),
+                pltpu.VMEM((5, 2, 1, hidden), f32), pltpu.VMEM((2 * n_all, group), f32), pltpu.VMEM((n_all, group), f32),
+                pltpu.VMEM((depth, seq_len, group), bf16), pltpu.VMEM((depth, seq_len, group), bf16),
+                pltpu.VMEM((depth, 2 * n_all, seq_len), bf16),
                 dma((4, per_link)), dma((4, per_link)), dma((2, 2 * chips)), dma((2, 2)), dma((2, 2)),
-                dma((depth, 2, 3)), dma((4,)), dma((2, 4)), dma((5,)), dma((5,)),
+                dma((depth, 4)), dma((4,)), dma((4,)), pltpu.SemaphoreType.REGULAR, dma((5,)), dma((5,)),
             ],
             compiler_params=pltpu.CompilerParams(collective_id=1, has_side_effects=True, vmem_limit_bytes=LANDING_LIMIT),
             name="rows_gather",

time: 447 us -> 420 us (0.940)
  Pallas kernels: 444 us -> 419 us
    pallas_call x1, Pallas kernels: 219 us -> 193 us  [body(): pl.pallas_call(lambda *refs: gather_kernel(n_parts, *refs), in_specs=[any...]
where the time goes in v7:
time: 420 us; the launch traced here: 419 us
  Pallas kernels  419 us (100%)
    pallas_call x1, Pallas kernels, body(): pl.pallas_call(reduce_kernel, in_specs=[anywhere, anywhere, vmem, vmem] +...  196 us
    pallas_call x1, Pallas kernels, body(): pl.pallas_call(lambda *refs: gather_kernel(n_parts, *refs), in_specs=[any...  193 us
    pallas_call x1, Pallas kernels, body(): pl.pallas_call(place_kernel, in_specs=[vmem, anywhere, vmem, vmem, vmem,...  29.2 us

profile of v7, /device:TPU:97, one launch (start us, length us, event | category | flops | bytes accessed | tf_op | source)
XLA Modules:
  0.0 419.4 jit_solution(1430554871712406854)
XLA Ops:
  0.6 196.3 %rows_reduce.1 = (bf16[256,2048]{1,0:T(8,128)(2,1)}, bf16[256,2048]{1,0:T(8,128)(2,1)}, f32[1,2048]{1,0:T(1,128)}, bf16[16,256,2048]{2,1,0:T(8,128)(2,1)}, bf16[16,1536,256]{2,1,0:T(8,128)(2,1)}) custom-call(bf16[32,256,2048]{2,1,0:T(8,128)(2,1)} %x_hbm.1, bf16[32,256,2048]{2,1,0:T(8,128)(2,1)} %refs_3_.1, s32[32,256]{1,0:T(8,128)} %seg_ref.1, ...), custom_call_target="tpu_custom_call" | custom-call | tf_op jit(solution)/shard_map/rows_reduce/pallas_call | solution.py:539
  196.9 193.1 %rows_gather.1 = (bf16[32,128,2048]{2,1,0:T(8,128)(2,1)S(1)}, bf16[32,128,2048]{2,1,0:T(8,128)(2,1)}, bf16[32,256,2048]{2,1,0:T(8,128)(2,1)S(1)}, bf16[2048]{0:T...) custom-call(bf16[256,2048]{1,0:T(8,128)(2,1)} %get-tuple-element.25.refs_0_, ...), custom_call_target="tpu_custom_call" | custom-call | tf_op jit(solution)/shard_map/rows_gather/pallas_call | solution.py:560
  390.1 29.2 %rows_place.1 = (bf16[32,256,2048]{2,1,0:T(8,128)(2,1)}, bf16[32,256,2048]{2,1,0:T(8,128)(2,1)}, bf16[192,2048]{1,0:T(8,128)(2,1)}, bf16[64,2048]{1,0:T(8,128)(2...) custom-call(bf16[32,128,2048]{2,1,0:T(8,128)(2,1)S(1)} %get-tuple-element.30.y_lo, ...), custom_call_target="tpu_custom_call" | custom-call | tf_op jit(solution)/shard_map/rows_place/pallas_call | solution.py:578

commit v8 on v4

v8 whole, which is shorter than its diff:
```python
import functools

import jax
import jax.numpy as jnp
from jax import lax
from jax.experimental import pallas as pl
from jax.experimental.pallas import tpu as pltpu
from jax.sharding import PartitionSpec as P

LN_EPS = 1e-5
RING = 4
MESH = pl.DeviceIdType.MESH
NT = (((1,), (1,)), ((), ()))
NN = (((1,), (0,)), ((), ()))
TN = (((0,), (0,)), ((), ()))
ORDER = ((2, 2), (1, 2), (2, 3), (2, 1), (3, 2), (3, 3), (1, 1), (0, 2),
         (2, 0), (0, 1), (3, 1), (1, 3), (1, 0), (3, 0), (0, 3), (0, 0))
SLOT = (0, 1, 2, 3, 4, 0, 1, 2, 3, 4, 1, 0, 2, 3, 0, 1)
SLOTS = max(SLOT) + 1
PASS, LOAD, ADD = range(3)
EVENTS = (
    (((0, 0, 0, 1, PASS), (0, 0, 1, 1, PASS), (0, 1, 0, 1, PASS), (0, 1, 1, 1, PASS)),
     ()),
    (((1, 0, 0, 1, PASS), (1, 0, 1, 1, PASS), (1, 1, 1, 1, PASS)),
     ()),
    (((2, 0, 0, 1, PASS), (2, 1, 0, 1, PASS), (2, 1, 1, 1, PASS), (1, 1, 0, 1, PASS), (2, 0, 1, 1, PASS)),
     ()),
    (((3, 0, 1, 1, PASS), (3, 1, 0, 1, PASS), (3, 1, 1, 1, PASS), (3, 0, 0, 1, PASS)),
     ()),
    (((4, 0, 0, 1, PASS), (4, 0, 1, 1, PASS), (4, 1, 0, 1, PASS), (4, 1, 1, 1, PASS)),
     ()),
    (((5, 0, 0, 1, PASS), (5, 1, 0, 1, PASS), (5, 1, 1, 1, PASS)),
     ()),
    (((6, 0, 1, 1, PASS), (6, 1, 1, 1, PASS), (6, 0, 0, 1, PASS)),
     ()),
    (((7, 1, 0, 1, LOAD), (7, 0, 0, 1, PASS), (7, 0, 1, 1, PASS), (5, 0, 1, 1, PASS), (6, 1, 0, 1, PASS)),
     ((7, 1, 1, 1, LOAD), (7, 1, 0, 1, ADD), (7, 1, 0, 2, PASS))),
    (((8, 0, 0, 1, LOAD), (8, 1, 0, 1, PASS), (8, 1, 1, 1, PASS), (7, 1, 1, 1, ADD), (8, 0, 1, 1, LOAD), (7, 1, 1, 2, PASS)),
     ((8, 0, 0, 1, ADD), (8, 0, 0, 2, PASS), (8, 0, 1, 1, ADD), (8, 0, 1, 2, PASS))),
    (((9, 0, 1, 1, PASS),),
     ()),
    (((10, 0, 1, 1, PASS), (10, 1, 0, 1, PASS), (10, 1, 1, 1, PASS), (10, 0, 0, 1, PASS)),
     ()),
    (((11, 0, 0, 1, PASS), (11, 1, 1, 1, PASS), (11, 0, 1, 1, PASS), (11, 1, 0, 1, PASS), (9, 0, 0, 1, PASS)),
     ()),
    (((12, 1, 1, 1, PASS), (12, 1, 0, 1, PASS)),
     ()),
    (((12, 0, 0, 1, LOAD), (13, 1, 0, 1, PASS), (13, 1, 1, 1, PASS)),
     ((12, 0, 0, 1, ADD), (9, 1, 0, 1, LOAD), (12, 0, 0, 2, PASS))),
    (((14, 1, 1, 1, LOAD), (14, 0, 0, 1, PASS), (14, 0, 1, 1, PASS), (9, 1, 0, 1, ADD), (14, 1, 0, 1, LOAD), (9, 1, 0, 2, PASS)),
     ((14, 1, 1, 1, ADD), (12, 0, 1, 1, LOAD), (14, 1, 1, 2, PASS), (14, 1, 0, 1, ADD), (14, 1, 0, 2, PASS), (12, 0, 1, 1, ADD), (13, 0, 1, 1, LOAD), (12, 0, 1, 2, PASS), (13, 0, 1, 1, ADD), (9, 1, 1, 1, LOAD), (13, 0, 1, 2, PASS), (9, 1, 1, 1, ADD), (9, 1, 1, 2, PASS))),
    ((),
     ((13, 0, 0, 1, LOAD), (13, 0, 0, 1, ADD), (13, 0, 0, 2, PASS), (15, 1, 0, 1, LOAD), (15, 1, 0, 1, ADD), (15, 0, 0, 1, LOAD), (15, 0, 1, 1, LOAD), (15, 0, 0, 1, ADD), (15, 0, 1, 1, ADD), (15, 1, 1, 1, LOAD), (15, 1, 1, 1, ADD), (15, 0, 1, 2, PASS), (15, 1, 1, 2, PASS), (15, 1, 0, 2, PASS), (15, 0, 0, 2, PASS))),
)
VMEM_LIMIT = 60 * 2 ** 20
LANDING_LIMIT = 8 * 2 ** 20


def dot(lhs, rhs, dims):
    return lax.dot_general(lhs, rhs, dims, preferred_element_type=jnp.float32)


def norm_rows(x_f32):
    mean_val = jnp.mean(x_f32, axis=-1, keepdims=True)
    centered = x_f32 - mean_val
    inv_std = lax.rsqrt(jnp.mean(centered * centered, axis=-1, keepdims=True) + LN_EPS)
    return centered * inv_std, inv_std


class Place:
    def __init__(self):
        me = lax.axis_index('model')
        self.core = me % 2
        self.x = (me // 2) % RING
        self.y = me // (2 * RING)
        self.me = me

    def index(self, d_y, d_x, core=None):
        core = self.core if core is None else core
        return (((self.y + d_y) % RING) * RING + (self.x + d_x) % RING) * 2 + core

    def peer(self, axis, offset):
        return self.index(offset % RING, 0) if axis == 'y' else self.index(0, offset % RING)

    def sibling(self):
        return self.index(0, 0, 1 - self.core)


def remote(src, dst, send_sem, recv_sem, device):
    return pltpu.make_async_remote_copy(src_ref=src, dst_ref=dst, send_sem=send_sem, recv_sem=recv_sem,
                                        device_id={'model': device}, device_id_type=MESH)


def greet(peers):
    barrier = pltpu.get_barrier_semaphore()
    for peer in peers:
        pl.semaphore_signal(barrier, inc=1, device_id={'model': peer}, device_id_type=MESH)
    return barrier


def pick(step, values):
    out = jnp.int32(0)
    for n, value in enumerate(values):
        out = jnp.where(step == n, value, out)
    return out


def rows_at(ref, at, count):
    return ref.at[pl.ds(pl.multiple_of(at, 16), count)]


def landed(ref, sem):
    pltpu.make_async_copy(ref, ref, sem).wait()


def add_into(dst, *sources):
    rows = dst.shape[0]
    tile = min(rows, 32)

    def tile_add(n, carry):
        at = pl.ds(pl.multiple_of(n * tile, tile), tile)
        total = dst[at, :].astype(jnp.float32)
        for source in sources:
            total += source[at, :].astype(jnp.float32)
        dst[at, :] = total.astype(dst.dtype)
        return carry

    lax.fori_loop(0, rows // tile, tile_add, 0)


def reduce_kernel(x_hbm, dy_hbm, seg_ref, gain_ref, wqkv_hbm, w1_hbm, wo_hbm, w2_hbm,
                  y_own, dx_own, dgain_ref, g_own, g_sib, full,
                  w_in, w_out, w1_raw, acc, x_buf, dy_buf, a_scr, hd_scr, stage, half, last_full, tmp,
                  row_sem, w_sem, ws_sem, wr_sem, send_sem, half_sem, full_sem, tmp_sem, end_sem, out_sem):
    place = Place()
    core = place.core
    _, seq_len, hidden = x_buf.shape
    mid = seq_len // 2
    n_qkv, n_up, n_o, n_dn = wqkv_hbm.shape[0], w1_hbm.shape[1], wo_hbm.shape[0], w2_hbm.shape[0]
    n_d = 2 * (n_qkv + n_up)
    steps = len(ORDER)

    def row_of(step):
        return place.index(pick(step, [o[0] for o in ORDER]), pick(step, [o[1] for o in ORDER]))

    def row_copy(row, buf, n):
        return pltpu.make_async_copy((x_hbm, dy_hbm)[n].at[row], (x_buf, dy_buf)[n].at[buf], row_sem.at[buf, n])

    up_spot = rows_at(w_in, 2 * n_qkv + core * n_up, n_up)
    spots = ((wqkv_hbm, rows_at(w_in, core * n_qkv, n_qkv)), (wo_hbm, rows_at(w_out, core * n_o, n_o)),
             (w2_hbm, rows_at(w_out, 2 * n_o + core * n_dn, n_dn)))

    gain = gain_ref[...].astype(jnp.float32)[None, :]
    sub = min(seq_len, 64)

    def norm_row(buf):
        for t in range(0, seq_len, sub):
            normed, _ = norm_rows(x_buf[buf, t:t + sub, :].astype(jnp.float32))
            a_scr[t:t + sub, :] = (normed * gain).astype(jnp.bfloat16)

    peers = [place.peer('x', 1), place.peer('x', -1), place.peer('y', 1), place.peer('y', -1), place.sibling()]
    barrier = greet(peers)
    raw = pltpu.make_async_copy(w1_hbm, w1_raw, w_sem.at[3])
    raw.start()
    for n in range(2):
        row_copy(row_of(0), 0, n).start()
    mine = [pltpu.make_async_copy(src, dst, w_sem.at[n]) for n, (src, dst) in enumerate(spots)]
    for copy in mine:
        copy.start()
    raw.wait()
    turn = min(hidden, 256)
    for h in range(0, hidden, turn):
        up_spot[:, h:h + turn] = w1_raw[h:h + turn, :].T
    pl.semaphore_wait(barrier, len(peers))
    swaps = [remote(src, dst, ws_sem.at[n], wr_sem.at[n], place.sibling()) for n, (src, dst) in enumerate(spots)]
    swaps.append(remote(up_spot, up_spot, ws_sem.at[3], wr_sem.at[3], place.sibling()))
    for n in (0, 3, 1, 2):
        swaps[n].start()
    row_copy(0, 0, 0).wait()
    norm_row(0)
    acc[...] = jnp.zeros_like(acc)
    mine[0].wait()
    for n in (0, 3):
        swaps[n].wait()

    scale = n_o ** -0.5
    cols_step = min(hidden, 512)

    def piece_of(ref, piece):
        return ref.at[pl.ds(piece * mid, mid)]

    def slot_sends(slot):
        return [pltpu.make_async_copy(piece_of(stage.at[slot, t], piece), piece_of(stage.at[slot, t], piece),
                                      send_sem.at[slot, t, piece]) for t in range(2) for piece in range(2)]

    def event(n, t, piece, ring, kind):
        d_y, d_x = ORDER[n]
        first, second = (('x', d_x), ('y', d_y)) if t == 0 else (('y', d_y), ('x', d_x))
        (axis, offset), line = (first, second[1]) if ring == 1 else (second, RING)
        ahead, behind = place.peer(axis, 1), place.peer(axis, -1)
        spot = piece_of(stage.at[SLOT[n], t], piece)

        def send(dst, recv_sem, device):
            remote(spot, dst, send_sem.at[SLOT[n], t, piece], recv_sem, device).start()

        if offset == 2:
            send(half.at[t, line, piece], half_sem.at[t, line, piece], ahead if piece == 0 else behind)
        elif offset in (1, 3):
            side = 0 if offset == 1 else 1
            if side == piece:
                landed(half.at[t, line, piece], half_sem.at[t, line, piece])
                add_into(spot, half.at[t, line, piece])
            dst = last_full.at[t, side] if line == RING else full.at[t, line, side]
            send(piece_of(dst, piece), full_sem.at[t, line, side, piece], ahead if side == 0 else behind)
        elif line == RING:
            came = [piece_of(last_full.at[t, side], piece) for side in range(2)]
            for side in range(2):
                landed(came[side], full_sem.at[t, line, side, piece])
            add_into(spot, *came)
        else:
            loads = [pltpu.make_async_copy(piece_of(full.at[t, line, side], piece), tmp.at[piece, side], tmp_sem.at[piece, side])
                     for side in range(2)]
            if kind == LOAD:
                for side in range(2):
                    landed(piece_of(full.at[t, line, side], piece), full_sem.at[t, line, side, piece])
                    loads[side].start()
            else:
                for load in loads:
                    load.wait()
                add_into(spot, tmp.at[piece, 0], tmp.at[piece, 1])

    def grad_copies():
        copies = []
        for n, (side, dst) in enumerate(((core, g_own), (1 - core, g_sib))):
            at, to = 0, 0
            for m, size in enumerate((n_qkv, n_up, n_o, n_dn)):
                copies.append(pltpu.make_async_copy(rows_at(acc, at + side * size, size), dst.at[pl.ds(to, size)], out_sem.at[4 * n + m]))
                at, to = at + 2 * size, to + size
        return copies

    def attend(qkv, d_attn, allowed):
        heads = range(2)
        parts = [[qkv[head * n_qkv + n * n_o:head * n_qkv + (n + 1) * n_o] for n in range(3)] for head in heads]
        d_o = [d_attn[head * n_o:(head + 1) * n_o] for head in heads]
        raw = [dot(keys, query, TN) for query, keys, _ in parts]
        d_p = [dot(parts[head][2], d_o[head], TN) for head in heads]
        expd = []
        for head in heads:
            scores = jnp.where(allowed, raw[head] * scale, -1e30)
            expd.append(jnp.exp(scores - jnp.max(scores, axis=0, keepdims=True)))
        probs = [e / jnp.sum(e, axis=0, keepdims=True) for e in expd]
        probs_b = [p.astype(jnp.bfloat16) for p in probs]
        d_s = [(probs[head] * (d_p[head] - jnp.sum(d_p[head] * probs[head], axis=0, keepdims=True)) * scale).astype(jnp.bfloat16)
               for head in heads]
        for head in heads:
            at = head * n_qkv
            query, keys, values = parts[head]
            hd_scr[n_d + head * n_o:n_d + (head + 1) * n_o, :] = dot(values, probs_b[head], NN).astype(jnp.bfloat16)
            hd_scr[at + 2 * n_o:at + 3 * n_o, :] = dot(d_o[head], probs_b[head], NT).astype(jnp.bfloat16)
            hd_scr[at:at + n_o, :] = dot(keys, d_s[head], NN).astype(jnp.bfloat16)
            hd_scr[at + n_o:at + 2 * n_o, :] = dot(query, d_s[head], NT).astype(jnp.bfloat16)

    def row_step(step, carry):
        buf = step % 2
        slot = pick(step, SLOT)
        row = row_of(step)

        @pl.when(step > 0)
        def _():
            row_copy(row, buf, 0).wait()
            norm_row(buf)

        row_copy(row, buf, 1).wait()

        @pl.when(step + 1 < steps)
        def _():
            ahead = row_of(step + 1)
            for n in range(2):
                row_copy(ahead, 1 - buf, n).start()

        @pl.when(step == 0)
        def _():
            for copy in mine[1:] + swaps[1:3]:
                copy.wait()

        proj = dot(w_in[...], a_scr[...], NT)
        d_proj = dot(w_out[...], dy_buf[buf], NT).astype(jnp.bfloat16)
        qkv = proj[:2 * n_qkv].astype(jnp.bfloat16)
        up = proj[2 * n_qkv:].astype(jnp.bfloat16).astype(jnp.float32)
        d_attn = d_proj[:2 * n_o]
        d_hid = d_proj[2 * n_o:].astype(jnp.float32)
        cdf = 0.5 * (1.0 + lax.erf(up * (0.5 ** 0.5)))
        hd_scr[n_d + 2 * n_o:, :] = (up * cdf).astype(jnp.bfloat16)
        slope = cdf + up * (jnp.exp(-0.5 * up * up) * 0.3989422804014327)
        hd_scr[2 * n_qkv:n_d, :] = (d_hid * slope).astype(jnp.bfloat16)

        seg_row = seg_ref[pl.ds(row, 1), :]
        classes = lax.broadcasted_iota(jnp.int32, (16, seq_len), 0)
        one_hot = (classes == jnp.broadcast_to(seg_row, (16, seq_len))).astype(jnp.bfloat16)
        same = dot(one_hot, one_hot, TN) > 0.5
        key_id = lax.broadcasted_iota(jnp.int32, (seq_len, seq_len), 0)
        query_id = lax.broadcasted_iota(jnp.int32, (seq_len, seq_len), 1)
        allowed = (key_id <= query_id) & same
        attend(qkv, d_attn, allowed)

        @pl.when(pick(step, [int(SLOT[n] in SLOT[:n]) for n in range(steps)]) == 1)
        def _():
            for copy in slot_sends(slot):
                copy.wait()

        for h in range(0, hidden, cols_step):
            cols = slice(h, h + cols_step)
            stage[slot, 0, :, cols] = dot(hd_scr[n_d:, :], w_out[:, cols], TN).astype(jnp.bfloat16)
            stage[slot, 1, :, cols] = dot(hd_scr[:n_d, :], w_in[:, cols], TN).astype(jnp.bfloat16)

        def pass_on(when):
            for n in range(steps - 1):
                if EVENTS[n][when]:
                    @pl.when(step == n)
                    def _():
                        for work in EVENTS[n][when]:
                            event(*work)

        pass_on(0)
        for h in range(0, hidden, cols_step):
            cols = slice(h, h + cols_step)
            acc[:n_d, cols] += dot(hd_scr[:n_d, :], a_scr[:, cols], NN)
            acc[n_d:, cols] += dot(hd_scr[n_d:, :], dy_buf[buf, :, cols], NN)
        pass_on(1)
        return carry

    lax.fori_loop(0, steps, row_step, 0)
    last, buf = SLOT[-1], (steps - 1) % 2
    for copy in grad_copies():
        copy.start()
    dgain_ref[...] = jnp.zeros_like(dgain_ref)
    fine = min(mid, 32)

    def finish(piece):
        def tile(n, d_gain):
            at = pl.ds(pl.multiple_of(piece * mid + n * fine, fine), fine)
            x_f32 = x_buf[buf, at, :].astype(jnp.float32)
            normed, inv_std = norm_rows(x_f32)
            grad = stage[last, 1, at, :].astype(jnp.float32)
            stage[last, 0, at, :] = (x_f32 + stage[last, 0, at, :].astype(jnp.float32)).astype(jnp.bfloat16)
            d_hat = grad * gain
            d_x = inv_std * (d_hat - jnp.mean(d_hat, axis=-1, keepdims=True) - normed * jnp.mean(d_hat * normed, axis=-1, keepdims=True))
            stage[last, 1, at, :] = (dy_buf[buf, at, :].astype(jnp.float32) + d_x).astype(jnp.bfloat16)
            return d_gain + jnp.sum(grad * normed, axis=0, keepdims=True)

        dgain_ref[...] += lax.fori_loop(0, mid // fine, tile, jnp.zeros((1, hidden), jnp.float32))
        copies = [pltpu.make_async_copy(piece_of(stage.at[last, t], piece), piece_of(dst, piece), end_sem.at[piece, t])
                  for t, dst in ((0, y_own), (1, dx_own))]
        for copy in copies:
            copy.start()
        return copies

    ends = []
    ended = {0: 0, 1: 0}
    for work in EVENTS[-1][1]:
        event(*work)
        n, _, piece, ring, _ = work
        if n == steps - 1 and ring == 2:
            ended[piece] += 1
            if ended[piece] == 2:
                ends += finish(piece)
    for slot in range(SLOTS):
        if slot != last:
            for copy in slot_sends(slot):
                copy.wait()
    for copy in ends + grad_copies():
        copy.wait()


def gather_kernel(y_own, dx_own, dgain_ref, g_own, g_sib, y_lo, y_hi, dx_all, g_recv, dgain_out, grads, d_up,
                  gain_scr, g_buf, t_buf, send_sem, link_sem, pair_sem, pair_recv, own_sem, g_sem, gb_sem, dg_send, dg_recv):
    place = Place()
    core = place.core
    _, seq_len, hidden = dx_all.shape
    mid = seq_len // 2
    links = (('x', 1), ('x', -1), ('y', 1), ('y', -1))
    peers = [place.peer(a, o) for a in ('x', 'y') for o in (1, -1)] + [place.sibling()]
    pl.semaphore_wait(greet(peers), len(peers))

    issued = {link: [] for link in links}
    sends = []

    def row_index(t, d_1, d_2):
        return place.index(d_1 % RING, d_2 % RING) if t == 0 else place.index(d_2 % RING, d_1 % RING)

    def spot_of(t, row, piece):
        if t == 1:
            return dx_all.at[row, pl.ds(piece * mid, mid)]
        return (y_lo, y_hi)[piece].at[row]

    def source(t, d_1, d_2, piece):
        if (d_1, d_2) == (0, 0):
            return (y_own, dx_own)[t].at[pl.ds(piece * mid, mid)]
        return spot_of(t, row_index(t, d_1, d_2), piece)

    def issue(link, t, d_1, d_2, piece):
        n = len(issued[link])
        which = links.index(link)
        copy = remote(source(t, d_1, d_2, piece), spot_of(t, row_index(t, d_1, d_2), piece),
                      send_sem.at[which, n], link_sem.at[which, n], place.peer(*link))
        copy.start()
        sends.append(copy)
        issued[link].append((t, d_1, d_2, piece))

    def pair(t, d_1, d_2, piece):
        slot = ((d_1 % RING) * RING + d_2 % RING) * 2 + piece
        copy = remote(source(t, d_1, d_2, piece), spot_of(t, row_index(t, d_1, d_2), piece),
                      pair_sem.at[t, slot], pair_recv.at[t, piece], place.sibling())
        copy.start()
        sends.append(copy)

    axes = (('y', 'x'), ('x', 'y'))
    for ring in range(2):
        for n in range(2):
            for t in range(2):
                for way in (1, -1):
                    issue((axes[t][ring], way), t, 0, 0, n if way == 1 else 1 - n)
    locals_ = []
    for t in range(2):
        for piece in range(2):
            pair(t, 0, 0, piece)
            copy = pltpu.make_async_copy(source(t, 0, 0, piece), spot_of(t, place.me, piece), own_sem.at[t, piece])
            copy.start()
            locals_.append(copy)

    g_copy = remote(g_sib, g_recv, g_sem.at[0], g_sem.at[1], place.sibling())
    g_copy.start()

    tile, turn = g_buf.shape[1], t_buf.shape[2]
    n_up = d_up.shape[1]
    n_qkv = 3 * tile

    def grad_tile(at, to):
        loads = [pltpu.make_async_copy(g.at[pl.ds(at, tile)], g_buf.at[n], gb_sem.at[n]) for n, g in enumerate((g_own, g_recv))]
        for load in loads:
            load.start()
        for load in loads:
            load.wait()
        grads[to:to + tile, :] = (g_buf[0] + g_buf[1]).astype(grads.dtype)

    def up_tile(h):
        loads = [pltpu.make_async_copy(g.at[pl.ds(n_qkv, n_up), pl.ds(h, turn)], t_buf.at[n], gb_sem.at[n])
                 for n, g in enumerate((g_own, g_recv))]
        for load in loads:
            load.start()
        for load in loads:
            load.wait()
        d_up[h:h + turn, :] = (t_buf[0] + t_buf[1]).T.astype(d_up.dtype)

    jobs = [functools.partial(grad_tile, at, at) for at in range(0, n_qkv, tile)]
    jobs += [functools.partial(grad_tile, at, at - n_up) for at in range(n_qkv + n_up, g_own.shape[0], tile)]
    jobs += [functools.partial(up_tile, h) for h in range(0, hidden, turn)]

    total = dgain_ref[...]
    for n, axis in enumerate(('core', 'x', 'x', 'y', 'y')):
        at = {'core': core, 'x': place.x, 'y': place.y}[axis]
        other = (RING - 1 - at) if n in (2, 4) else at + 1 - 2 * (at % 2)
        device = place.sibling() if axis == 'core' else place.peer(axis, other - at)
        gain_scr[n, 0] = total
        copy = remote(gain_scr.at[n, 0], gain_scr.at[n, 1], dg_send.at[n], dg_recv.at[n], device)
        copy.start()
        copy.wait()
        total = gain_scr[n, 0] + gain_scr[n, 1]
    dgain_out[...] = jnp.sum(total, axis=0).astype(dgain_out.dtype)

    rounds = RING * RING - 1
    for n in range(rounds):
        for link in links:
            t, d_1, d_2, piece = issued[link][n]
            axis, way = link
            on_first = axis == axes[t][0]
            d_1, d_2 = (d_1 - way, d_2) if on_first else (d_1, d_2 - way)
            landed(spot_of(t, row_index(t, d_1, d_2), piece), link_sem.at[links.index(link), n])
            along = d_1 if on_first else d_2
            if abs(along) == 1 and piece == (0 if way == 1 else 1):
                issue(link, t, d_1, d_2, piece)
            if on_first:
                for other in (1, -1):
                    issue((axes[t][1], other), t, d_1, d_2, piece)
            pair(t, d_1, d_2, piece)
        if n == 2:
            g_copy.wait()
        if n >= 2:
            for job in jobs[2 * (n - 2):2 * (n - 1)]:
                job()

    for t in range(2):
        for piece in range(2):
            theirs = dx_all.at[pl.ds(0, RING * RING), pl.ds(piece * mid, mid)] if t else (y_lo, y_hi)[piece].at[pl.ds(0, RING * RING)]
            landed(theirs, pair_recv.at[t, piece])
    for copy in sends:
        copy.wait_send()
    for copy in locals_:
        copy.wait()


def place_kernel(y_lo, y_hi, dx_all, grads, d_up, dgain, y_out, dx_out, d_wqkv, d_wout, d_wdown, d_wup, dgain_out, bounce, in_sem, out_sem, sem):
    rows, mid, _ = y_lo.shape
    n_qkv, n_o, n_dn = d_wqkv.shape[0], d_wout.shape[0], d_wdown.shape[0]
    bufs, per = bounce.shape[0], bounce.shape[1]
    count = rows // per
    loads = [pltpu.make_async_copy(y_hi.at[pl.ds(n * per, per)], bounce.at[n % bufs], in_sem.at[n % bufs]) for n in range(count)]
    stores = [pltpu.make_async_copy(bounce.at[n % bufs], y_out.at[pl.ds(n * per, per), pl.ds(mid, mid)], out_sem.at[n % bufs]) for n in range(count)]
    for n in range(min(bufs, count)):
        loads[n].start()
    split = 4
    part = rows // split
    direct = []
    for n in range(split):
        at = pl.ds(n * part, part)
        direct += [(dx_all.at[at], dx_out.at[at]), (y_lo.at[at], y_out.at[at, pl.ds(0, mid)])]
    direct += [(grads.at[pl.ds(0, n_qkv)], d_wqkv),
               (grads.at[pl.ds(n_qkv, n_o)], d_wout), (grads.at[pl.ds(n_qkv + n_o, n_dn)], d_wdown), (d_up, d_wup)]
    copies = [pltpu.make_async_copy(src, dst, sem.at[n]) for n, (src, dst) in enumerate(direct)]
    for copy in copies:
        copy.start()
    dgain_out[...] = dgain[...]
    for n in range(count):
        loads[n].wait()
        stores[n].start()
        if n >= 1 and n - 1 + bufs < count:
            stores[n - 1].wait()
            loads[n - 1 + bufs].start()
    for n in range(max(0, count - bufs), count):
        stores[n].wait()
    for copy in copies:
        copy.wait()


def solution(mesh):
    devices = mesh.shape['model']
    assert devices == 2 * RING * RING

    def body(x_in, seg_ids, ln_gain, w_qkv, w_out, w_up, w_down, dy_in):
        rows, seq_len, hidden = x_in.shape
        assert rows == devices
        wqkv = w_qkv.transpose(1, 2, 3, 0).reshape(-1, hidden)
        wo = w_out.reshape(-1, hidden)
        n_qkv, n_up, n_o, n_dn = wqkv.shape[0], w_up.shape[1], wo.shape[0], w_down.shape[0]
        n_in, n_out = n_qkv + n_up, n_o + n_dn
        n_all = n_in + n_out
        bf16, f32 = jnp.bfloat16, jnp.float32
        vmem, anywhere = pl.BlockSpec(memory_space=pltpu.VMEM), pl.BlockSpec(memory_space=pl.ANY)
        dma = pltpu.SemaphoreType.DMA
        shape = jax.ShapeDtypeStruct
        chips, mid = RING * RING, seq_len // 2
        fixed = lambda array: pltpu.with_memory_space_constraint(array, pltpu.VMEM)
        y_own, dx_own, d_gain, g_own, g_sib, _ = pl.pallas_call(
            reduce_kernel,
            in_specs=[anywhere, anywhere, vmem, vmem] + [anywhere] * 4,
            out_specs=[anywhere, anywhere, vmem, anywhere, anywhere, anywhere],
            out_shape=[shape((seq_len, hidden), bf16), shape((seq_len, hidden), bf16), shape((1, hidden), f32),
                       shape((n_all, hidden), f32), shape((n_all, hidden), f32), shape((2, RING, 2, seq_len, hidden), bf16)],
            scratch_shapes=[
                pltpu.VMEM((2 * n_in, hidden), bf16), pltpu.VMEM((2 * n_out, hidden), bf16), pltpu.VMEM((hidden, n_up), bf16),
                pltpu.VMEM((2 * n_all, hidden), f32),
                pltpu.VMEM((2, seq_len, hidden), bf16), pltpu.VMEM((2, seq_len, hidden), bf16),
                pltpu.VMEM((seq_len, hidden), bf16), pltpu.VMEM((2 * n_all, seq_len), bf16),
                pltpu.VMEM((SLOTS, 2, seq_len, hidden), bf16),
                pltpu.VMEM((2, RING + 1, 2, mid, hidden), bf16),
                pltpu.VMEM((2, 2, seq_len, hidden), bf16), pltpu.VMEM((2, 2, mid, hidden), bf16),
                dma((2, 2)), dma((4,)), dma((4,)), dma((4,)), dma((SLOTS, 2, 2)),
                dma((2, RING + 1, 2)), dma((2, RING + 1, 2, 2)), dma((2, 2)), dma((2, 2)), dma((8,)),
            ],
            compiler_params=pltpu.CompilerParams(collective_id=0, has_side_effects=True, vmem_limit_bytes=VMEM_LIMIT),
            name="rows_reduce",
        )(x_in, dy_in, seg_ids, ln_gain, wqkv, w_up, wo, w_down)

        per_link = chips - 1
        y_lo, y_hi, dx_all, _, d_gain, grads, d_up = pl.pallas_call(
            gather_kernel,
            in_specs=[anywhere, anywhere, vmem, anywhere, anywhere],
            out_specs=[vmem, anywhere, vmem, anywhere, vmem, vmem, vmem],
            out_shape=[pltpu.VMEM((rows, mid, hidden), bf16), shape((rows, mid, hidden), bf16), pltpu.VMEM((rows, seq_len, hidden), bf16),
                       shape(g_sib.shape, f32), pltpu.VMEM((hidden,), bf16),
                       pltpu.VMEM((n_all - n_up, hidden), bf16), pltpu.VMEM((hidden, n_up), bf16)],
            scratch_shapes=[
                pltpu.VMEM((5, 2, 1, hidden), f32), pltpu.VMEM((2, n_o, hidden), f32), pltpu.VMEM((2, n_up, min(hidden, 256)), f32),
                dma((4, per_link)), dma((4, per_link)), dma((2, 2 * chips)), dma((2, 2)), dma((2, 2)), dma((2,)), dma((2,)),
                dma((5,)), dma((5,)),
            ],
            compiler_params=pltpu.CompilerParams(collective_id=1, has_side_effects=True, vmem_limit_bytes=LANDING_LIMIT),
            name="rows_gather",
        )(y_own, dx_own, d_gain, g_own, g_sib)

        bufs = 6
        y_out, dx_out, d_wqkv, d_wout, d_wdown, d_wup, d_gain = pl.pallas_call(
            place_kernel,
            in_specs=[vmem, anywhere, vmem, vmem, vmem, vmem],
            out_specs=[anywhere] * 6 + [vmem],
            out_shape=[shape(x_in.shape, bf16), shape(x_in.shape, bf16), shape(wqkv.shape, bf16), shape(wo.shape, bf16),
                       shape(w_down.shape, bf16), shape(w_up.shape, bf16), shape((hidden,), bf16)],
            scratch_shapes=[pltpu.VMEM((bufs, 2, mid, hidden), bf16), dma((bufs,)), dma((bufs,)), dma((12,))],
            compiler_params=pltpu.CompilerParams(vmem_limit_bytes=LANDING_LIMIT),
            name="rows_place",
        )(fixed(y_lo), pltpu.with_memory_space_constraint(y_hi, pltpu.HBM), fixed(dx_all), fixed(grads), fixed(d_up), fixed(d_gain))
        d_wqkv = d_wqkv.reshape(w_qkv.shape[1:] + (hidden,)).transpose(3, 0, 1, 2)
        return y_out, dx_out, d_gain, d_wqkv, d_wout.reshape(w_out.shape), d_wup, d_wdown

    in_specs = (P('data'), P('data'), P(), P(None, 'model'), P('model'), P(None, 'model'), P('model'), P('data'))
    out_specs = (P('data'), P('data'), P('data'), P('data', 'model'), P(('data', 'model')), P('data', 'model'), P(('data', 'model')))
    return jax.shard_map(body, mesh=mesh, in_specs=in_specs, out_specs=out_specs, check_vma=False)
```

time: 415 us -> 415 us (level)
  no operation moved by 1% of the time
where the time goes in v8:
time: 415 us; the launch traced here: 414 us
  Pallas kernels  413 us (100%)
    pallas_call x1, Pallas kernels, body(): pl.pallas_call(reduce_kernel, in_specs=[anywhere, anywhere, vmem, vmem] +...  196 us
    pallas_call x1, Pallas kernels, body(): pl.pallas_call(gather_kernel, in_specs=[anywhere, anywhere, vmem, anywher...  187 us
    pallas_call x1, Pallas kernels, body(): pl.pallas_call(place_kernel, in_specs=[vmem, anywhere, vmem, vmem, vmem,...  29.2 us

profile of v8, /device:TPU:97, one launch (start us, length us, event | category | flops | bytes accessed | tf_op | source)
XLA Modules:
  0.0 413.8 jit_solution(3892316101504474573)
XLA Ops:
  0.6 196.4 %rows_reduce.1 = (bf16[256,2048]{1,0:T(8,128)(2,1)}, bf16[256,2048]{1,0:T(8,128)(2,1)}, f32[1,2048]{1,0:T(1,128)}, f32[768,2048]{1,0:T(8,128)}, f32[768,2048]{1,...) custom-call(bf16[32,256,2048]{2,1,0:T(8,128)(2,1)} %x_hbm.1, bf16[32,256,2048]{2,1,0:T(8,128)(2,1)} %dy_hbm.1, ...), custom_call_target="tpu_custom_call" | custom-call | tf_op jit(solution)/shard_map/rows_reduce/pallas_call | solution.py:553
  197.0 187.5 %rows_gather.1 = (bf16[32,128,2048]{2,1,0:T(8,128)(2,1)S(1)}, bf16[32,128,2048]{2,1,0:T(8,128)(2,1)}, bf16[32,256,2048]{2,1,0:T(8,128)(2,1)S(1)}, f32[768,2048]{...) custom-call(bf16[256,2048]{1,0:T(8,128)(2,1)} %get-tuple-element.25.y_own, ...), custom_call_target="tpu_custom_call" | custom-call | tf_op jit(solution)/shard_map/rows_gather/pallas_call | solution.py:575
  384.5 29.2 %rows_place.1 = (bf16[32,256,2048]{2,1,0:T(8,128)(2,1)}, bf16[32,256,2048]{2,1,0:T(8,128)(2,1)}, bf16[192,2048]{1,0:T(8,128)(2,1)}, bf16[64,2048]{1,0:T(8,128)(2...) custom-call(bf16[32,128,2048]{2,1,0:T(8,128)(2,1)S(1)} %get-tuple-element.30.y_lo, ...), custom_call_target="tpu_custom_call" | custom-call | tf_op jit(solution)/shard_map/rows_place/pallas_call | solution.py:592

commit v9 on v8

--- a/solution.py
+++ b/solution.py
@@ -379,7 +379,7 @@
     _, seq_len, hidden = dx_all.shape
     mid = seq_len // 2
     links = (('x', 1), ('x', -1), ('y', 1), ('y', -1))
-    peers = [place.peer(a, o) for a in ('x', 'y') for o in (1, -1)] + [place.sibling()]
+    peers = [place.peer(a, o) for a in ('x', 'y') for o in (1, 2, 3)] + [place.sibling()]
     pl.semaphore_wait(greet(peers), len(peers))
 
     issued = {link: [] for link in links}
@@ -415,6 +415,29 @@
         sends.append(copy)
 
     axes = (('y', 'x'), ('x', 'y'))
+    def gain_swap(n):
+        axis = ('x', 'core', 'y')[n]
+        at = {'core': place.core, 'x': place.x, 'y': place.y}[axis]
+        devices = [place.sibling()] if axis == 'core' else [place.peer(axis, offset) for offset in (1, 2, 3)]
+        return at, [remote(gain_scr.at[n, at], gain_scr.at[n, at], dg_send.at[n, m], dg_recv.at[n, m], device)
+                    for m, device in enumerate(devices)]
+
+    def gain_start(n, value):
+        at, copies = gain_swap(n)
+        gain_scr[n, at] = value
+        for copy in copies:
+            copy.start()
+
+    def gain_end(n):
+        _, copies = gain_swap(n)
+        for copy in copies:
+            copy.wait()
+        total = gain_scr[n, 0]
+        for m in range(1, len(copies) + 1):
+            total = total + gain_scr[n, m]
+        return total
+
+    gain_start(0, dgain_ref[...])
     for ring in range(2):
         for n in range(2):
             for t in range(2):
@@ -456,18 +479,7 @@
     jobs += [functools.partial(grad_tile, at, at - n_up) for at in range(n_qkv + n_up, g_own.shape[0], tile)]
     jobs += [functools.partial(up_tile, h) for h in range(0, hidden, turn)]
 
-    total = dgain_ref[...]
-    for n, axis in enumerate(('core', 'x', 'x', 'y', 'y')):
-        at = {'core': core, 'x': place.x, 'y': place.y}[axis]
-        other = (RING - 1 - at) if n in (2, 4) else at + 1 - 2 * (at % 2)
-        device = place.sibling() if axis == 'core' else place.peer(axis, other - at)
-        gain_scr[n, 0] = total
-        copy = remote(gain_scr.at[n, 0], gain_scr.at[n, 1], dg_send.at[n], dg_recv.at[n], device)
-        copy.start()
-        copy.wait()
-        total = gain_scr[n, 0] + gain_scr[n, 1]
-    dgain_out[...] = jnp.sum(total, axis=0).astype(dgain_out.dtype)
-
+    gain_start(1, gain_end(0))
     rounds = RING * RING - 1
     for n in range(rounds):
         for link in links:
@@ -483,6 +495,10 @@
                 for other in (1, -1):
                     issue((axes[t][1], other), t, d_1, d_2, piece)
             pair(t, d_1, d_2, piece)
+        if n == 0:
+            gain_start(2, gain_end(1))
+        if n == 10:
+            dgain_out[...] = jnp.sum(gain_end(2), axis=0).astype(dgain_out.dtype)
         if n == 2:
             g_copy.wait()
         if n >= 2:
@@ -580,9 +596,9 @@
                        shape(g_sib.shape, f32), pltpu.VMEM((hidden,), bf16),
                        pltpu.VMEM((n_all - n_up, hidden), bf16), pltpu.VMEM((hidden, n_up), bf16)],
             scratch_shapes=[
-                pltpu.VMEM((5, 2, 1, hidden), f32), pltpu.VMEM((2, n_o, hidden), f32), pltpu.VMEM((2, n_up, min(hidden, 256)), f32),
+                pltpu.VMEM((3, RING, 1, hidden), f32), pltpu.VMEM((2, n_o, hidden), f32), pltpu.VMEM((2, n_up, min(hidden, 256)), f32),
                 dma((4, per_link)), dma((4, per_link)), dma((2, 2 * chips)), dma((2, 2)), dma((2, 2)), dma((2,)), dma((2,)),
-                dma((5,)), dma((5,)),
+                dma((3, 3)), dma((3, 3)),
             ],
             compiler_params=pltpu.CompilerParams(collective_id=1, has_side_effects=True, vmem_limit_bytes=LANDING_LIMIT),
             name="rows_gather",

time: 415 us -> 408 us (0.983)
  Pallas kernels: 413 us -> 407 us
    pallas_call x1, Pallas kernels: 187 us -> 181 us  [body(): pl.pallas_call(gather_kernel, in_specs=[anywhere, anywhere, vmem, anywher...]
where the time goes in v9:
time: 408 us; the launch traced here: 407 us
  Pallas kernels  407 us (100%)
    pallas_call x1, Pallas kernels, body(): pl.pallas_call(reduce_kernel, in_specs=[anywhere, anywhere, vmem, vmem] +...  196 us
    pallas_call x1, Pallas kernels, body(): pl.pallas_call(gather_kernel, in_specs=[anywhere, anywhere, vmem, anywher...  181 us
    pallas_call x1, Pallas kernels, body(): pl.pallas_call(place_kernel, in_specs=[vmem, anywhere, vmem, vmem, vmem,...  29.2 us

profile of v9, /device:TPU:97, one launch (start us, length us, event | category | flops | bytes accessed | tf_op | source)
XLA Modules:
  0.0 407.5 jit_solution(7375327730115541569)
XLA Ops:
  0.6 196.4 %rows_reduce.1 = (bf16[256,2048]{1,0:T(8,128)(2,1)}, bf16[256,2048]{1,0:T(8,128)(2,1)}, f32[1,2048]{1,0:T(1,128)}, f32[768,2048]{1,0:T(8,128)}, f32[768,2048]{1,...) custom-call(bf16[32,256,2048]{2,1,0:T(8,128)(2,1)} %x_hbm.1, bf16[32,256,2048]{2,1,0:T(8,128)(2,1)} %dy_hbm.1, ...), custom_call_target="tpu_custom_call" | custom-call | tf_op jit(solution)/shard_map/rows_reduce/pallas_call | solution.py:569
  197.0 181.1 %rows_gather.1 = (bf16[32,128,2048]{2,1,0:T(8,128)(2,1)S(1)}, bf16[32,128,2048]{2,1,0:T(8,128)(2,1)}, bf16[32,256,2048]{2,1,0:T(8,128)(2,1)S(1)}, f32[768,2048]{...) custom-call(bf16[256,2048]{1,0:T(8,128)(2,1)} %get-tuple-element.25.y_own, ...), custom_call_target="tpu_custom_call" | custom-call | tf_op jit(solution)/shard_map/rows_gather/pallas_call | solution.py:591
  378.1 29.2 %rows_place.1 = (bf16[32,256,2048]{2,1,0:T(8,128)(2,1)}, bf16[32,256,2048]{2,1,0:T(8,128)(2,1)}, bf16[192,2048]{1,0:T(8,128)(2,1)}, bf16[64,2048]{1,0:T(8,128)(2...) custom-call(bf16[32,128,2048]{2,1,0:T(8,128)(2,1)S(1)} %get-tuple-element.30.y_lo, ...), custom_call_target="tpu_custom_call" | custom-call | tf_op jit(solution)/shard_map/rows_place/pallas_call | solution.py:608

commit v10 on v9

--- a/solution.py
+++ b/solution.py
@@ -53,7 +53,7 @@
      ((13, 0, 0, 1, LOAD), (13, 0, 0, 1, ADD), (13, 0, 0, 2, PASS), (15, 1, 0, 1, LOAD), (15, 1, 0, 1, ADD), (15, 0, 0, 1, LOAD), (15, 0, 1, 1, LOAD), (15, 0, 0, 1, ADD), (15, 0, 1, 1, ADD), (15, 1, 1, 1, LOAD), (15, 1, 1, 1, ADD), (15, 0, 1, 2, PASS), (15, 1, 1, 2, PASS), (15, 1, 0, 2, PASS), (15, 0, 0, 2, PASS))),
 )
 VMEM_LIMIT = 60 * 2 ** 20
-LANDING_LIMIT = 8 * 2 ** 20
+LANDING_LIMIT = 5 * 2 ** 20
 
 
 def dot(lhs, rhs, dims):
@@ -131,7 +131,7 @@
 def reduce_kernel(x_hbm, dy_hbm, seg_ref, gain_ref, wqkv_hbm, w1_hbm, wo_hbm, w2_hbm,
                   y_own, dx_own, dgain_ref, g_own, g_sib, full,
                   w_in, w_out, w1_raw, acc, x_buf, dy_buf, a_scr, hd_scr, stage, half, last_full, tmp,
-                  row_sem, w_sem, ws_sem, wr_sem, send_sem, half_sem, full_sem, tmp_sem, end_sem, out_sem):
+                  row_sem, w_sem, ws_sem, wr_sem, send_sem, half_sem, full_sem, tmp_sem, out_sem):
     place = Place()
     core = place.core
     _, seq_len, hidden = x_buf.shape
@@ -172,14 +172,15 @@
     for h in range(0, hidden, turn):
         up_spot[:, h:h + turn] = w1_raw[h:h + turn, :].T
     pl.semaphore_wait(barrier, len(peers))
-    swaps = [remote(src, dst, ws_sem.at[n], wr_sem.at[n], place.sibling()) for n, (src, dst) in enumerate(spots)]
+    swaps = [remote(dst, dst, ws_sem.at[n], wr_sem.at[n], place.sibling()) for n, (_, dst) in enumerate(spots)]
     swaps.append(remote(up_spot, up_spot, ws_sem.at[3], wr_sem.at[3], place.sibling()))
     for n in (0, 3, 1, 2):
+        if n < 3:
+            mine[n].wait()
         swaps[n].start()
     row_copy(0, 0, 0).wait()
     norm_row(0)
     acc[...] = jnp.zeros_like(acc)
-    mine[0].wait()
     for n in (0, 3):
         swaps[n].wait()
 
@@ -280,7 +281,7 @@
 
         @pl.when(step == 0)
         def _():
-            for copy in mine[1:] + swaps[1:3]:
+            for copy in swaps[1:3]:
                 copy.wait()
 
         proj = dot(w_in[...], a_scr[...], NT)
@@ -342,20 +343,14 @@
             x_f32 = x_buf[buf, at, :].astype(jnp.float32)
             normed, inv_std = norm_rows(x_f32)
             grad = stage[last, 1, at, :].astype(jnp.float32)
-            stage[last, 0, at, :] = (x_f32 + stage[last, 0, at, :].astype(jnp.float32)).astype(jnp.bfloat16)
+            y_own[at, :] = (x_f32 + stage[last, 0, at, :].astype(jnp.float32)).astype(jnp.bfloat16)
             d_hat = grad * gain
             d_x = inv_std * (d_hat - jnp.mean(d_hat, axis=-1, keepdims=True) - normed * jnp.mean(d_hat * normed, axis=-1, keepdims=True))
-            stage[last, 1, at, :] = (dy_buf[buf, at, :].astype(jnp.float32) + d_x).astype(jnp.bfloat16)
+            dx_own[at, :] = (dy_buf[buf, at, :].astype(jnp.float32) + d_x).astype(jnp.bfloat16)
             return d_gain + jnp.sum(grad * normed, axis=0, keepdims=True)
 
         dgain_ref[...] += lax.fori_loop(0, mid // fine, tile, jnp.zeros((1, hidden), jnp.float32))
-        copies = [pltpu.make_async_copy(piece_of(stage.at[last, t], piece), piece_of(dst, piece), end_sem.at[piece, t])
-                  for t, dst in ((0, y_own), (1, dx_own))]
-        for copy in copies:
-            copy.start()
-        return copies
-
-    ends = []
+
     ended = {0: 0, 1: 0}
     for work in EVENTS[-1][1]:
         event(*work)
@@ -363,12 +358,12 @@
         if n == steps - 1 and ring == 2:
             ended[piece] += 1
             if ended[piece] == 2:
-                ends += finish(piece)
+                finish(piece)
     for slot in range(SLOTS):
         if slot != last:
             for copy in slot_sends(slot):
                 copy.wait()
-    for copy in ends + grad_copies():
+    for copy in grad_copies():
         copy.wait()
 
 
@@ -443,14 +438,11 @@
             for t in range(2):
                 for way in (1, -1):
                     issue((axes[t][ring], way), t, 0, 0, n if way == 1 else 1 - n)
-    locals_ = []
     for t in range(2):
         for piece in range(2):
             pair(t, 0, 0, piece)
-            copy = pltpu.make_async_copy(source(t, 0, 0, piece), spot_of(t, place.me, piece), own_sem.at[t, piece])
-            copy.start()
-            locals_.append(copy)
-
+    own_copy = pltpu.make_async_copy(y_own.at[pl.ds(mid, mid)], y_hi.at[place.me], own_sem)
+    own_copy.start()
     g_copy = remote(g_sib, g_recv, g_sem.at[0], g_sem.at[1], place.sibling())
     g_copy.start()
 
@@ -497,6 +489,8 @@
             pair(t, d_1, d_2, piece)
         if n == 0:
             gain_start(2, gain_end(1))
+            y_lo[place.me] = y_own[0:mid, :]
+            dx_all[place.me] = dx_own[...]
         if n == 10:
             dgain_out[...] = jnp.sum(gain_end(2), axis=0).astype(dgain_out.dtype)
         if n == 2:
@@ -511,11 +505,10 @@
             landed(theirs, pair_recv.at[t, piece])
     for copy in sends:
         copy.wait_send()
-    for copy in locals_:
-        copy.wait()
-
-
-def place_kernel(y_lo, y_hi, dx_all, grads, d_up, dgain, y_out, dx_out, d_wqkv, d_wout, d_wdown, d_wup, dgain_out, bounce, in_sem, out_sem, sem):
+    own_copy.wait()
+
+
+def place_kernel(y_lo, y_hi, dx_all, grads, d_up, dgain, _y_own, _dx_own, y_out, dx_out, d_wqkv, d_wout, d_wdown, d_wup, dgain_out, bounce, in_sem, out_sem, sem):
     rows, mid, _ = y_lo.shape
     n_qkv, n_o, n_dn = d_wqkv.shape[0], d_wout.shape[0], d_wdown.shape[0]
     bufs, per = bounce.shape[0], bounce.shape[1]
@@ -569,8 +562,8 @@
         y_own, dx_own, d_gain, g_own, g_sib, _ = pl.pallas_call(
             reduce_kernel,
             in_specs=[anywhere, anywhere, vmem, vmem] + [anywhere] * 4,
-            out_specs=[anywhere, anywhere, vmem, anywhere, anywhere, anywhere],
-            out_shape=[shape((seq_len, hidden), bf16), shape((seq_len, hidden), bf16), shape((1, hidden), f32),
+            out_specs=[vmem, vmem, vmem, anywhere, anywhere, anywhere],
+            out_shape=[pltpu.VMEM((seq_len, hidden), bf16), pltpu.VMEM((seq_len, hidden), bf16), shape((1, hidden), f32),
                        shape((n_all, hidden), f32), shape((n_all, hidden), f32), shape((2, RING, 2, seq_len, hidden), bf16)],
             scratch_shapes=[
                 pltpu.VMEM((2 * n_in, hidden), bf16), pltpu.VMEM((2 * n_out, hidden), bf16), pltpu.VMEM((hidden, n_up), bf16),
@@ -581,7 +574,7 @@
                 pltpu.VMEM((2, RING + 1, 2, mid, hidden), bf16),
                 pltpu.VMEM((2, 2, seq_len, hidden), bf16), pltpu.VMEM((2, 2, mid, hidden), bf16),
                 dma((2, 2)), dma((4,)), dma((4,)), dma((4,)), dma((SLOTS, 2, 2)),
-                dma((2, RING + 1, 2)), dma((2, RING + 1, 2, 2)), dma((2, 2)), dma((2, 2)), dma((8,)),
+                dma((2, RING + 1, 2)), dma((2, RING + 1, 2, 2)), dma((2, 2)), dma((8,)),
             ],
             compiler_params=pltpu.CompilerParams(collective_id=0, has_side_effects=True, vmem_limit_bytes=VMEM_LIMIT),
             name="rows_reduce",
@@ -590,31 +583,32 @@
         per_link = chips - 1
         y_lo, y_hi, dx_all, _, d_gain, grads, d_up = pl.pallas_call(
             gather_kernel,
-            in_specs=[anywhere, anywhere, vmem, anywhere, anywhere],
+            in_specs=[vmem, vmem, vmem, anywhere, anywhere],
             out_specs=[vmem, anywhere, vmem, anywhere, vmem, vmem, vmem],
             out_shape=[pltpu.VMEM((rows, mid, hidden), bf16), shape((rows, mid, hidden), bf16), pltpu.VMEM((rows, seq_len, hidden), bf16),
                        shape(g_sib.shape, f32), pltpu.VMEM((hidden,), bf16),
                        pltpu.VMEM((n_all - n_up, hidden), bf16), pltpu.VMEM((hidden, n_up), bf16)],
             scratch_shapes=[
                 pltpu.VMEM((3, RING, 1, hidden), f32), pltpu.VMEM((2, n_o, hidden), f32), pltpu.VMEM((2, n_up, min(hidden, 256)), f32),
-                dma((4, per_link)), dma((4, per_link)), dma((2, 2 * chips)), dma((2, 2)), dma((2, 2)), dma((2,)), dma((2,)),
+                dma((4, per_link)), dma((4, per_link)), dma((2, 2 * chips)), dma((2, 2)), dma, dma((2,)), dma((2,)),
                 dma((3, 3)), dma((3, 3)),
             ],
             compiler_params=pltpu.CompilerParams(collective_id=1, has_side_effects=True, vmem_limit_bytes=LANDING_LIMIT),
             name="rows_gather",
-        )(y_own, dx_own, d_gain, g_own, g_sib)
-
-        bufs = 6
+        )(fixed(y_own), fixed(dx_own), d_gain, g_own, g_sib)
+
+        bufs = 4
         y_out, dx_out, d_wqkv, d_wout, d_wdown, d_wup, d_gain = pl.pallas_call(
             place_kernel,
-            in_specs=[vmem, anywhere, vmem, vmem, vmem, vmem],
+            in_specs=[vmem, anywhere] + [vmem] * 6,
             out_specs=[anywhere] * 6 + [vmem],
             out_shape=[shape(x_in.shape, bf16), shape(x_in.shape, bf16), shape(wqkv.shape, bf16), shape(wo.shape, bf16),
                        shape(w_down.shape, bf16), shape(w_up.shape, bf16), shape((hidden,), bf16)],
             scratch_shapes=[pltpu.VMEM((bufs, 2, mid, hidden), bf16), dma((bufs,)), dma((bufs,)), dma((12,))],
             compiler_params=pltpu.CompilerParams(vmem_limit_bytes=LANDING_LIMIT),
             name="rows_place",
-        )(fixed(y_lo), pltpu.with_memory_space_constraint(y_hi, pltpu.HBM), fixed(dx_all), fixed(grads), fixed(d_up), fixed(d_gain))
+        )(fixed(y_lo), pltpu.with_memory_space_constraint(y_hi, pltpu.HBM), fixed(dx_all), fixed(grads), fixed(d_up), fixed(d_gain),
+          fixed(y_own), fixed(dx_own))
         d_wqkv = d_wqkv.reshape(w_qkv.shape[1:] + (hidden,)).transpose(3, 0, 1, 2)
         return y_out, dx_out, d_gain, d_wqkv, d_wout.reshape(w_out.shape), d_wup, d_wdown
 

time: 408 us -> 407 us (level)
  no operation moved by 1% of the time
where the time goes in v10:
time: 407 us
  Pallas kernels  406 us (100%)
    pallas_call x1, Pallas kernels, body(): pl.pallas_call(reduce_kernel, in_specs=[anywhere, anywhere, vmem, vmem] +...  195 us
    pallas_call x1, Pallas kernels, body(): pl.pallas_call(gather_kernel, in_specs=[vmem, vmem, vmem, anywhere, anywh...  181 us
    pallas_call x1, Pallas kernels, body(): pl.pallas_call(place_kernel, in_specs=[vmem, anywhere] + [vmem] * 6, out_...  29.3 us

profile of v10, /device:TPU:97, one launch (start us, length us, event | category | flops | bytes accessed | tf_op | source)
XLA Modules:
  0.0 406.6 jit_solution(2804694527459628762)
XLA Ops:
  0.6 195.4 %rows_reduce.1 = (bf16[256,2048]{1,0:T(8,128)(2,1)S(1)}, bf16[256,2048]{1,0:T(8,128)(2,1)S(1)}, f32[1,2048]{1,0:T(1,128)}, f32[768,2048]{1,0:T(8,128)}, f32[768,...) custom-call(bf16[32,256,2048]{2,1,0:T(8,128)(2,1)} %x_hbm.1, bf16[32,256,2048]{2,1,0:T(8,128)(2,1)} %dy_hbm.1, ...), custom_call_target="tpu_custom_call" | custom-call | tf_op jit(solution)/shard_map/rows_reduce/pallas_call | solution.py:562
  196.0 181.1 %rows_gather.1 = (bf16[32,128,2048]{2,1,0:T(8,128)(2,1)S(1)}, bf16[32,128,2048]{2,1,0:T(8,128)(2,1)}, bf16[32,256,2048]{2,1,0:T(8,128)(2,1)S(1)}, f32[768,2048]{...) custom-call(bf16[256,2048]{1,0:T(8,128)(2,1)S(1)} %get-tuple-element.25.y_ow, ...), custom_call_target="tpu_custom_call" | custom-call | tf_op jit(solution)/shard_map/rows_gather/pallas_call | solution.py:584
  377.1 29.3 %rows_place.1 = (bf16[32,256,2048]{2,1,0:T(8,128)(2,1)}, bf16[32,256,2048]{2,1,0:T(8,128)(2,1)}, bf16[192,2048]{1,0:T(8,128)(2,1)}, bf16[64,2048]{1,0:T(8,128)(2...) custom-call(bf16[32,128,2048]{2,1,0:T(8,128)(2,1)S(1)} %get-tuple-element.30.y_lo, ...), custom_call_target="tpu_custom_call" | custom-call | tf_op jit(solution)/shard_map/rows_place/pallas_call | solution.py:601
